TPU v7x, 256 devices: a 8x8x2 block of a 8x8x16 slice. The times are simulated.
256 devices in a mesh: groups: 2 (over z), section: 64 (over y, x), head: 2 (over core).
Axes of the slice: x: 8, y: 8, z: 2, core: 2. Of those that a mesh axis runs over, the one named last changes fastest.
The devices are a block of a 8x8x16 slice.
Arguments:
- video_tokens: bfloat16 [65536, 1536], P(('groups', 'section', 'head')), parts along dimension 0, may hold values from -6 to 6
- modulation: float32 [6, 1536], P('groups'), parts along dimension 0, may hold values from -3 to 3
- project_weight: bfloat16 [3, 1536, 1536], P(None, None, 'head'), may hold values from -0.15625 to 0.15625
- output_weight: bfloat16 [1536, 1536], P('head'), may hold values from -0.15625 to 0.15625
- norm_gains: float32 [3, 128], replicated, may hold values from 1 to 2
- text_cache: bfloat16 [2, 512, 1536], P(None, 'groups', 'head'), parts along dimension 1, may hold values from -6 to 6
- text_count: int32 [2], P('groups'), parts along dimension 0, may hold values from 1 to 256, as said below
- video_keep: int32 [65536], P('groups'), parts along dimension 0, may hold values 0 or 1
- patch_order: int32 [128], P('groups'), parts along dimension 0, may hold values from 0 to 63, each once
- stale_cache: bfloat16 [2, 65536, 1536], P(None, ('groups', 'section'), 'head'), parts along dimension 1, may hold values from -6 to 6
Outputs:
- updated: bfloat16 [65536, 1536], P(('groups', 'section', 'head')), parts along dimension 0
- fresh_cache: bfloat16 [2, 65536, 1536], P(None, ('groups', 'section'), 'head'), parts along dimension 1
There are 2 independent parts, one for each index of `groups`. A program takes and returns all parts, laid end to end along the dimension named above; an argument that names none is the same for every part. Nothing has to cross between parts.
Inputs may be any that keep to these rules, and one draw needn't show every extreme that they name: The first text_count text tokens are real, the rest are padding. `video_keep`: 1 keeps a video token as a key, 0 marks padding. `patch_order`: each place 0 to 63 is held by exactly one patch.
All inputs are finite; a program needn't handle non-finite values.
Results may differ from a plain program's by a relative error of at most 0.0049.
Values may be sent and summed in bfloat16 or wider, within the bound.
No kernel may reach another device: no remote copies, remote signals or barrier semaphores. Data moves between devices by JAX's collectives and lax.ppermute only.
A program may use at most 128 MiB of HBM per device.

v0:
```python
import jax
import jax.numpy as jnp
from jax import lax
from jax.sharding import PartitionSpec as P

epsilon = 1e-06


def copy_for_each(array, axis):
    copies = jnp.broadcast_to(array, (lax.axis_size(axis), *array.shape))
    return lax.all_to_all(copies, axis, split_axis=0, concat_axis=0, tiled=True)


def in_order(pieces, dim):
    dims = list(pieces.shape[1:])
    dims[dim] *= pieces.shape[0]
    return jnp.moveaxis(pieces, 0, dim).reshape(dims)


def gathered_copies(array, axis, dim):
    pieces = copy_for_each(array, axis)
    return in_order(pieces, dim)


def from_behind(array, axis, by):
    count = lax.axis_size(axis)
    pairs = [(i, i + by) for i in range(count) if 0 <= i + by < count]
    return lax.ppermute(array, axis, pairs)


def in_blocks(array, dim, count):
    before, after = (array.shape[:dim], array.shape[dim + 1 :])
    return jnp.moveaxis(array.reshape(*before, count, -1, *after), dim, 0)


def sum_at_owner(array, axis, dim):
    count = lax.axis_size(axis)
    pieces = lax.all_to_all(in_blocks(array, dim, count), axis, 0, 0, tiled=True)
    return jnp.sum(pieces.astype(jnp.float32), axis=0)


def layer_norm(values):
    center = jnp.mean(values, axis=-1, keepdims=True)
    shifted = values - center
    spread = jnp.mean(shifted * shifted, axis=-1, keepdims=True)
    return shifted * lax.rsqrt(spread + epsilon)


def head_norm(inputs, gain_row):
    heads_local = inputs.shape[-1] // gain_row.shape[0]
    per_head = inputs.astype(jnp.float32).reshape(inputs.shape[0], heads_local, gain_row.shape[0])
    scaled = (
        per_head
        * lax.rsqrt(jnp.mean(per_head * per_head, axis=-1, keepdims=True) + epsilon)
        * gain_row
    )
    return scaled.astype(jnp.bfloat16)


def lookup(entries, wanted):
    positions = jnp.arange(entries.shape[0], dtype=jnp.int32)
    return jnp.sum(jnp.where(positions == wanted, entries, 0))


def attend_block(queries, key_rows, values, key_live, score_scale):
    scores = (
        jnp.einsum("qhd,khd->hqk", queries, key_rows, preferred_element_type=jnp.float32)
        * score_scale
    )
    weights = jnp.where(key_live[None, None, :], jnp.exp(scores), 0.0)
    total = jnp.sum(weights, axis=-1)
    numerator = jnp.einsum(
        "hqk,khd->qhd", weights.astype(jnp.bfloat16), values, preferred_element_type=jnp.float32
    )
    return (numerator / jnp.transpose(total)[:, :, None]).astype(jnp.bfloat16)


def on_device(
    video_tokens,
    modulation,
    project_weight,
    output_weight,
    norm_gains,
    text_cache,
    text_count,
    video_keep,
    patch_order,
    stale_cache,
):
    section_count = lax.axis_size("section")
    section_place = lax.axis_index("section")
    head_size = norm_gains.shape[1]
    local_width = project_weight.shape[2]
    local_heads = local_width // head_size
    patch_size = stale_cache.shape[1]
    text_rows = text_cache.shape[1]
    hidden = video_tokens.astype(jnp.float32)
    normed = (layer_norm(hidden) * (1.0 + modulation[1]) + modulation[0]).astype(jnp.bfloat16)
    segment = gathered_copies(normed, "head", 0)
    joined = jnp.einsum("rd,cdh->rch", segment, project_weight, preferred_element_type=jnp.float32)
    projected = joined.reshape(segment.shape[0], 3 * local_width)
    key_raw = projected[:, local_width : 2 * local_width].astype(jnp.bfloat16)
    value_raw = projected[:, 2 * local_width :].astype(jnp.bfloat16)
    fresh_cache = jnp.stack([key_raw, value_raw])
    own_slot = lookup(patch_order, section_place)
    left_place = jnp.maximum(section_place - 1, 0)
    right_place = jnp.minimum(section_place + 1, section_count - 1)
    left_slot = lookup(patch_order, left_place)
    right_slot = lookup(patch_order, right_place)
    to_right = jnp.where(own_slot < right_slot, fresh_cache, stale_cache)
    to_left = jnp.where(own_slot < left_slot, fresh_cache, stale_cache)
    left_cache = from_behind(to_right, "section", 1)
    right_cache = from_behind(to_left, "section", -1)
    keep_left = lax.dynamic_slice_in_dim(video_keep, left_place * patch_size, patch_size) > 0
    keep_own = lax.dynamic_slice_in_dim(video_keep, section_place * patch_size, patch_size) > 0
    keep_right = lax.dynamic_slice_in_dim(video_keep, right_place * patch_size, patch_size) > 0
    text_live = jnp.arange(text_rows, dtype=jnp.int32) < text_count[0]
    key_live = jnp.concatenate(
        [
            keep_left & (section_place > 0),
            keep_own,
            keep_right & (section_place < section_count - 1),
            text_live,
        ]
    )
    video_keys = head_norm(
        jnp.concatenate([left_cache[0], key_raw, right_cache[0]], axis=0), norm_gains[1]
    )
    text_keys = head_norm(text_cache[0], norm_gains[2])
    all_keys = jnp.concatenate([video_keys, text_keys], axis=0)
    values = jnp.concatenate(
        [left_cache[1], value_raw, right_cache[1], text_cache[1]], axis=0
    ).reshape(-1, local_heads, head_size)
    queries = head_norm(projected[:, :local_width], norm_gains[0])
    block_rows = min(patch_size, 512)
    score_scale = head_size ** (-0.5)

    def attend(query_block):
        return attend_block(query_block, all_keys, values, key_live, score_scale)

    attended = lax.map(
        attend, queries.reshape(patch_size // block_rows, block_rows, local_heads, head_size)
    ).reshape(patch_size, local_width)
    mixed_rows = sum_at_owner(
        jnp.dot(attended, output_weight, preferred_element_type=jnp.float32).astype(jnp.bfloat16),
        "head",
        0,
    )
    updated = (hidden + modulation[2] * mixed_rows).astype(jnp.bfloat16)
    return (updated, fresh_cache)


def solution(mesh):
    placed = (
        P(("groups", "section", "head"), None),
        P("groups", None),
        P(None, None, "head"),
        P("head", None),
        P(),
        P(None, "groups", "head"),
        P("groups"),
        P("groups"),
        P("groups"),
        P(None, ("groups", "section"), "head"),
    )
    return jax.shard_map(
        on_device,
        mesh=mesh,
        in_specs=placed,
        out_specs=(P(("groups", "section", "head"), None), P(None, ("groups", "section"), "head")),
        check_vma=False,
    )
```

profile of v0, /device:TPU:513, one launch (start us, length us, event | category | flops | bytes accessed | tf_op | source)
XLA Modules:
  0.0 151.1 jit_solution(6374956476702802500)
XLA Ops:
  0.6 1.5 convert_reduce_fusion.1
  2.1 1.5 fusion.23
  4.5 1.5 fusion.26
  7.3 25.0 %all-to-all-start = ((bf16[2,256,1536]{2,1,0:T(8,128)(2,1)}), bf16[2,256,1536]{2,1,0:T(8,128)(2,1)}, u32[]{:S(2)}, u32[]{:S(2)}) async-start(bf16[2,256,1536]{2,1,0:T(8,128)(2,1)} %broadcast_in_dim.40), calls=%async_computation | async-start | bytes 3145728 | tf_op jit(solution)/shard_map/all_to_all | solution.py:11
  35.6 10.3 %copy.20 = bf16[3,1536,768]{1,2,0:T(8,128)(2,1)} copy(bf16[3,1536,768]{2,1,0:T(8,128)(2,1)} %param.12) | data formatting | bytes 14155776 | tf_op args[2]
  45.9 9.6 %fusion.48 = (bf16[512,2304]{1,0:T(8,128)(2,1)S(1)}, f32[512,2304]{1,0:T(8,128)}) fusion(bf16[512,1536]{1,0:T(8,128)(2,1)} %bitcast, bf16[2304,1536]{1,0:T(8,128)(2,1)} %bitcast.37), kind=kOutput, calls=%fused_computation.81 | convolution fusion | flops 3625058304 | bytes 15728640 | tf_op jit(solution)/shard_map/rd,cdh->rch/dot_general | solution.py:100
  57.2 1.4 broadcast_select_fusion.1
  58.5 1.5 broadcast_select_fusion
  60.2 1.3 collective-permute-start.1
  61.5 5.2 %collective-permute-start = (bf16[2,512,768]{2,1,0:T(8,128)(2,1)}, bf16[2,512,768]{2,1,0:T(8,128)(2,1)}, u32[]{:S(2)}, u32[]{:S(2)}) collective-permute-start(bf16[2,512,768]{2,1,0:T(8,128)(2,1)} %get-tuple-element.26), channel_id=1, source_target_pairs={{0,2},{2,4},{4,6},{6,8},{8,10},{10,12},{12,14},{14,16},{16,18},{18... | collective-permute-start | bytes 4718600 | tf_op jit(solution)/shard_map/ppermute | solution.py:28
  68.7 1.9 %fusion.47 = (bf16[1,256,768]{2,1,0:T(8,128)(2,1)S(1)}, bf16[1,256,768]{2,1,0:T(8,128)(2,1)}) fusion(bf16[2,256,768]{2,1,0:T(8,128)(2,1)} %param.15), kind=kLoop, calls=%fused_computation.80 | loop fusion | bytes 1572864 | tf_op jit(solution)/shard_map/slice | solution.py:132
  74.3 2.3 %copy.22 = bf16[512,768]{0,1:T(8,128)(2,1)} copy(bf16[512,768]{1,0:T(8,128)(2,1)} %get-tuple-element.28) | data formatting | bytes 1572864 | tf_op jit(solution)/shard_map/slice | solution.py:103
  77.8 1.5 copy.30
  79.3 2.7 %slice.66 = f32[512,768]{1,0:T(8,128)} slice(f32[512,2304]{1,0:T(8,128)} %get-tuple-element.45), slice={[0:512], [0:768]} | slice | bytes 3145728 | tf_op jit(solution)/shard_map/slice | solution.py:134
  82.0 3.0 %copy.25 = f32[512,768]{0,1:T(8,128)} copy(f32[512,768]{1,0:T(8,128)} %slice.66) | data formatting | bytes 3145728 | tf_op jit(solution)/shard_map/slice | solution.py:134
  85.1 1.7 %multiply_reduce_fusion = f32[512,6]{0,1:T(8,128)S(1)} fusion(f32[512,6,128]{0,2,1:T(8,128)} %bitcast.38), kind=kLoop, calls=%fused_computation.40 | loop fusion | flops 783360 | bytes 1585152 | tf_op jit(solution)/shard_map/reduce_sum | solution.py:54
  86.8 1.3 slice_bitcast_fusion.2
  89.0 9.3 %collective-permute-done.1 = bf16[2,512,768]{2,1,0:T(8,128)(2,1)} collective-permute-done((bf16[2,512,768]{2,1,0:T(8,128)(2,1)}, bf16[2,512,768]{2,1,0:T(8,128)(2,1)}, u32[]{:S(2)}, u32[]{:S(2)}) %collective-permute-start.1) | collective-permute-done | bytes 1572896 | tf_op jit(solution)/shard_map/ppermute | solution.py:28
  98.3 2.6 %fusion.46 = (bf16[1,512,768]{2,1,0:T(8,128)(2,1)}, bf16[1,512,768]{2,1,0:T(8,128)(2,1)}) fusion(bf16[2,512,768]{2,1,0:T(8,128)(2,1)} %collective-permute-done.1), kind=kLoop, calls=%fused_computation.79 | loop fusion | bytes 3145728 | tf_op jit(solution)/shard_map/slice | solution.py:132
  101.0 2.3 %copy.23 = bf16[1,512,768]{1,2,0:T(8,128)(2,1)} copy(bf16[1,512,768]{2,1,0:T(8,128)(2,1)} %get-tuple-element.34) | data formatting | bytes 1572864 | tf_op jit(solution)/shard_map/slice | solution.py:132
  103.3 2.3 %copy.28 = bf16[1,512,768]{1,2,0:T(8,128)(2,1)} copy(bf16[1,512,768]{2,1,0:T(8,128)(2,1)} %get-tuple-element.35) | data formatting | bytes 1572864 | tf_op jit(solution)/shard_map/slice | solution.py:127
  105.6 2.3 %copy.31 = bf16[512,6,128]{2,0,1:T(8,128)(2,1)} copy(bf16[512,6,128]{0,2,1:T(8,128)(2,1)} %bitcast.44) | data formatting | bytes 1572864 | tf_op jit(solution)/shard_map/concatenate | solution.py:127
  107.9 2.6 %fusion.45 = (bf16[1,512,768]{2,1,0:T(8,128)(2,1)}, bf16[1,512,768]{2,1,0:T(8,128)(2,1)}) fusion(bf16[2,512,768]{2,1,0:T(8,128)(2,1)} %collective-permute-done), kind=kLoop, calls=%fused_computation.78 | loop fusion | bytes 3145728 | tf_op jit(solution)/shard_map/slice | solution.py:132
  110.5 2.3 %copy.21 = bf16[1,512,768]{1,2,0:T(8,128)(2,1)} copy(bf16[1,512,768]{2,1,0:T(8,128)(2,1)} %get-tuple-element.32) | data formatting | bytes 1572864 | tf_op jit(solution)/shard_map/slice | solution.py:132
  112.8 2.3 %copy.26 = bf16[1,512,768]{1,2,0:T(8,128)(2,1)} copy(bf16[1,512,768]{2,1,0:T(8,128)(2,1)} %get-tuple-element.33) | data formatting | bytes 1572864 | tf_op jit(solution)/shard_map/slice | solution.py:127
  115.1 2.3 %copy.29 = bf16[512,6,128]{2,0,1:T(8,128)(2,1)} copy(bf16[512,6,128]{0,2,1:T(8,128)(2,1)} %bitcast.45) | data formatting | bytes 1572864 | tf_op jit(solution)/shard_map/concatenate | solution.py:127
  117.4 2.8 %fusion.7 = f32[1536,6]{0,1:T(8,128)S(1)} fusion(bf16[512,6,128]{2,0,1:T(8,128)(2,1)} %copy.31, bf16[512,6,128]{2,0,1:T(8,128)(2,1)S(1)} %copy.30, bf16[512,6,128]{2,0,1:T(8,128)(2,1)} %copy.29), kind=kLoop, calls=%fused_computation.9 | loop fusion | flops 9427968 | bytes 2396160 | tf_op jit(solution)/shard_map/reduce_sum | solution.py:54
  120.2 1.7 %fusion.9 = bf16[1536,6,128]{2,0,1:T(8,128)(2,1)S(1)} fusion(f32[128]{0:T(128)S(1)} %get-tuple-element.43, f32[1536,6]{0,1:T(8,128)S(1)} %add_rsqrt_fusion, bf16[512,6,128]{2,0,1:T(8,128)(2,1)S(1)} %copy-done.2, bf16[512,6,128]{2,0,1:T(8,128)(2,1)S(1)} %copy.30, bf16[512,6,128]{2,0,1:T(8,128)(2,1)S(1)} %copy-done.3), kind=kLoop, calls=%fused_computation.11 | loop fusion | flops 10616832 | bytes 4755968 | tf_op jit(solution)/shard_map/convert_element_type | solution.py:57
  122.0 10.0 %fusion = (f32[6,512]{1,0:T(8,128)S(1)}, f32[6,512,1792]{2,1,0:T(8,128)}) fusion(pred[1792]{0:T(1024)(128)(4,1)S(1)} %pad_add_fusion, bf16[256,6,128]{2,0,1:T(8,128)(2,1)S(1)} %multiply_convert_fusion.2, bf16[1536,6,128]{2,0,1:T(8,128)(2,1)S(1)} %fusion.9, f32[512,6,128]{0,2,1:T(8,128)S(1)} %bitcast.39, f32[128]{0:T(128)S(1)} %copy-done.14, ...), kind=kOutput, calls=%fused_computation.1 | convolution fusion | flops 1432482816 | bytes 26372352 | tf_op jit(solution)/shard_map/while/body/eval_jaxpr/qhd,khd->hqk/dot_general | solution.py:67
  131.9 9.9 %fusion.28 = bf16[512,6,128]{0,2,1:T(8,128)(2,1)S(1)} fusion(f32[6,512,1792]{2,1,0:T(8,128)} %get-tuple-element.47, pred[1792]{0:T(1024)(128)(4,1)S(1)} %pad_add_fusion, bf16[256,6,128]{0,2,1:T(8,128)(2,1)S(1)} %bitcast.50, bf16[512,6,128]{0,2,1:T(8,128)(2,1)S(1)} %bitcast.48, bf16[512,6,128]{0,2,1:T(8,128)(2,1)S(1)} %bitcast.47, ...), kind=kOutput, calls=%fused_computation.38 | convolution fusion | flops 1437597696 | bytes 25573120 | tf_op jit(solution)/shard_map/while/body/eval_jaxpr/hqk,khd->qhd/dot_general | solution.py:72
  141.9 1.4 convolution_convert_fusion
  143.3 5.5 %all_to_all.10 = bf16[2,256,1536]{2,1,0:T(8,128)(2,1)S(1)} all-to-all(bf16[2,256,1536]{2,1,0:T(8,128)(2,1)S(1)} %bitcast.40), channel_id=1, replica_groups=mesh['groups'=2,'section'=64,'head'=2] {'head'}, dimensions={0} | all-to-all | bytes 3145728 | tf_op jit(solution)/shard_map/all_to_all | solution.py:38
  (52 shorter events, 14.2 us)
Async XLA Ops:
  0.6 141.2 %copy-start = (bf16[768,1536]{1,0:T(8,128)(2,1)S(1)}, bf16[768,1536]{1,0:T(8,128)(2,1)}, u32[]{:S(2)}) copy-start(bf16[768,1536]{1,0:T(8,128)(2,1)} %param.13) | copy-start | bytes 7077892
  6.0 26.3 %copy-start.13 = (s32[64]{0:T(128)S(1)}, s32[64]{0:T(128)}, u32[]{:S(2)}) copy-start(s32[64]{0:T(128)} %param.18) | copy-start | bytes 772
  7.3 38.6 %all-to-all-start = ((bf16[2,256,1536]{2,1,0:T(8,128)(2,1)}), bf16[2,256,1536]{2,1,0:T(8,128)(2,1)}, u32[]{:S(2)}, u32[]{:S(2)}) async-start(bf16[2,256,1536]{2,1,0:T(8,128)(2,1)} %broadcast_in_dim.40), calls=%async_computation | async-start | bytes 3145728 | tf_op jit(solution)/shard_map/all_to_all | solution.py:11
  55.5 1.7 %copy-start.4 = (bf16[2,512,768]{2,1,0:T(8,128)(2,1)S(1)}, bf16[2,512,768]{2,1,0:T(8,128)(2,1)}, u32[]{:S(2)}) copy-start(bf16[2,512,768]{2,1,0:T(8,128)(2,1)} %param.19) | copy-start | bytes 4718596
  58.5 1.7 %copy-start.5 = (bf16[2,512,768]{2,1,0:T(8,128)(2,1)}, bf16[2,512,768]{2,1,0:T(8,128)(2,1)S(1)}, u32[]{:S(2)}) copy-start(bf16[2,512,768]{2,1,0:T(8,128)(2,1)S(1)} %get-tuple-element.27) | copy-start | bytes 4718596
  60.2 38.1 %collective-permute-start.1 = (bf16[2,512,768]{2,1,0:T(8,128)(2,1)}, bf16[2,512,768]{2,1,0:T(8,128)(2,1)}, u32[]{:S(2)}, u32[]{:S(2)}) collective-permute-start(bf16[2,512,768]{2,1,0:T(8,128)(2,1)} %broadcast_select_fusion), channel_id=1, source_target_pairs={{2,0},{4,2},{6,4},{8,6},{10,8},{12,10},{14,12},{16,14},{18,16},{20... | collective-permute-start | bytes 4718600 | tf_op jit(solution)/shard_map/ppermute | solution.py:28
  61.5 46.4 %collective-permute-start = (bf16[2,512,768]{2,1,0:T(8,128)(2,1)}, bf16[2,512,768]{2,1,0:T(8,128)(2,1)}, u32[]{:S(2)}, u32[]{:S(2)}) collective-permute-start(bf16[2,512,768]{2,1,0:T(8,128)(2,1)} %get-tuple-element.26), channel_id=1, source_target_pairs={{0,2},{2,4},{4,6},{6,8},{8,10},{10,12},{12,14},{14,16},{16,18},{18... | collective-permute-start | bytes 4718600 | tf_op jit(solution)/shard_map/ppermute | solution.py:28
  85.0 3.7 %copy-start.7 = (f32[256,6,128]{2,0,1:T(8,128)S(1)}, f32[256,6,128]{2,0,1:T(8,128)}, u32[]{:S(2)}) copy-start(f32[256,6,128]{2,0,1:T(8,128)} %copy.33) | copy-start | bytes 2359300
  117.4 2.8 %copy-start.2 = (bf16[512,6,128]{2,0,1:T(8,128)(2,1)S(1)}, bf16[512,6,128]{2,0,1:T(8,128)(2,1)}, u32[]{:S(2)}) copy-start(bf16[512,6,128]{2,0,1:T(8,128)(2,1)} %copy.31) | copy-start | bytes 2359300
  117.4 2.8 %copy-start.3 = (bf16[512,6,128]{2,0,1:T(8,128)(2,1)S(1)}, bf16[512,6,128]{2,0,1:T(8,128)(2,1)}, u32[]{:S(2)}) copy-start(bf16[512,6,128]{2,0,1:T(8,128)(2,1)} %copy.29) | copy-start | bytes 2359300
  120.2 1.7 %copy-start.6 = (f32[512,768]{0,1:T(8,128)S(1)}, f32[512,768]{0,1:T(8,128)}, u32[]{:S(2)}) copy-start(f32[512,768]{0,1:T(8,128)} %copy.25) | copy-start | bytes 4718596
  120.2 1.7 %copy-start.12 = (f32[512,6]{0,1:T(8,128)S(1)}, f32[512,6]{0,1:T(8,128)}, u32[]{:S(2)}) copy-start(f32[512,6]{0,1:T(8,128)} %add_rsqrt_fusion.1) | copy-start | bytes 36868
  120.2 1.7 %copy-start.14 = (f32[128]{0:T(128)S(1)}, f32[128]{0:T(128)}, u32[]{:S(2)}) copy-start(f32[128]{0:T(128)} %get-tuple-element.41) | copy-start | bytes 1540
  121.9 10.0 %copy-start.8 = (bf16[512,768]{0,1:T(8,128)(2,1)S(1)}, bf16[512,768]{0,1:T(8,128)(2,1)}, u32[]{:S(2)}) copy-start(bf16[512,768]{0,1:T(8,128)(2,1)} %copy.22) | copy-start | bytes 2359300
  121.9 10.0 %copy-start.9 = (bf16[1,512,768]{1,2,0:T(8,128)(2,1)S(1)}, bf16[1,512,768]{1,2,0:T(8,128)(2,1)}, u32[]{:S(2)}) copy-start(bf16[1,512,768]{1,2,0:T(8,128)(2,1)} %copy.23) | copy-start | bytes 2359300
  121.9 10.0 %copy-start.10 = (bf16[1,512,768]{1,2,0:T(8,128)(2,1)S(1)}, bf16[1,512,768]{1,2,0:T(8,128)(2,1)}, u32[]{:S(2)}) copy-start(bf16[1,512,768]{1,2,0:T(8,128)(2,1)} %copy.21) | copy-start | bytes 2359300
  121.9 10.0 %copy-start.11 = (bf16[1,256,768]{1,2,0:T(8,128)(2,1)S(1)}, bf16[1,256,768]{1,2,0:T(8,128)(2,1)}, u32[]{:S(2)}) copy-start(bf16[1,256,768]{1,2,0:T(8,128)(2,1)} %copy.24) | copy-start | bytes 1179652
  148.8 1.1 copy-start.1
where the time goes:
time: 152 us; the launch traced here: 151 us
  local copies, waits for them, and re-layouts  50.4 us (33%)
  starting transfers between devices  31.5 us (21%)
  matrix products  30.9 us (20%)
  other arithmetic  19.3 us (13%)
  waiting for transfers between devices  9.35 us (6%)
  blocking collectives  5.55 us (4%)
  between operations  4.12 us (3%)
    all_to_all x1, starting transfers between devices, copy_for_each(): return lax.all_to_all(copies, axis, split_axis=0, concat_axis=0, tiled=True)  25 us
    unnamed x32, local copies, waits for them, and re-layouts  13.1 us
    dot_general x1, matrix products, attend_block(): jnp.einsum('qhd,khd->hqk', queries, key_rows, preferred_element_type=jnp....  9.97 us
    dot_general x1, matrix products, attend_block(): jnp.einsum('hqk,khd->qhd', weights.astype(jnp.bfloat16), values, preferre...  9.9 us
    dot_general x1, matrix products, on_device(): jnp.einsum('rd,cdh->rch', segment, project_weight, preferred_element_type...  9.58 us
    ppermute x2, waiting for transfers between devices, from_behind(): return lax.ppermute(array, axis, pairs)  9.35 us
    ppermute x2, starting transfers between devices, from_behind(): return lax.ppermute(array, axis, pairs)  6.48 us
    concatenate x3, local copies, waits for them, and re-layouts, on_device(): jnp.concatenate([left_cache[0], key_raw, right_cache[0]], axis=0)  6.08 us
  transfers between devices with their start and end apart: 3, of which 1 were waited for; matrix products, arithmetic and copies ran while one was open for 28% of the time, Pallas kernels for 0%

commit v1 on v0

v1 whole, which is shorter than its diff:
```python
import functools
import math

import jax
import jax.numpy as jnp
from jax import lax
from jax.experimental import pallas as pl
from jax.experimental.pallas import tpu as pltpu
from jax.sharding import PartitionSpec as P


epsilon = 1e-06
f32 = jnp.float32
bf16 = jnp.bfloat16
MIB = 1024 * 1024

VMEM = pl.BlockSpec(memory_space=pltpu.VMEM)
SMEM = pl.BlockSpec(memory_space=pltpu.SMEM)
HBM = pl.BlockSpec(memory_space=pltpu.HBM)


def params(mib):
    return pltpu.CompilerParams(vmem_limit_bytes=mib * MIB)


def in_hbm(array):
    return pltpu.with_memory_space_constraint(array, pltpu.HBM)


def cost(flops, nbytes):
    return pl.CostEstimate(flops=flops, bytes_accessed=nbytes, transcendentals=0)


def slots(place, order, sections):
    p = place[0]
    left = jnp.maximum(p - 1, 0)
    right = jnp.minimum(p + 1, sections - 1)
    return order[p], order[left], order[right]


def gain_row(gains, which):
    return gains[which : which + 1, :]


def head_normed(part, gain):
    spread = jnp.mean(part * part, axis=-1, keepdims=True)
    return (part * lax.rsqrt(spread + epsilon) * gain).astype(bf16)


def heads_normed(part, gain):
    size = gain.shape[-1]
    pieces = [
        head_normed(part[:, i : i + size], gain) for i in range(0, part.shape[-1], size)
    ]
    return jnp.concatenate(pieces, axis=-1)


def mask_columns(row, lanes):
    return jnp.broadcast_to(row, (lanes, row.shape[1])).T.astype(bf16)


def first_kernel(sections, place, order, x, mod, stale, normed, to_right, to_left, held, sem):
    load = pltpu.make_async_copy(stale.at[0], held, sem)
    load.start()
    rows, width = x.shape
    step = 64
    scale = 1.0 + mod[1:2, :]
    shift = mod[0:1, :]
    for r in range(0, rows, step):
        v = x[r : r + step, :].astype(f32)
        shifted = v - jnp.mean(v, axis=-1, keepdims=True)
        spread = jnp.mean(shifted * shifted, axis=-1, keepdims=True)
        normed[r : r + step, :] = (shifted * lax.rsqrt(spread + epsilon) * scale + shift).astype(
            bf16
        )
    load.wait()
    own, left, right = slots(place, order, sections)
    half = width // 2

    def fill(out, fresh):
        @pl.when(fresh)
        def _():
            out[...] = normed[...]

        @pl.when(jnp.logical_not(fresh))
        def _():
            out[:, :half] = held[:rows, :]
            out[:, half:] = held[rows:, :]

    fill(to_right, own < right)
    fill(to_left, own < left)


def project_kernel(
    sections,
    place,
    side,
    order,
    own_half,
    other_half,
    weight,
    gains,
    stale,
    cache,
    queries,
    keys,
    to_right,
    to_left,
    wbuf,
    held,
    wsem,
    sem,
):
    rows = own_half.shape[0]
    width = queries.shape[1]
    block = wbuf.shape[2]
    blocks = width // block
    size = gains.shape[1]
    kinds = (2, 1, 0)
    copies = []
    for t, c in enumerate(kinds):
        for j in range(blocks):
            n = t * blocks + j
            copy = pltpu.make_async_copy(
                weight.at[c, :, j * block : (j + 1) * block], wbuf.at[n], wsem.at[n]
            )
            copy.start()
            copies.append(copy)
    load = pltpu.make_async_copy(stale.at[1], held, sem)
    load.start()
    h = side[0]
    places = (
        (own_half, pl.multiple_of(h * rows, rows)),
        (other_half, pl.multiple_of((1 - h) * rows, rows)),
    )
    factor = math.log2(math.e) * size**-0.5
    query_gain = gain_row(gains, 0) * factor
    key_gain = gain_row(gains, 1)
    for t, c in enumerate(kinds):
        for j in range(blocks):
            n = t * blocks + j
            copies[n].wait()
            cols = slice(j * block, (j + 1) * block)
            for half, at in places:
                y = jnp.dot(half[...], wbuf[n], preferred_element_type=f32)
                at = pl.ds(at, rows)
                if c == 0:
                    queries[at, cols] = heads_normed(y, query_gain)
                else:
                    rounded = y.astype(bf16)
                    cache[c - 1, at, cols] = rounded
                    if c == 1:
                        keys[at, cols] = heads_normed(rounded.astype(f32), key_gain)
        if c == 2:
            load.wait()
            own, left, right = slots(place, order, sections)
            for out, fresh in ((to_right, own < right), (to_left, own < left)):

                @pl.when(fresh)
                def _():
                    out[...] = cache[1]

                @pl.when(jnp.logical_not(fresh))
                def _():
                    out[...] = held[...]


def own_kernel(place, count, queries, keys, cache, text, gains, keep, total, vbuf):
    patch, width = queries.shape
    text_rows = text.shape[1]
    size = gains.shape[1]
    own_mask = mask_columns((keep[pl.ds(place[0], 1), :] > 0).astype(f32), size)
    live = lax.broadcasted_iota(jnp.int32, (text_rows, size), 0) < count[0]
    text_mask = live.astype(f32).astype(bf16)
    vbuf[:patch, size:] = own_mask
    vbuf[patch:, size:] = text_mask
    gain = gain_row(gains, 2)
    for h in range(width // size):
        cols = slice(h * size, (h + 1) * size)
        text_key = head_normed(text[0, :, cols].astype(f32), gain)
        all_keys = jnp.concatenate([keys[:, cols], text_key], axis=0)
        vbuf[:patch, :size] = cache[1, :, cols] * own_mask
        vbuf[patch:, :size] = text[1, :, cols] * text_mask
        s = lax.dot_general(
            queries[:, cols], all_keys, (((1,), (1,)), ((), ())), preferred_element_type=f32
        )
        w = jnp.exp2(s).astype(bf16)
        total[:, 2 * h * size : 2 * (h + 1) * size] = jnp.dot(
            w, vbuf[...], preferred_element_type=f32
        )


def near_kernel(
    sections,
    place,
    side,
    order,
    left_own,
    left_other,
    right_own,
    right_other,
    weight,
    gains,
    queries,
    weights,
    wbuf,
    kbuf,
    wsem,
):
    rows = left_own.shape[0]
    patch, width = queries.shape
    block = wbuf.shape[2]
    size = gains.shape[1]
    copies = []
    for j in range(width // block):
        copy = pltpu.make_async_copy(
            weight.at[1, :, j * block : (j + 1) * block], wbuf.at[j], wsem.at[j]
        )
        copy.start()
        copies.append(copy)
    h = side[0]
    own_at = pl.multiple_of(h * rows, rows)
    other_at = pl.multiple_of((1 - h) * rows, rows)
    own, left, right = slots(place, order, sections)
    gain = gain_row(gains, 1)
    for j in range(width // block):
        copies[j].wait()
        for n, (mine, other, fresh) in enumerate(
            ((left_own, left_other, left < own), (right_own, right_other, right < own))
        ):
            base = n * patch

            @pl.when(fresh)
            def _():
                for half, at in ((mine, own_at), (other, other_at)):
                    y = jnp.dot(half[...], wbuf[j], preferred_element_type=f32).astype(bf16)
                    kbuf[pl.ds(base + at, rows), :] = heads_normed(y.astype(f32), gain)

            @pl.when(jnp.logical_not(fresh))
            def _():
                for i in range(patch // rows):
                    y = mine[:, i * width + j * block : i * width + (j + 1) * block]
                    kbuf[base + i * rows : base + (i + 1) * rows, :] = heads_normed(
                        y.astype(f32), gain
                    )

        for i in range(block // size):
            cols = slice(j * block + i * size, j * block + (i + 1) * size)
            s = lax.dot_general(
                queries[:, cols],
                kbuf[:, i * size : (i + 1) * size],
                (((1,), (1,)), ((), ())),
                preferred_element_type=f32,
            )
            weights[j * (block // size) + i] = jnp.exp2(s).astype(bf16)


def last_kernel(
    sections, flip, place, side, weights, left_values, right_values, total, keep, weight, out,
    vbuf, att, wbuf, wsem,
):
    load = pltpu.make_async_copy(weight, wbuf, wsem)
    load.start()
    rows = out.shape[0]
    heads, patch, _ = weights.shape
    size = vbuf.shape[1] // 2
    p = place[0]
    h = side[0]
    at = pl.ds(pl.multiple_of((1 - h if flip else h) * rows, rows), rows)
    left_row = keep[pl.ds(jnp.maximum(p - 1, 0), 1), :]
    right_row = keep[pl.ds(jnp.minimum(p + 1, sections - 1), 1), :]
    left_mask = mask_columns(((left_row > 0) & (p > 0)).astype(f32), size)
    right_mask = mask_columns(((right_row > 0) & (p < sections - 1)).astype(f32), size)
    vbuf[:patch, size:] = left_mask
    vbuf[patch:, size:] = right_mask
    for i in range(heads):
        cols = slice(i * size, (i + 1) * size)
        vbuf[:patch, :size] = left_values[:, cols] * left_mask
        vbuf[patch:, :size] = right_values[:, cols] * right_mask
        sums = total[at, 2 * i * size : 2 * (i + 1) * size] + jnp.dot(
            weights[i, at, :], vbuf[...], preferred_element_type=f32
        )
        att[:, cols] = (sums[:, :size] / sums[:, size:]).astype(bf16)
    load.wait()
    out[...] = jnp.dot(att[...], wbuf[...], preferred_element_type=f32).astype(bf16)


def swapped(array):
    return lax.ppermute(array, "head", [(0, 1), (1, 0)])


def from_behind(array, axis, by):
    count = lax.axis_size(axis)
    pairs = [(i, i + by) for i in range(count) if 0 <= i + by < count]
    return lax.ppermute(array, axis, pairs)


def on_device(
    video_tokens,
    modulation,
    project_weight,
    output_weight,
    norm_gains,
    text_cache,
    text_count,
    video_keep,
    patch_order,
    stale_cache,
):
    sections = lax.axis_size("section")
    place = lax.axis_index("section").astype(jnp.int32).reshape(1)
    side = lax.axis_index("head").astype(jnp.int32).reshape(1)
    rows, model = video_tokens.shape
    size = norm_gains.shape[1]
    width = project_weight.shape[2]
    heads = width // size
    patch = stale_cache.shape[1]
    text_rows = text_cache.shape[1]
    block = 2 * size
    project_weight = in_hbm(project_weight)
    output_weight = in_hbm(output_weight)
    stale_cache = in_hbm(stale_cache)
    keep = video_keep.reshape(sections, patch)
    half_shape = jax.ShapeDtypeStruct((rows, model), bf16)
    side_shape = jax.ShapeDtypeStruct((patch, width), bf16)

    normed, to_right, to_left = pl.pallas_call(
        functools.partial(first_kernel, sections),
        out_shape=(half_shape, half_shape, half_shape),
        in_specs=[SMEM, SMEM, VMEM, VMEM, HBM],
        out_specs=(VMEM, VMEM, VMEM),
        scratch_shapes=[pltpu.VMEM((patch, width), bf16), pltpu.SemaphoreType.DMA],
        compiler_params=params(10),
        cost_estimate=cost(10 * rows * model, 10 * rows * model),
        name="first",
    )(place, patch_order, video_tokens, modulation, stale_cache)

    other = swapped(normed)
    left_own = from_behind(to_right, "section", 1)
    right_own = from_behind(to_left, "section", -1)

    fresh_cache, queries, keys, values_right, values_left = pl.pallas_call(
        functools.partial(project_kernel, sections),
        out_shape=(
            jax.ShapeDtypeStruct((2, patch, width), bf16),
            side_shape,
            side_shape,
            side_shape,
            side_shape,
        ),
        in_specs=[SMEM, SMEM, SMEM, VMEM, VMEM, HBM, VMEM, HBM],
        out_specs=(VMEM,) * 5,
        scratch_shapes=[
            pltpu.VMEM((3 * width // block, model, block), bf16),
            pltpu.VMEM((patch, width), bf16),
            pltpu.SemaphoreType.DMA((3 * width // block,)),
            pltpu.SemaphoreType.DMA,
        ],
        compiler_params=params(24),
        cost_estimate=cost(2 * patch * model * 3 * width, 6 * model * width),
        name="project",
    )(place, side, patch_order, normed, other, project_weight, norm_gains, stale_cache)

    left_values = from_behind(values_right, "section", 1)
    right_values = from_behind(values_left, "section", -1)
    left_own, right_own, queries = lax.optimization_barrier((left_own, right_own, queries))
    left_other = swapped(left_own)
    right_other = swapped(right_own)

    total = pl.pallas_call(
        own_kernel,
        out_shape=jax.ShapeDtypeStruct((patch, 2 * width), f32),
        in_specs=[SMEM, SMEM] + [VMEM] * 6,
        out_specs=VMEM,
        scratch_shapes=[pltpu.VMEM((patch + text_rows, 2 * size), bf16)],
        compiler_params=params(20),
        cost_estimate=cost(8 * patch * (patch + text_rows) * width, 6 * patch * width),
        name="own",
    )(place, text_count, queries, keys, fresh_cache, text_cache, norm_gains, keep)

    weights = pl.pallas_call(
        functools.partial(near_kernel, sections),
        out_shape=jax.ShapeDtypeStruct((heads, patch, 2 * patch), bf16),
        in_specs=[SMEM] * 3 + [VMEM] * 4 + [HBM, VMEM, VMEM],
        out_specs=VMEM,
        scratch_shapes=[
            pltpu.VMEM((width // block, model, block), bf16),
            pltpu.VMEM((2 * patch, block), bf16),
            pltpu.SemaphoreType.DMA((width // block,)),
        ],
        compiler_params=params(24),
        cost_estimate=cost(4 * patch * model * width + 8 * patch * patch * width, 6 * patch * width),
        name="near",
    )(
        place,
        side,
        patch_order,
        left_own,
        left_other,
        right_own,
        right_other,
        project_weight,
        norm_gains,
        queries,
    )

    def finish(flip):
        return pl.pallas_call(
            functools.partial(last_kernel, sections, flip),
            out_shape=half_shape,
            in_specs=[SMEM, SMEM] + [VMEM] * 5 + [HBM],
            out_specs=VMEM,
            scratch_shapes=[
                pltpu.VMEM((2 * patch, 2 * size), bf16),
                pltpu.VMEM((rows, width), bf16),
                pltpu.VMEM((width, model), bf16),
                pltpu.SemaphoreType.DMA,
            ],
            compiler_params=params(26),
            cost_estimate=cost(
                8 * rows * patch * width + 2 * rows * width * model, 6 * patch * width
            ),
            name="last_sent" if flip else "last_kept",
        )(place, side, weights, left_values, right_values, total, keep, output_weight)

    sent = finish(True)
    received = swapped(sent)
    kept = finish(False)
    mixed = kept.astype(f32) + received.astype(f32)
    updated = (video_tokens.astype(f32) + modulation[2] * mixed).astype(bf16)
    return (updated, fresh_cache)


def solution(mesh):
    placed = (
        P(("groups", "section", "head"), None),
        P("groups", None),
        P(None, None, "head"),
        P("head", None),
        P(),
        P(None, "groups", "head"),
        P("groups"),
        P("groups"),
        P("groups"),
        P(None, ("groups", "section"), "head"),
    )

    return jax.shard_map(
        on_device,
        mesh=mesh,
        in_specs=placed,
        out_specs=(P(("groups", "section", "head"), None), P(None, ("groups", "section"), "head")),
        check_vma=False,
    )
```

time: 152 us -> 83.4 us (0.55)
  local copies, waits for them, and re-layouts: 50.4 us -> 9.89 us
  matrix products: 30.9 us -> 0 us
  Pallas kernels: 0 us -> 29.6 us
  other arithmetic: 19.3 us -> 1.22 us
  blocking collectives: 5.55 us -> 0 us
  starting transfers between devices: 31.5 us -> 28.4 us
  waiting for transfers between devices: 9.35 us -> 12.1 us
  between operations: 4.12 us -> 1.51 us
    dot_general x4 -> x0, matrix products: 30.9 us -> none  [the longest x1 9.97 us: attend_block(): jnp.einsum('qhd,khd->hqk', queries, key_rows, preferred_element_type=jnp....]
    pallas_call x0 -> x6, Pallas kernels: none -> 29.6 us  [the longest x1 10.4 us: on_device(): pl.pallas_call(functools.partial(project_kernel, sections), out_shape=(ja...]
    slice x13 -> x1, local copies, waits for them, and re-layouts: 27.5 us -> 0.76 us  [on_device(): updated = (video_tokens.astype(f32) + modulation[2] * mixed).astype(bf16)]
    all_to_all x1 -> x0, starting transfers between devices: 25 us -> none  [copy_for_each(): return lax.all_to_all(copies, axis, split_axis=0, concat_axis=0, tiled=True)]
    ppermute x0 -> x4, starting transfers between devices: none -> 23.1 us  [swapped(): return lax.ppermute(array, 'head', [(0, 1), (1, 0)])]
    reduce_sum x7 -> x0, other arithmetic: 8.44 us -> none  [the longest x3 4.52 us: head_norm(): jnp.mean(per_head * per_head, axis=-1, keepdims=True) + epsilon]
    concatenate x3 -> x0, local copies, waits for them, and re-layouts: 6.08 us -> none  [on_device(): jnp.concatenate([left_cache[0], key_raw, right_cache[0]], axis=0)]
    all_to_all x1 -> x0, blocking collectives: 5.55 us -> none  [sum_at_owner(): lax.all_to_all(in_blocks(array, dim, count), axis, 0, 0, tiled=True)]
  transfers between devices with their start and end apart: 3 -> 8, of which waited for: 1 -> 4; matrix products, arithmetic and copies ran while one was open for 28% -> 1% of each run, Pallas kernels for 0% -> 28%
where the time goes in v1:
time: 83.4 us; the launch traced here: 82.7 us
  Pallas kernels  29.6 us (35%)
  starting transfers between devices  28.4 us (34%)
  waiting for transfers between devices  12.1 us (15%)
  local copies, waits for them, and re-layouts  9.89 us (12%)
  between operations  1.51 us (2%)
  other arithmetic  1.22 us (1%)
    ppermute x4, starting transfers between devices, swapped(): return lax.ppermute(array, 'head', [(0, 1), (1, 0)])  23.1 us
    ppermute x4, waiting for transfers between devices, from_behind(): return lax.ppermute(array, axis, pairs)  12.1 us
    pallas_call x1, Pallas kernels, on_device(): pl.pallas_call(functools.partial(project_kernel, sections), out_shape=(ja...  10.4 us
    unnamed x28, local copies, waits for them, and re-layouts  9.11 us
    pallas_call x2, Pallas kernels, finish(): pl.pallas_call(functools.partial(last_kernel, sections, flip), out_shape=...  7.46 us
    pallas_call x1, Pallas kernels, on_device(): pl.pallas_call(functools.partial(near_kernel, sections), out_shape=jax.Sh...  6.19 us
    ppermute x4, starting transfers between devices, from_behind(): return lax.ppermute(array, axis, pairs)  5.3 us
    pallas_call x1, Pallas kernels, on_device(): pl.pallas_call(own_kernel, out_shape=jax.ShapeDtypeStruct((patch, 2 * wid...  2.9 us
  transfers between devices with their start and end apart: 8, of which 4 were waited for; matrix products, arithmetic and copies ran while one was open for 1% of the time, Pallas kernels for 28%

profile of v1, /device:TPU:513, one launch (start us, length us, event | category | flops | bytes accessed | tf_op | source)
XLA Modules:
  0.0 82.7 jit_solution(10056088551441716531)
XLA Ops:
  0.7 1.1 %copy-done = bf16[256,1536]{1,0:T(8,128)(2,1)S(1)} copy-done((bf16[256,1536]{1,0:T(8,128)(2,1)S(1)}, bf16[256,1536]{1,0:T(8,128)(2,1)}, u32[]{:S(2)}) %copy-start) | copy-done | bytes 786456
  1.8 0.7 copy-done.5
  2.5 0.7 copy-done.7
  3.2 2.7 %first.1 = (bf16[256,1536]{1,0:T(8,128)(2,1)}, bf16[256,1536]{1,0:T(8,128)(2,1)S(1)}, bf16[256,1536]{1,0:T(8,128)(2,1)S(1)}) custom-call(s32[1]{0:T(128)} %bitcast.place, s32[64]{0:T(128)S(1)} %copy-done.7, bf16[256,1536]{1,0:T(8,128)(2,1)S(1)} %copy-done, f32[3,1536]{1,0:T(4,128)S(1)} %copy-done.5, bf16[2,512,768]{2,1,0:T(8,128)(2,1)} %stale.3), custom_call_target="tpu_custom_call" | custom-call | flops 3932160 | bytes 3932160 | tf_op jit(solution)/shard_map/first/pallas_call | solution.py:327
  5.9 20.5 %collective-permute-start.2 = (bf16[256,1536]{1,0:T(8,128)(2,1)}, bf16[256,1536]{1,0:T(8,128)(2,1)}, u32[]{:S(2)}, u32[]{:S(2)}) collective-permute-start(bf16[256,1536]{1,0:T(8,128)(2,1)} %get-tuple-element.15.own_half), channel_id=1, source_target_pairs={{0,1},{1,0},{2,3},{3,2},{4,5},{5,4},{6,7},{7,6},{8,9},{9,8},{10,11... | collective-permute-start | bytes 2359304 | tf_op jit(solution)/shard_map/ppermute | solution.py:289
  26.4 1.3 %collective-permute-start = (bf16[256,1536]{1,0:T(8,128)(2,1)S(1)}, bf16[256,1536]{1,0:T(8,128)(2,1)S(1)}, u32[]{:S(2)}, u32[]{:S(2)}) collective-permute-start(bf16[256,1536]{1,0:T(8,128)(2,1)S(1)} %get-tuple-element.13), channel_id=1, source_target_pairs={{0,2},{2,4},{4,6},{6,8},{8,10},{10,12},{12,14},{14,16},{16,18},{18... | collective-permute-start | bytes 2359304 | tf_op jit(solution)/shard_map/ppermute | solution.py:295
  27.8 1.3 %collective-permute-start.1 = (bf16[256,1536]{1,0:T(8,128)(2,1)S(1)}, bf16[256,1536]{1,0:T(8,128)(2,1)S(1)}, u32[]{:S(2)}, u32[]{:S(2)}) collective-permute-start(bf16[256,1536]{1,0:T(8,128)(2,1)S(1)} %get-tuple-element.14), channel_id=1, source_target_pairs={{2,0},{4,2},{6,4},{8,6},{10,8},{12,10},{14,12},{16,14},{18,16},{20... | collective-permute-start | bytes 2359304 | tf_op jit(solution)/shard_map/ppermute | solution.py:295
  29.1 0.0 copy-start.13
  29.1 10.4 %project.1 = (bf16[2,512,768]{2,1,0:T(8,128)(2,1)}, bf16[512,768]{1,0:T(8,128)(2,1)S(1)}, bf16[512,768]{1,0:T(8,128)(2,1)S(1)}, bf16[512,768]{1,0:T(8,128)(2,1)}, bf16[512,768]{1,0:T(8,128)(2,1)}) custom-call(s32[1]{0:T(128)} %bitcast.place, s32[1]{0:T(128)} %bitcast.1.side, s32[64]{0:T(128)S(1)} %copy-done.8, bf16[256,1536]{1,0:T(8,128)(2,1)} %get-tuple-element.15.own_half, ...), custom_call_target="tpu_custom_call" | custom-call | flops 3623878656 | bytes 7077888 | tf_op jit(solution)/shard_map/project/pallas_call | solution.py:342
  39.5 0.0 copy-start.2
  39.5 0.9 %copy-done.2 = bf16[512,768]{1,0:T(8,128)(2,1)} copy-done((bf16[512,768]{1,0:T(8,128)(2,1)}, bf16[512,768]{1,0:T(8,128)(2,1)S(1)}, u32[]{:S(2)}) %copy-start.2) | copy-done | bytes 786456
  40.4 0.9 %copy-done.11 = bf16[512,768]{1,0:T(8,128)(2,1)} copy-done((bf16[512,768]{1,0:T(8,128)(2,1)}, bf16[512,768]{1,0:T(8,128)(2,1)S(1)}, u32[]{:S(2)}) %copy-start.11) | copy-done | bytes 786456
  41.3 3.6 %collective-permute-done.left_own = bf16[256,1536]{1,0:T(8,128)(2,1)S(1)} collective-permute-done((bf16[256,1536]{1,0:T(8,128)(2,1)S(1)}, bf16[256,1536]{1,0:T(8,128)(2,1)S(1)}, u32[]{:S(2)}, u32[]{:S(2)}) %collective-permute-start) | collective-permute-done | bytes 786464 | tf_op jit(solution)/shard_map/ppermute | solution.py:295
  44.8 3.9 %collective-permute-done.1.right_own = bf16[256,1536]{1,0:T(8,128)(2,1)S(1)} collective-permute-done((bf16[256,1536]{1,0:T(8,128)(2,1)S(1)}, bf16[256,1536]{1,0:T(8,128)(2,1)S(1)}, u32[]{:S(2)}, u32[]{:S(2)}) %collective-permute-start.1) | collective-permute-done | bytes 786464 | tf_op jit(solution)/shard_map/ppermute | solution.py:295
  48.7 0.9 %collective-permute-start.3 = (bf16[256,1536]{1,0:T(8,128)(2,1)S(1)}, bf16[256,1536]{1,0:T(8,128)(2,1)}, u32[]{:S(2)}, u32[]{:S(2)}) collective-permute-start(bf16[256,1536]{1,0:T(8,128)(2,1)S(1)} %collective-permute-done.left_own), channel_id=1, source_target_pairs={{0,1},{1,0},{2,3},{3,2},{4,5},{5,4},{6,7},{7,6},{8,9},{9,8},{10,11... | collective-permute-start | bytes 2359304 | tf_op jit(solution)/shard_map/ppermute | solution.py:289
  49.6 1.3 %collective-permute-start.5 = (bf16[512,768]{1,0:T(8,128)(2,1)}, bf16[512,768]{1,0:T(8,128)(2,1)S(1)}, u32[]{:S(2)}, u32[]{:S(2)}) collective-permute-start(bf16[512,768]{1,0:T(8,128)(2,1)} %get-tuple-element.20), channel_id=1, source_target_pairs={{0,2},{2,4},{4,6},{6,8},{8,10},{10,12},{12,14},{14,16},{16,18},{18... | collective-permute-start | bytes 2359304 | tf_op jit(solution)/shard_map/ppermute | solution.py:295
  51.0 1.3 %collective-permute-start.6 = (bf16[512,768]{1,0:T(8,128)(2,1)}, bf16[512,768]{1,0:T(8,128)(2,1)S(1)}, u32[]{:S(2)}, u32[]{:S(2)}) collective-permute-start(bf16[512,768]{1,0:T(8,128)(2,1)} %get-tuple-element.21), channel_id=1, source_target_pairs={{2,0},{4,2},{6,4},{8,6},{10,8},{12,10},{14,12},{16,14},{18,16},{20... | collective-permute-start | bytes 2359304 | tf_op jit(solution)/shard_map/ppermute | solution.py:295
  53.0 0.0 copy-start.3
  53.0 1.1 %copy-done.3 = bf16[512,768]{1,0:T(8,128)(2,1)S(1)} copy-done((bf16[512,768]{1,0:T(8,128)(2,1)S(1)}, bf16[512,768]{1,0:T(8,128)(2,1)}, u32[]{:S(2)}) %copy-start.3) | copy-done | bytes 786456
  54.1 1.1 %copy-done.9 = bf16[2,256,768]{2,1,0:T(8,128)(2,1)S(1)} copy-done((bf16[2,256,768]{2,1,0:T(8,128)(2,1)S(1)}, bf16[2,256,768]{2,1,0:T(8,128)(2,1)}, u32[]{:S(2)}) %copy-start.9) | copy-done | bytes 786456
  55.3 1.4 %copy-done.10 = bf16[2,512,768]{2,1,0:T(8,128)(2,1)S(1)} copy-done((bf16[2,512,768]{2,1,0:T(8,128)(2,1)S(1)}, bf16[2,512,768]{2,1,0:T(8,128)(2,1)}, u32[]{:S(2)}) %copy-start.10) | copy-done | bytes 1572888
  56.7 1.1 %copy-done.12 = bf16[512,768]{1,0:T(8,128)(2,1)S(1)} copy-done((bf16[512,768]{1,0:T(8,128)(2,1)S(1)}, bf16[512,768]{1,0:T(8,128)(2,1)}, u32[]{:S(2)}) %copy-start.12) | copy-done | bytes 786456
  57.8 2.9 %own.1.total = f32[512,1536]{1,0:T(8,128)S(1)} custom-call(s32[1]{0:T(128)} %bitcast.place, s32[1]{0:T(128)S(6)} %copy.12.count, bf16[512,768]{1,0:T(8,128)(2,1)S(1)} %copy-done.3, bf16[512,768]{1,0:T(8,128)(2,1)S(1)} %copy-done.12, bf16[2,512,768]{2,1,0:T(8,128)(2,1)S(1)} %copy-done.10, bf16[2,256,768]{2,1,0:T(8,128)(2,1)S(1)} %copy-done.9, ...), custom_call_target="tpu_custom_call" | custom-call | flops 2415919104 | bytes 2359296 | tf_op jit(solution)/shard_map/own/pallas_call | solution.py:370
  60.7 6.2 %near.1.weights = bf16[6,512,1024]{2,1,0:T(8,128)(2,1)S(1)} custom-call(s32[1]{0:T(128)} %bitcast.place, s32[1]{0:T(128)} %bitcast.1.side, s32[64]{0:T(128)S(1)} %copy-done.8, bf16[256,1536]{1,0:T(8,128)(2,1)S(1)} %collective-permute-done.left_own, bf16[256,1536]{1,0:T(8,128)(2,1)} %collective-permute-done.3.left_other, ...), custom_call_target="tpu_custom_call" | custom-call | flops 4026531840 | bytes 2359296 | tf_op jit(solution)/shard_map/near/pallas_call | solution.py:381
  66.9 0.8 collective-permute-done.5.left_values
  67.7 3.8 %collective-permute-done.6.right_values = bf16[512,768]{1,0:T(8,128)(2,1)S(1)} collective-permute-done((bf16[512,768]{1,0:T(8,128)(2,1)}, bf16[512,768]{1,0:T(8,128)(2,1)S(1)}, u32[]{:S(2)}, u32[]{:S(2)}) %collective-permute-start.6) | collective-permute-done | bytes 786464 | tf_op jit(solution)/shard_map/ppermute | solution.py:295
  71.5 3.7 %last_sent.1 = bf16[256,1536]{1,0:T(8,128)(2,1)S(1)} custom-call(s32[1]{0:T(128)} %bitcast.place, s32[1]{0:T(128)} %bitcast.1.side, bf16[6,512,1024]{2,1,0:T(8,128)(2,1)S(1)} %near.1.weights, bf16[512,768]{1,0:T(8,128)(2,1)S(1)} %collective-permute-done.5.left_values, bf16[512,768]{1,0:T(8,128)(2,1)S(1)} %collective-permute-done.6.right_values, ...), custom_call_target="tpu_custom_call" | custom-call | flops 1409286144 | bytes 2359296 | tf_op jit(solution)/shard_map/last_sent/pallas_call | solution.py:408
  75.3 1.7 %collective-permute-start.7 = (bf16[256,1536]{1,0:T(8,128)(2,1)S(1)}, bf16[256,1536]{1,0:T(8,128)(2,1)S(1)}, u32[]{:S(2)}, u32[]{:S(2)}) collective-permute-start(bf16[256,1536]{1,0:T(8,128)(2,1)S(1)} %last_sent.1), channel_id=1, source_target_pairs={{0,1},{1,0},{2,3},{3,2},{4,5},{5,4},{6,7},{7,6},{8,9},{9,8},{10,11... | collective-permute-start | bytes 2359304 | tf_op jit(solution)/shard_map/ppermute | solution.py:289
  76.9 0.8 slice_reduce_fusion
  77.7 0.0 copy-start.1
  77.7 3.7 %last_kept.1 = bf16[256,1536]{1,0:T(8,128)(2,1)S(1)} custom-call(s32[1]{0:T(128)} %bitcast.place, s32[1]{0:T(128)} %bitcast.1.side, bf16[6,512,1024]{2,1,0:T(8,128)(2,1)S(1)} %near.1.weights, bf16[512,768]{1,0:T(8,128)(2,1)S(1)} %collective-permute-done.5.left_values, bf16[512,768]{1,0:T(8,128)(2,1)S(1)} %collective-permute-done.6.right_values, ...), custom_call_target="tpu_custom_call" | custom-call | flops 1409286144 | bytes 2359296 | tf_op jit(solution)/shard_map/last_kept/pallas_call | solution.py:408
  81.5 1.2 %add_convert_fusion = bf16[256,1536]{1,0:T(8,128)(2,1)} fusion(bf16[256,1536]{1,0:T(8,128)(2,1)S(1)} %collective-permute-done.7, bf16[256,1536]{1,0:T(8,128)(2,1)S(1)} %last_kept.1, bf16[256,1536]{1,0:T(8,128)(2,1)S(1)} %copy-done.1, f32[1536]{0:T(1024)S(1)} %slice_reduce_fusion), kind=kLoop, calls=%fused_computation | loop fusion | flops 2752512 | bytes 3151872 | tf_op jit(solution)/shard_map/convert_element_type | solution.py:430
  (21 shorter events, 0.1 us)
Async XLA Ops:
  0.6 28.5 %copy-start.8 = (s32[64]{0:T(128)S(1)}, s32[64]{0:T(128)}, u32[]{:S(2)}) copy-start(s32[64]{0:T(128)} %order.5) | copy-start | bytes 772
  0.6 28.5 %copy-start.6 = (f32[3,128]{1,0:T(4,128)S(1)}, f32[3,128]{1,0:T(4,128)}, u32[]{:S(2)}) copy-start(f32[3,128]{1,0:T(4,128)} %gains.5) | copy-start | bytes 4612
  0.7 1.1 %copy-start = (bf16[256,1536]{1,0:T(8,128)(2,1)S(1)}, bf16[256,1536]{1,0:T(8,128)(2,1)}, u32[]{:S(2)}) copy-start(bf16[256,1536]{1,0:T(8,128)(2,1)} %x.1) | copy-start | bytes 2359300
  1.8 0.7 copy-start.5
  2.5 0.7 copy-start.7
  5.9 23.2 %collective-permute-start.2 = (bf16[256,1536]{1,0:T(8,128)(2,1)}, bf16[256,1536]{1,0:T(8,128)(2,1)}, u32[]{:S(2)}, u32[]{:S(2)}) collective-permute-start(bf16[256,1536]{1,0:T(8,128)(2,1)} %get-tuple-element.15.own_half), channel_id=1, source_target_pairs={{0,1},{1,0},{2,3},{3,2},{4,5},{5,4},{6,7},{7,6},{8,9},{9,8},{10,11... | collective-permute-start | bytes 2359304 | tf_op jit(solution)/shard_map/ppermute | solution.py:289
  26.4 18.4 %collective-permute-start = (bf16[256,1536]{1,0:T(8,128)(2,1)S(1)}, bf16[256,1536]{1,0:T(8,128)(2,1)S(1)}, u32[]{:S(2)}, u32[]{:S(2)}) collective-permute-start(bf16[256,1536]{1,0:T(8,128)(2,1)S(1)} %get-tuple-element.13), channel_id=1, source_target_pairs={{0,2},{2,4},{4,6},{6,8},{8,10},{10,12},{12,14},{14,16},{16,18},{18... | collective-permute-start | bytes 2359304 | tf_op jit(solution)/shard_map/ppermute | solution.py:295
  27.8 21.0 %collective-permute-start.1 = (bf16[256,1536]{1,0:T(8,128)(2,1)S(1)}, bf16[256,1536]{1,0:T(8,128)(2,1)S(1)}, u32[]{:S(2)}, u32[]{:S(2)}) collective-permute-start(bf16[256,1536]{1,0:T(8,128)(2,1)S(1)} %get-tuple-element.14), channel_id=1, source_target_pairs={{2,0},{4,2},{6,4},{8,6},{10,8},{12,10},{14,12},{16,14},{18,16},{20... | collective-permute-start | bytes 2359304 | tf_op jit(solution)/shard_map/ppermute | solution.py:295
  29.1 23.8 %copy-start.13 = (s32[32768]{0:T(1024)S(1)}, s32[32768]{0:T(1024)}, u32[]{:S(2)}) copy-start(s32[32768]{0:T(1024)} %param.17) | copy-start | bytes 393220
  39.5 0.9 %copy-start.2 = (bf16[512,768]{1,0:T(8,128)(2,1)}, bf16[512,768]{1,0:T(8,128)(2,1)S(1)}, u32[]{:S(2)}) copy-start(bf16[512,768]{1,0:T(8,128)(2,1)S(1)} %get-tuple-element.19.queries) | copy-start | bytes 2359300
  40.4 0.9 %copy-start.11 = (bf16[512,768]{1,0:T(8,128)(2,1)}, bf16[512,768]{1,0:T(8,128)(2,1)S(1)}, u32[]{:S(2)}) copy-start(bf16[512,768]{1,0:T(8,128)(2,1)S(1)} %get-tuple-element.22.keys) | copy-start | bytes 2359300
  48.7 12.0 %collective-permute-start.3 = (bf16[256,1536]{1,0:T(8,128)(2,1)S(1)}, bf16[256,1536]{1,0:T(8,128)(2,1)}, u32[]{:S(2)}, u32[]{:S(2)}) collective-permute-start(bf16[256,1536]{1,0:T(8,128)(2,1)S(1)} %collective-permute-done.left_own), channel_id=1, source_target_pairs={{0,1},{1,0},{2,3},{3,2},{4,5},{5,4},{6,7},{7,6},{8,9},{9,8},{10,11... | collective-permute-start | bytes 2359304 | tf_op jit(solution)/shard_map/ppermute | solution.py:289
  49.6 11.1 %collective-permute-start.4 = (bf16[256,1536]{1,0:T(8,128)(2,1)S(1)}, bf16[256,1536]{1,0:T(8,128)(2,1)}, u32[]{:S(2)}, u32[]{:S(2)}) collective-permute-start(bf16[256,1536]{1,0:T(8,128)(2,1)S(1)} %collective-permute-done.1.right_own), channel_id=1, source_target_pairs={{0,1},{1,0},{2,3},{3,2},{4,5},{5,4},{6,7},{7,6},{8,9},{9,8},{10,11... | collective-permute-start | bytes 2359304 | tf_op jit(solution)/shard_map/ppermute | solution.py:289
  49.6 18.1 %collective-permute-start.5 = (bf16[512,768]{1,0:T(8,128)(2,1)}, bf16[512,768]{1,0:T(8,128)(2,1)S(1)}, u32[]{:S(2)}, u32[]{:S(2)}) collective-permute-start(bf16[512,768]{1,0:T(8,128)(2,1)} %get-tuple-element.20), channel_id=1, source_target_pairs={{0,2},{2,4},{4,6},{6,8},{8,10},{10,12},{12,14},{14,16},{16,18},{18... | collective-permute-start | bytes 2359304 | tf_op jit(solution)/shard_map/ppermute | solution.py:295
  51.0 20.5 %collective-permute-start.6 = (bf16[512,768]{1,0:T(8,128)(2,1)}, bf16[512,768]{1,0:T(8,128)(2,1)S(1)}, u32[]{:S(2)}, u32[]{:S(2)}) collective-permute-start(bf16[512,768]{1,0:T(8,128)(2,1)} %get-tuple-element.21), channel_id=1, source_target_pairs={{2,0},{4,2},{6,4},{8,6},{10,8},{12,10},{14,12},{16,14},{18,16},{20... | collective-permute-start | bytes 2359304 | tf_op jit(solution)/shard_map/ppermute | solution.py:295
  53.0 1.1 %copy-start.3 = (bf16[512,768]{1,0:T(8,128)(2,1)S(1)}, bf16[512,768]{1,0:T(8,128)(2,1)}, u32[]{:S(2)}) copy-start(bf16[512,768]{1,0:T(8,128)(2,1)} %copy-done.2) | copy-start | bytes 2359300
  54.1 1.1 %copy-start.9 = (bf16[2,256,768]{2,1,0:T(8,128)(2,1)S(1)}, bf16[2,256,768]{2,1,0:T(8,128)(2,1)}, u32[]{:S(2)}) copy-start(bf16[2,256,768]{2,1,0:T(8,128)(2,1)} %text.1) | copy-start | bytes 2359300
  55.3 1.4 %copy-start.10 = (bf16[2,512,768]{2,1,0:T(8,128)(2,1)S(1)}, bf16[2,512,768]{2,1,0:T(8,128)(2,1)}, u32[]{:S(2)}) copy-start(bf16[2,512,768]{2,1,0:T(8,128)(2,1)} %get-tuple-element.12.cache) | copy-start | bytes 4718596
  56.7 1.1 %copy-start.12 = (bf16[512,768]{1,0:T(8,128)(2,1)S(1)}, bf16[512,768]{1,0:T(8,128)(2,1)}, u32[]{:S(2)}) copy-start(bf16[512,768]{1,0:T(8,128)(2,1)} %copy-done.11) | copy-start | bytes 2359300
  57.8 2.9 %copy-start.4 = (bf16[512,768]{1,0:T(8,128)(2,1)S(1)}, bf16[512,768]{1,0:T(8,128)(2,1)}, u32[]{:S(2)}) copy-start(bf16[512,768]{1,0:T(8,128)(2,1)} %copy-done.2) | copy-start | bytes 2359300
  75.3 6.2 %collective-permute-start.7 = (bf16[256,1536]{1,0:T(8,128)(2,1)S(1)}, bf16[256,1536]{1,0:T(8,128)(2,1)S(1)}, u32[]{:S(2)}, u32[]{:S(2)}) collective-permute-start(bf16[256,1536]{1,0:T(8,128)(2,1)S(1)} %last_sent.1), channel_id=1, source_target_pairs={{0,1},{1,0},{2,3},{3,2},{4,5},{5,4},{6,7},{7,6},{8,9},{9,8},{10,11... | collective-permute-start | bytes 2359304 | tf_op jit(solution)/shard_map/ppermute | solution.py:289
  77.7 3.8 %copy-start.1 = (bf16[256,1536]{1,0:T(8,128)(2,1)S(1)}, bf16[256,1536]{1,0:T(8,128)(2,1)}, u32[]{:S(2)}) copy-start(bf16[256,1536]{1,0:T(8,128)(2,1)} %x.1) | copy-start | bytes 2359300

commit v2 on v1

v2 whole, which is shorter than its diff:
```python
import functools
import math

import jax
import jax.numpy as jnp
from jax import lax
from jax.experimental import pallas as pl
from jax.experimental.pallas import tpu as pltpu
from jax.sharding import PartitionSpec as P


epsilon = 1e-06
f32 = jnp.float32
bf16 = jnp.bfloat16
MIB = 1024 * 1024

VMEM = pl.BlockSpec(memory_space=pltpu.VMEM)
SMEM = pl.BlockSpec(memory_space=pltpu.SMEM)
HBM = pl.BlockSpec(memory_space=pltpu.HBM)


def params(mib):
    return pltpu.CompilerParams(vmem_limit_bytes=mib * MIB)


def in_hbm(array):
    return pltpu.with_memory_space_constraint(array, pltpu.HBM)


def cost(flops, nbytes):
    return pl.CostEstimate(flops=flops, bytes_accessed=nbytes, transcendentals=0)


def slots(place, order, sections):
    p = place[0]
    left = jnp.maximum(p - 1, 0)
    right = jnp.minimum(p + 1, sections - 1)
    return order[p], order[left], order[right]


def gain_row(gains, which):
    return gains[which : which + 1, :]


def head_normed(part, gain):
    spread = jnp.mean(part * part, axis=-1, keepdims=True)
    return (part * lax.rsqrt(spread + epsilon) * gain).astype(bf16)


def heads_normed(part, gain):
    size = gain.shape[-1]
    pieces = [
        head_normed(part[:, i : i + size], gain) for i in range(0, part.shape[-1], size)
    ]
    return jnp.concatenate(pieces, axis=-1)


def mask_columns(row, lanes):
    return jnp.broadcast_to(row, (lanes, row.shape[1])).T.astype(bf16)


def first_kernel(
    sections, place, order_in, x_in, mod_in, stale, normed, to_right, to_left, values,
    order, x, mod, held, sems,
):
    copies = [
        pltpu.make_async_copy(source, target, sems.at[i])
        for i, (source, target) in enumerate(
            (
                (order_in, order),
                (x_in, x),
                (mod_in, mod),
                (stale.at[0], held),
                (stale.at[1], values),
            )
        )
    ]
    for copy in copies:
        copy.start()
    rows, width = x.shape
    for copy in copies[:3]:
        copy.wait()
    scale = 1.0 + mod[1:2, :]
    shift = mod[0:1, :]
    step = 64
    for r in range(0, rows, step):
        v = x[r : r + step, :].astype(f32)
        shifted = v - jnp.mean(v, axis=-1, keepdims=True)
        spread = jnp.mean(shifted * shifted, axis=-1, keepdims=True)
        normed[r : r + step, :] = (shifted * lax.rsqrt(spread + epsilon) * scale + shift).astype(
            bf16
        )
    copies[3].wait()
    own, left, right = slots(place, order, sections)
    half = width // 2

    def fill(out, fresh):
        @pl.when(fresh)
        def _():
            out[...] = normed[...]

        @pl.when(jnp.logical_not(fresh))
        def _():
            out[:, :half] = held[:rows, :]
            out[:, half:] = held[rows:, :]

    fill(to_right, own < right)
    fill(to_left, own < left)
    copies[4].wait()


def attend(queries, keys, vbuf):
    s = lax.dot_general(queries, keys, (((1,), (1,)), ((), ())), preferred_element_type=f32)
    return jnp.dot(jnp.exp2(s).astype(bf16), vbuf, preferred_element_type=f32)


def project_kernel(
    place,
    side,
    count,
    own_half,
    other_half,
    weight,
    gains,
    text,
    keep,
    cache,
    queries,
    total,
    key_weight,
    value_weight,
    query_weight,
    keys,
    vbuf,
    sems,
):
    rows = own_half.shape[0]
    patch, width = queries.shape
    text_rows = text.shape[1]
    size = gains.shape[1]
    block = 2 * size
    buffers = {2: value_weight, 1: key_weight, 0: query_weight}
    pieces = ((2, 0, block), (2, block, width), (1, 0, width), (0, 0, width))
    copies = []
    for n, (c, low, high) in enumerate(pieces):
        copy = pltpu.make_async_copy(
            weight.at[c, :, low:high], buffers[c].at[:, low:high], sems.at[n]
        )
        copy.start()
        copies.append(copy)
    own_mask = mask_columns((keep[pl.ds(place[0], 1), :] > 0).astype(f32), size)
    live = lax.broadcasted_iota(jnp.int32, (text_rows, size), 0) < count[0]
    text_mask = live.astype(f32).astype(bf16)
    heads = width // size
    text_gain = gain_row(gains, 2)
    for i in range(heads):
        cols = slice(i * size, (i + 1) * size)
        keys[patch:, cols] = head_normed(text[0, :, cols].astype(f32), text_gain)
        vbuf[i, :patch, size:] = own_mask
        vbuf[i, patch:, size:] = text_mask
        vbuf[i, patch:, :size] = text[1, :, cols] * text_mask
    h = side[0]
    places = (
        (own_half, pl.multiple_of(h * rows, rows)),
        (other_half, pl.multiple_of((1 - h) * rows, rows)),
    )
    factor = math.log2(math.e) * size**-0.5
    query_gain = gain_row(gains, 0) * factor
    key_gain = gain_row(gains, 1)
    for n, (c, low, high) in enumerate(pieces):
        copies[n].wait()
        for j in range(low, high, block):
            cols = slice(j, j + block)
            for half, at in places:
                y = jnp.dot(half[...], buffers[c][:, cols], preferred_element_type=f32)
                at = pl.ds(at, rows)
                if c == 0:
                    queries[at, cols] = heads_normed(y, query_gain)
                else:
                    rounded = y.astype(bf16)
                    cache[c - 1, at, cols] = rounded
                    if c == 1:
                        keys[at, cols] = heads_normed(rounded.astype(f32), key_gain)
    for i in range(heads):
        cols = slice(i * size, (i + 1) * size)
        vbuf[i, :patch, :size] = cache[1, :, cols] * own_mask
        total[:, 2 * i * size : 2 * (i + 1) * size] = attend(
            queries[:, cols], keys[:, cols], vbuf[i]
        )


def side_mask(keep, place, sections, by, size):
    wanted = place[0] + by
    there = (wanted >= 0) & (wanted < sections)
    row = keep[pl.ds(jnp.clip(wanted, 0, sections - 1), 1), :]
    return mask_columns(((row > 0) & there).astype(f32), size)


def add_side(queries, keys, vbuf, total, size):
    for i in range(queries.shape[1] // size):
        cols = slice(i * size, (i + 1) * size)
        wide = slice(2 * i * size, 2 * (i + 1) * size)
        total[:, wide] += attend(queries[:, cols], keys[:, cols], vbuf[i])


def fresh_kernel(
    sections,
    place,
    side,
    order,
    left_own,
    left_other,
    right_own,
    right_other,
    key_weight,
    value_weight,
    gains,
    queries,
    keep,
    total_in,
    total,
    keys,
    vbuf,
):
    rows = left_own.shape[0]
    _, width = queries.shape
    size = gains.shape[1]
    block = 2 * size
    h = side[0]
    own, left, right = slots(place, order, sections)
    gain = gain_row(gains, 1)
    total[...] = total_in[...]
    for mine, other, fresh, by in (
        (left_own, left_other, left < own, -1),
        (right_own, right_other, right < own, 1),
    ):

        @pl.when(fresh)
        def _():
            mask = side_mask(keep, place, sections, by, size)
            for i in range(width // size):
                vbuf[i, :, size:] = mask
            for half, at in ((mine, h), (other, 1 - h)):
                at = pl.ds(pl.multiple_of(at * rows, rows), rows)
                for j in range(0, width, block):
                    cols = slice(j, j + block)
                    y = jnp.dot(half[...], key_weight[:, cols], preferred_element_type=f32)
                    keys[at, cols] = heads_normed(y.astype(bf16).astype(f32), gain)
                for j in range(0, width, block):
                    cols = slice(j, j + block)
                    y = jnp.dot(half[...], value_weight[:, cols], preferred_element_type=f32)
                    y = y.astype(bf16)
                    for i in range(block // size):
                        vbuf[j // size + i, at, :size] = (
                            y[:, i * size : (i + 1) * size] * vbuf[0, at, size:]
                        )
            add_side(queries, keys, vbuf, total, size)


def stale_kernel(
    sections,
    place,
    side,
    order,
    left_keys,
    left_values,
    right_keys,
    right_values,
    gains,
    queries,
    keep,
    total_in,
    weight,
    sent,
    kept,
    keys,
    vbuf,
    total,
    att,
):
    rows = sent.shape[0]
    patch, width = queries.shape
    size = gains.shape[1]
    p = place[0]
    h = side[0]
    own, left, right = slots(place, order, sections)
    gain = gain_row(gains, 1)
    total[...] = total_in[...]
    for raw, values, wanted, by in (
        (left_keys, left_values, (left > own) & (p > 0), -1),
        (right_keys, right_values, (right > own) & (p < sections - 1), 1),
    ):

        @pl.when(wanted)
        def _():
            mask = side_mask(keep, place, sections, by, size)
            for r in range(patch // rows):
                keys[r * rows : (r + 1) * rows, :] = heads_normed(
                    raw[:, r * width : (r + 1) * width].astype(f32), gain
                )
            for i in range(width // size):
                cols = slice(i * size, (i + 1) * size)
                vbuf[i, :, size:] = mask
                vbuf[i, :, :size] = values[:, cols] * mask
            add_side(queries, keys, vbuf, total, size)

    for i in range(width // size):
        low = 2 * i * size
        att[:, i * size : (i + 1) * size] = (
            total[:, low : low + size] / total[:, low + size : low + 2 * size]
        ).astype(bf16)
    for out, at in ((sent, 1 - h), (kept, h)):
        at = pl.ds(pl.multiple_of(at * rows, rows), rows)
        out[...] = jnp.dot(att[at, :], weight[...], preferred_element_type=f32).astype(bf16)


def swapped(array):
    return lax.ppermute(array, "head", [(0, 1), (1, 0)])


def from_behind(array, axis, by):
    count = lax.axis_size(axis)
    pairs = [(i, i + by) for i in range(count) if 0 <= i + by < count]
    return lax.ppermute(array, axis, pairs)


def on_device(
    video_tokens,
    modulation,
    project_weight,
    output_weight,
    norm_gains,
    text_cache,
    text_count,
    video_keep,
    patch_order,
    stale_cache,
):
    sections = lax.axis_size("section")
    place = lax.axis_index("section").astype(jnp.int32).reshape(1)
    side = lax.axis_index("head").astype(jnp.int32).reshape(1)
    rows, model = video_tokens.shape
    size = norm_gains.shape[1]
    width = project_weight.shape[2]
    heads = width // size
    patch = stale_cache.shape[1]
    text_rows = text_cache.shape[1]
    keep = video_keep.reshape(sections, patch)
    half_shape = jax.ShapeDtypeStruct((rows, model), bf16)
    side_shape = jax.ShapeDtypeStruct((patch, width), bf16)
    weight_shape = jax.ShapeDtypeStruct((model, width), bf16)
    total_shape = jax.ShapeDtypeStruct((patch, 2 * width), f32)

    normed, to_right, to_left, values = pl.pallas_call(
        functools.partial(first_kernel, sections),
        out_shape=(half_shape, half_shape, half_shape, side_shape),
        in_specs=[SMEM, HBM, HBM, HBM, HBM],
        out_specs=(VMEM,) * 4,
        scratch_shapes=[
            pltpu.SMEM(patch_order.shape, jnp.int32),
            pltpu.VMEM((rows, model), bf16),
            pltpu.VMEM(modulation.shape, f32),
            pltpu.VMEM((patch, width), bf16),
            pltpu.SemaphoreType.DMA((5,)),
        ],
        compiler_params=params(10),
        cost_estimate=cost(10 * rows * model, 10 * rows * model),
        name="first",
    )(
        place,
        in_hbm(patch_order),
        in_hbm(video_tokens),
        in_hbm(modulation),
        in_hbm(stale_cache),
    )

    left_own = from_behind(to_right, "section", 1)
    right_own = from_behind(to_left, "section", -1)
    left_values = from_behind(values, "section", 1)
    right_values = from_behind(values, "section", -1)
    other = swapped(normed)

    fresh_cache, queries, total, key_weight, value_weight = pl.pallas_call(
        project_kernel,
        out_shape=(
            jax.ShapeDtypeStruct((2, patch, width), bf16),
            side_shape,
            total_shape,
            weight_shape,
            weight_shape,
        ),
        in_specs=[SMEM, SMEM, SMEM, VMEM, VMEM, HBM, VMEM, VMEM, VMEM],
        out_specs=(VMEM,) * 5,
        scratch_shapes=[
            pltpu.VMEM((model, width), bf16),
            pltpu.VMEM((patch + text_rows, width), bf16),
            pltpu.VMEM((heads, patch + text_rows, 2 * size), bf16),
            pltpu.SemaphoreType.DMA((4,)),
        ],
        compiler_params=params(28),
        cost_estimate=cost(2 * patch * model * 3 * width, 6 * model * width),
        name="project",
    )(
        place,
        side,
        text_count,
        normed,
        other,
        in_hbm(project_weight),
        norm_gains,
        text_cache,
        keep,
    )

    left_own, right_own, queries = lax.optimization_barrier((left_own, right_own, queries))
    left_other = swapped(left_own)
    right_other = swapped(right_own)

    total = pl.pallas_call(
        functools.partial(fresh_kernel, sections),
        out_shape=total_shape,
        in_specs=[SMEM] * 3 + [VMEM] * 10,
        out_specs=VMEM,
        scratch_shapes=[
            pltpu.VMEM((patch, width), bf16),
            pltpu.VMEM((heads, patch, 2 * size), bf16),
        ],
        input_output_aliases={12: 0},
        compiler_params=params(24),
        cost_estimate=cost(4 * patch * model * width, 6 * patch * width),
        name="fresh",
    )(
        place,
        side,
        patch_order,
        left_own,
        left_other,
        right_own,
        right_other,
        key_weight,
        value_weight,
        norm_gains,
        queries,
        keep,
        total,
    )

    sent, kept = pl.pallas_call(
        functools.partial(stale_kernel, sections),
        out_shape=(half_shape, half_shape),
        in_specs=[SMEM] * 3 + [VMEM] * 9,
        out_specs=(VMEM, VMEM),
        scratch_shapes=[
            pltpu.VMEM((patch, width), bf16),
            pltpu.VMEM((heads, patch, 2 * size), bf16),
            pltpu.VMEM((patch, 2 * width), f32),
            pltpu.VMEM((patch, width), bf16),
        ],
        compiler_params=params(24),
        cost_estimate=cost(2 * patch * width * model, 6 * patch * width),
        name="stale",
    )(
        place,
        side,
        patch_order,
        left_own,
        left_values,
        right_own,
        right_values,
        norm_gains,
        queries,
        keep,
        total,
        output_weight,
    )
    received = swapped(sent)
    mixed = kept.astype(f32) + received.astype(f32)
    updated = (video_tokens.astype(f32) + modulation[2] * mixed).astype(bf16)
    return (updated, fresh_cache)


def solution(mesh):
    placed = (
        P(("groups", "section", "head"), None),
        P("groups", None),
        P(None, None, "head"),
        P("head", None),
        P(),
        P(None, "groups", "head"),
        P("groups"),
        P("groups"),
        P("groups"),
        P(None, ("groups", "section"), "head"),
    )

    return jax.shard_map(
        on_device,
        mesh=mesh,
        in_specs=placed,
        out_specs=(P(("groups", "section", "head"), None), P(None, ("groups", "section"), "head")),
        check_vma=False,
    )
```

time: 83.4 us -> 79.6 us (0.954)
  waiting for transfers between devices: 12.1 us -> 28 us
  Pallas kernels: 29.6 us -> 19.3 us
  local copies, waits for them, and re-layouts: 9.89 us -> 0.81 us
    ppermute x4, waiting for transfers between devices: 12.1 us -> 26.5 us  [from_behind(): return lax.ppermute(array, axis, pairs)]
    pallas_call x5 -> x3, Pallas kernels: 26.9 us -> 16 us  [the longest x1 10.1 us: on_device(): pl.pallas_call(project_kernel, out_shape=(jax.ShapeDtypeStruct((2, patch,...]
    unnamed x28 -> x12, local copies, waits for them, and re-layouts: 9.11 us -> 0.03 us
    ppermute x4, waiting for transfers between devices: 0.01 us -> 1.51 us  [swapped(): return lax.ppermute(array, 'head', [(0, 1), (1, 0)])]
  transfers between devices with their start and end apart: 8 -> 8, of which waited for: 4 -> 6; matrix products, arithmetic and copies ran while one was open for 1% -> 1% of each run, Pallas kernels for 28% -> 14%
where the time goes in v2:
time: 79.6 us; the launch traced here: 79.3 us
  starting transfers between devices  28.5 us (36%)
  waiting for transfers between devices  28 us (35%)
  Pallas kernels  19.3 us (24%)
  between operations  1.45 us (2%)
  other arithmetic  1.21 us (2%)
  local copies, waits for them, and re-layouts  0.81 us (1%)
    ppermute x4, waiting for transfers between devices, from_behind(): return lax.ppermute(array, axis, pairs)  26.5 us
    ppermute x4, starting transfers between devices, swapped(): return lax.ppermute(array, 'head', [(0, 1), (1, 0)])  23.2 us
    pallas_call x1, Pallas kernels, on_device(): pl.pallas_call(project_kernel, out_shape=(jax.ShapeDtypeStruct((2, patch,...  10.1 us
    ppermute x4, starting transfers between devices, from_behind(): return lax.ppermute(array, axis, pairs)  5.3 us
    pallas_call x1, Pallas kernels, on_device(): pl.pallas_call(functools.partial(stale_kernel, sections), out_shape=(half...  4.78 us
    pallas_call x1, Pallas kernels, on_device(): pl.pallas_call(functools.partial(first_kernel, sections), out_shape=(half...  3.34 us
  transfers between devices with their start and end apart: 8, of which 6 were waited for; matrix products, arithmetic and copies ran while one was open for 1% of the time, Pallas kernels for 14%

profile of v2, /device:TPU:513, one launch (start us, length us, event | category | flops | bytes accessed | tf_op | source)
XLA Modules:
  0.0 79.3 jit_solution(14353730234277221770)
XLA Ops:
  0.6 0.0 copy-start.5
  0.6 0.0 copy-start.1
  0.7 0.0 copy-start.3
  0.7 3.3 %first.1 = (bf16[256,1536]{1,0:T(8,128)(2,1)}, bf16[256,1536]{1,0:T(8,128)(2,1)}, bf16[256,1536]{1,0:T(8,128)(2,1)}, bf16[512,768]{1,0:T(8,128)(2,1)S(1)}) custom-call(s32[1]{0:T(128)} %bitcast.place, s32[64]{0:T(128)} %order.3, bf16[256,1536]{1,0:T(8,128)(2,1)} %x_in.1, f32[3,1536]{1,0:T(4,128)} %mod_in.1, bf16[2,512,768]{2,1,0:T(8,128)(2,1)} %stale.2), custom_call_target="tpu_custom_call" | custom-call | flops 3932160 | bytes 3932160 | tf_op jit(solution)/shard_map/first/pallas_call | solution.py:354
  4.0 20.5 %collective-permute-start.2 = (bf16[256,1536]{1,0:T(8,128)(2,1)}, bf16[256,1536]{1,0:T(8,128)(2,1)}, u32[]{:S(2)}, u32[]{:S(2)}) collective-permute-start(bf16[256,1536]{1,0:T(8,128)(2,1)} %get-tuple-element.18.own_half), channel_id=1, source_target_pairs={{0,1},{1,0},{2,3},{3,2},{4,5},{5,4},{6,7},{7,6},{8,9},{9,8},{10,11... | collective-permute-start | bytes 2359304 | tf_op jit(solution)/shard_map/ppermute | solution.py:318
  24.6 1.3 %collective-permute-start = (bf16[256,1536]{1,0:T(8,128)(2,1)}, bf16[256,1536]{1,0:T(8,128)(2,1)S(1)}, u32[]{:S(2)}, u32[]{:S(2)}) collective-permute-start(bf16[256,1536]{1,0:T(8,128)(2,1)} %get-tuple-element.16), channel_id=1, source_target_pairs={{0,2},{2,4},{4,6},{6,8},{8,10},{10,12},{12,14},{14,16},{16,18},{18... | collective-permute-start | bytes 2359304 | tf_op jit(solution)/shard_map/ppermute | solution.py:324
  25.9 1.3 %collective-permute-start.1 = (bf16[256,1536]{1,0:T(8,128)(2,1)}, bf16[256,1536]{1,0:T(8,128)(2,1)S(1)}, u32[]{:S(2)}, u32[]{:S(2)}) collective-permute-start(bf16[256,1536]{1,0:T(8,128)(2,1)} %get-tuple-element.17), channel_id=1, source_target_pairs={{2,0},{4,2},{6,4},{8,6},{10,8},{12,10},{14,12},{16,14},{18,16},{20... | collective-permute-start | bytes 2359304 | tf_op jit(solution)/shard_map/ppermute | solution.py:324
  27.2 0.0 copy-done.5
  27.9 0.0 collective-permute-done.2.other_half
  27.9 0.0 copy-done.1
  27.9 0.0 copy-done.3
  27.9 0.0 copy-start.2
  28.0 10.1 %project.1 = (bf16[2,512,768]{2,1,0:T(8,128)(2,1)}, bf16[512,768]{1,0:T(8,128)(2,1)S(1)}, f32[512,1536]{1,0:T(8,128)S(1)}, bf16[1536,768]{1,0:T(8,128)(2,1)S(1)}, bf16[1536,768]{1,0:T(8,128)(2,1)S(1)}) custom-call(s32[1]{0:T(128)} %bitcast.place, s32[1]{0:T(128)} %bitcast.1.side, s32[1]{0:T(128)S(6)} %copy.14.count, ...), custom_call_target="tpu_custom_call" | custom-call | flops 3623878656 | bytes 7077888 | tf_op jit(solution)/shard_map/project/pallas_call | solution.py:383
  38.0 5.3 %collective-permute-done.left_own.left_keys = bf16[256,1536]{1,0:T(8,128)(2,1)S(1)} collective-permute-done((bf16[256,1536]{1,0:T(8,128)(2,1)}, bf16[256,1536]{1,0:T(8,128)(2,1)S(1)}, u32[]{:S(2)}, u32[]{:S(2)}) %collective-permute-start) | collective-permute-done | bytes 786464 | tf_op jit(solution)/shard_map/ppermute | solution.py:324
  43.3 3.8 %collective-permute-done.1.right_own.right_keys = bf16[256,1536]{1,0:T(8,128)(2,1)S(1)} collective-permute-done((bf16[256,1536]{1,0:T(8,128)(2,1)}, bf16[256,1536]{1,0:T(8,128)(2,1)S(1)}, u32[]{:S(2)}, u32[]{:S(2)}) %collective-permute-start.1) | collective-permute-done | bytes 786464 | tf_op jit(solution)/shard_map/ppermute | solution.py:324
  47.1 0.9 %collective-permute-start.5 = (bf16[256,1536]{1,0:T(8,128)(2,1)S(1)}, bf16[256,1536]{1,0:T(8,128)(2,1)S(1)}, u32[]{:S(2)}, u32[]{:S(2)}) collective-permute-start(bf16[256,1536]{1,0:T(8,128)(2,1)S(1)} %collective-permute-done.left_own.left_keys), channel_id=1, source_target_pairs={{0,1},{1,0},{2,3},{3,2},{4,5},{5,4},{6,7},{7,6},{8,9},{9,8},{10,11... | collective-permute-start | bytes 2359304 | tf_op jit(solution)/shard_map/ppermute | solution.py:318
  48.0 0.0 collective-permute-start.6
  48.0 1.3 %collective-permute-start.3 = (bf16[512,768]{1,0:T(8,128)(2,1)S(1)}, bf16[512,768]{1,0:T(8,128)(2,1)S(1)}, u32[]{:S(2)}, u32[]{:S(2)}) collective-permute-start(bf16[512,768]{1,0:T(8,128)(2,1)S(1)} %get-tuple-element.21), channel_id=1, source_target_pairs={{0,2},{2,4},{4,6},{6,8},{8,10},{10,12},{12,14},{14,16},{16,18},{18... | collective-permute-start | bytes 2359304 | tf_op jit(solution)/shard_map/ppermute | solution.py:324
  49.3 1.3 %collective-permute-start.4 = (bf16[512,768]{1,0:T(8,128)(2,1)S(1)}, bf16[512,768]{1,0:T(8,128)(2,1)S(1)}, u32[]{:S(2)}, u32[]{:S(2)}) collective-permute-start(bf16[512,768]{1,0:T(8,128)(2,1)S(1)} %get-tuple-element.21), channel_id=1, source_target_pairs={{2,0},{4,2},{6,4},{8,6},{10,8},{12,10},{14,12},{16,14},{18,16},{20... | collective-permute-start | bytes 2359304 | tf_op jit(solution)/shard_map/ppermute | solution.py:324
  50.7 0.0 collective-permute-done.5.left_other
  50.7 0.4 collective-permute-done.6.right_other
  51.0 0.0 copy-done.2
  51.0 1.1 %fresh.1.total_in = f32[512,1536]{1,0:T(8,128)S(1)} custom-call(s32[1]{0:T(128)} %bitcast.place, s32[1]{0:T(128)} %bitcast.1.side, s32[64]{0:T(128)S(1)} %copy-done.2, bf16[256,1536]{1,0:T(8,128)(2,1)S(1)} %collective-permute-done.left_own.left_keys, bf16[256,1536]{1,0:T(8,128)(2,1)S(1)} %collective-permute-done.5.left_other, ...), custom_call_target="tpu_custom_call", output_to_operand_aliasing={{}: (12, {})} | custom-call | flops 2415919104 | bytes 2359296 | tf_op jit(solution)/shard_map/fresh/pallas_call | solution.py:419
  52.2 0.0 copy-start.4
  52.2 13.5 %collective-permute-done.3.left_values = bf16[512,768]{1,0:T(8,128)(2,1)S(1)} collective-permute-done((bf16[512,768]{1,0:T(8,128)(2,1)S(1)}, bf16[512,768]{1,0:T(8,128)(2,1)S(1)}, u32[]{:S(2)}, u32[]{:S(2)}) %collective-permute-start.3) | collective-permute-done | bytes 786464 | tf_op jit(solution)/shard_map/ppermute | solution.py:324
  65.7 3.9 %collective-permute-done.4.right_values = bf16[512,768]{1,0:T(8,128)(2,1)S(1)} collective-permute-done((bf16[512,768]{1,0:T(8,128)(2,1)S(1)}, bf16[512,768]{1,0:T(8,128)(2,1)S(1)}, u32[]{:S(2)}, u32[]{:S(2)}) %collective-permute-start.4) | collective-permute-done | bytes 786464 | tf_op jit(solution)/shard_map/ppermute | solution.py:324
  69.6 0.0 copy-done
  69.6 4.8 %stale.3 = (bf16[256,1536]{1,0:T(8,128)(2,1)S(1)}, bf16[256,1536]{1,0:T(8,128)(2,1)S(1)}) custom-call(s32[1]{0:T(128)} %bitcast.place, s32[1]{0:T(128)} %bitcast.1.side, s32[64]{0:T(128)S(1)} %copy-done.2, bf16[256,1536]{1,0:T(8,128)(2,1)S(1)} %collective-permute-done.left_own.left_keys, bf16[512,768]{1,0:T(8,128)(2,1)S(1)} %collective-permute-done.3.left_values, ...), custom_call_target="tpu_custom_call" | custom-call | flops 1207959552 | bytes 2359296 | tf_op jit(solution)/shard_map/stale/pallas_call | solution.py:448
  74.4 1.8 %collective-permute-start.7 = (bf16[256,1536]{1,0:T(8,128)(2,1)S(1)}, bf16[256,1536]{1,0:T(8,128)(2,1)S(1)}, u32[]{:S(2)}, u32[]{:S(2)}) collective-permute-start(bf16[256,1536]{1,0:T(8,128)(2,1)S(1)} %get-tuple-element.28), channel_id=1, source_target_pairs={{0,1},{1,0},{2,3},{3,2},{4,5},{5,4},{6,7},{7,6},{8,9},{9,8},{10,11... | collective-permute-start | bytes 2359304 | tf_op jit(solution)/shard_map/ppermute | solution.py:318
  76.1 0.8 slice_reduce_fusion
  76.9 1.1 %collective-permute-done.7 = bf16[256,1536]{1,0:T(8,128)(2,1)S(1)} collective-permute-done((bf16[256,1536]{1,0:T(8,128)(2,1)S(1)}, bf16[256,1536]{1,0:T(8,128)(2,1)S(1)}, u32[]{:S(2)}, u32[]{:S(2)}) %collective-permute-start.7) | collective-permute-done | bytes 786464 | tf_op jit(solution)/shard_map/ppermute | solution.py:318
  78.1 1.2 %add_convert_fusion = bf16[256,1536]{1,0:T(8,128)(2,1)} fusion(bf16[256,1536]{1,0:T(8,128)(2,1)S(1)} %collective-permute-done.7, bf16[256,1536]{1,0:T(8,128)(2,1)S(1)} %get-tuple-element.27, bf16[256,1536]{1,0:T(8,128)(2,1)S(1)} %copy-done.4, f32[1536]{0:T(1024)S(1)} %slice_reduce_fusion), kind=kLoop, calls=%fused_computation | loop fusion | flops 2752512 | bytes 3151872 | tf_op jit(solution)/shard_map/convert_element_type | solution.py:478
  (3 shorter events, 0.0 us)
Async XLA Ops:
  0.6 26.6 %copy-start.5 = (s32[32768]{0:T(1024)S(1)}, s32[32768]{0:T(1024)}, u32[]{:S(2)}) copy-start(s32[32768]{0:T(1024)} %param.17) | copy-start | bytes 393220
  0.6 27.3 %copy-start.1 = (f32[3,128]{1,0:T(4,128)S(1)}, f32[3,128]{1,0:T(4,128)}, u32[]{:S(2)}) copy-start(f32[3,128]{1,0:T(4,128)} %gains.5) | copy-start | bytes 4612
  0.7 27.3 %copy-start.3 = (bf16[2,256,768]{2,1,0:T(8,128)(2,1)S(1)}, bf16[2,256,768]{2,1,0:T(8,128)(2,1)}, u32[]{:S(2)}) copy-start(bf16[2,256,768]{2,1,0:T(8,128)(2,1)} %text.1) | copy-start | bytes 2359300
  4.0 23.9 %collective-permute-start.2 = (bf16[256,1536]{1,0:T(8,128)(2,1)}, bf16[256,1536]{1,0:T(8,128)(2,1)}, u32[]{:S(2)}, u32[]{:S(2)}) collective-permute-start(bf16[256,1536]{1,0:T(8,128)(2,1)} %get-tuple-element.18.own_half), channel_id=1, source_target_pairs={{0,1},{1,0},{2,3},{3,2},{4,5},{5,4},{6,7},{7,6},{8,9},{9,8},{10,11... | collective-permute-start | bytes 2359304 | tf_op jit(solution)/shard_map/ppermute | solution.py:318
  24.6 18.7 %collective-permute-start = (bf16[256,1536]{1,0:T(8,128)(2,1)}, bf16[256,1536]{1,0:T(8,128)(2,1)S(1)}, u32[]{:S(2)}, u32[]{:S(2)}) collective-permute-start(bf16[256,1536]{1,0:T(8,128)(2,1)} %get-tuple-element.16), channel_id=1, source_target_pairs={{0,2},{2,4},{4,6},{6,8},{8,10},{10,12},{12,14},{14,16},{16,18},{18... | collective-permute-start | bytes 2359304 | tf_op jit(solution)/shard_map/ppermute | solution.py:324
  25.9 21.2 %collective-permute-start.1 = (bf16[256,1536]{1,0:T(8,128)(2,1)}, bf16[256,1536]{1,0:T(8,128)(2,1)S(1)}, u32[]{:S(2)}, u32[]{:S(2)}) collective-permute-start(bf16[256,1536]{1,0:T(8,128)(2,1)} %get-tuple-element.17), channel_id=1, source_target_pairs={{2,0},{4,2},{6,4},{8,6},{10,8},{12,10},{14,12},{16,14},{18,16},{20... | collective-permute-start | bytes 2359304 | tf_op jit(solution)/shard_map/ppermute | solution.py:324
  27.9 23.1 %copy-start.2 = (s32[64]{0:T(128)S(1)}, s32[64]{0:T(128)}, u32[]{:S(2)}) copy-start(s32[64]{0:T(128)} %order.3) | copy-start | bytes 772
  47.1 3.6 %collective-permute-start.5 = (bf16[256,1536]{1,0:T(8,128)(2,1)S(1)}, bf16[256,1536]{1,0:T(8,128)(2,1)S(1)}, u32[]{:S(2)}, u32[]{:S(2)}) collective-permute-start(bf16[256,1536]{1,0:T(8,128)(2,1)S(1)} %collective-permute-done.left_own.left_keys), channel_id=1, source_target_pairs={{0,1},{1,0},{2,3},{3,2},{4,5},{5,4},{6,7},{7,6},{8,9},{9,8},{10,11... | collective-permute-start | bytes 2359304 | tf_op jit(solution)/shard_map/ppermute | solution.py:318
  48.0 3.0 %collective-permute-start.6 = (bf16[256,1536]{1,0:T(8,128)(2,1)S(1)}, bf16[256,1536]{1,0:T(8,128)(2,1)S(1)}, u32[]{:S(2)}, u32[]{:S(2)}) collective-permute-start(bf16[256,1536]{1,0:T(8,128)(2,1)S(1)} %collective-permute-done.1.right_own.right_keys), channel_id=1, source_target_pairs={{0,1},{1,0},{2,3},{3,2},{4,5},{5,4},{6,7},{7,6},{8,9},{9,8},{10,11... | collective-permute-start | bytes 2359304 | tf_op jit(solution)/shard_map/ppermute | solution.py:318
  48.0 17.7 %collective-permute-start.3 = (bf16[512,768]{1,0:T(8,128)(2,1)S(1)}, bf16[512,768]{1,0:T(8,128)(2,1)S(1)}, u32[]{:S(2)}, u32[]{:S(2)}) collective-permute-start(bf16[512,768]{1,0:T(8,128)(2,1)S(1)} %get-tuple-element.21), channel_id=1, source_target_pairs={{0,2},{2,4},{4,6},{6,8},{8,10},{10,12},{12,14},{14,16},{16,18},{18... | collective-permute-start | bytes 2359304 | tf_op jit(solution)/shard_map/ppermute | solution.py:324
  49.3 20.2 %collective-permute-start.4 = (bf16[512,768]{1,0:T(8,128)(2,1)S(1)}, bf16[512,768]{1,0:T(8,128)(2,1)S(1)}, u32[]{:S(2)}, u32[]{:S(2)}) collective-permute-start(bf16[512,768]{1,0:T(8,128)(2,1)S(1)} %get-tuple-element.21), channel_id=1, source_target_pairs={{2,0},{4,2},{6,4},{8,6},{10,8},{12,10},{14,12},{16,14},{18,16},{20... | collective-permute-start | bytes 2359304 | tf_op jit(solution)/shard_map/ppermute | solution.py:324
  51.0 18.6 %copy-start = (bf16[768,1536]{1,0:T(8,128)(2,1)S(1)}, bf16[768,1536]{1,0:T(8,128)(2,1)}, u32[]{:S(2)}) copy-start(bf16[768,1536]{1,0:T(8,128)(2,1)} %weight.3) | copy-start | bytes 7077892
  52.2 25.9 %copy-start.4 = (bf16[256,1536]{1,0:T(8,128)(2,1)S(1)}, bf16[256,1536]{1,0:T(8,128)(2,1)}, u32[]{:S(2)}) copy-start(bf16[256,1536]{1,0:T(8,128)(2,1)} %x_in.1) | copy-start | bytes 2359300
  74.4 3.7 %collective-permute-start.7 = (bf16[256,1536]{1,0:T(8,128)(2,1)S(1)}, bf16[256,1536]{1,0:T(8,128)(2,1)S(1)}, u32[]{:S(2)}, u32[]{:S(2)}) collective-permute-start(bf16[256,1536]{1,0:T(8,128)(2,1)S(1)} %get-tuple-element.28), channel_id=1, source_target_pairs={{0,1},{1,0},{2,3},{3,2},{4,5},{5,4},{6,7},{7,6},{8,9},{9,8},{10,11... | collective-permute-start | bytes 2359304 | tf_op jit(solution)/shard_map/ppermute | solution.py:318

commit v3 on v2

--- a/solution.py
+++ b/solution.py
@@ -60,53 +60,85 @@
 
 
 def first_kernel(
-    sections, place, order_in, x_in, mod_in, stale, normed, to_right, to_left, values,
-    order, x, mod, held, sems,
+    sections, place, order_in, x_in, mod_in, stale, normed_out, to_right, to_left, values_out,
+    order, x, mod, held, values, normed, sems, out_sems,
 ):
+    rows, width = x.shape
+    part = rows // 2
+    half = width // 2
+    loads = [(mod_in, mod)] + [(x_in.at[r : r + part], x.at[r : r + part]) for r in (0, part)]
+    loads += [(order_in, order), (stale.at[0], held), (stale.at[1], values)]
     copies = [
         pltpu.make_async_copy(source, target, sems.at[i])
-        for i, (source, target) in enumerate(
-            (
-                (order_in, order),
-                (x_in, x),
-                (mod_in, mod),
-                (stale.at[0], held),
-                (stale.at[1], values),
-            )
-        )
+        for i, (source, target) in enumerate(loads)
     ]
     for copy in copies:
         copy.start()
-    rows, width = x.shape
-    for copy in copies[:3]:
-        copy.wait()
+    copies[0].wait()
     scale = 1.0 + mod[1:2, :]
     shift = mod[0:1, :]
-    step = 64
-    for r in range(0, rows, step):
-        v = x[r : r + step, :].astype(f32)
-        shifted = v - jnp.mean(v, axis=-1, keepdims=True)
-        spread = jnp.mean(shifted * shifted, axis=-1, keepdims=True)
-        normed[r : r + step, :] = (shifted * lax.rsqrt(spread + epsilon) * scale + shift).astype(
-            bf16
-        )
+
+    def norm(n):
+        copies[1 + n].wait()
+        step = 64
+        for r in range(n * part, (n + 1) * part, step):
+            v = x[r : r + step, :].astype(f32)
+            shifted = v - jnp.mean(v, axis=-1, keepdims=True)
+            spread = jnp.mean(shifted * shifted, axis=-1, keepdims=True)
+            y = shifted * lax.rsqrt(spread + epsilon) * scale + shift
+            normed[r : r + step, :] = y.astype(bf16)
+
+    norm(0)
     copies[3].wait()
     own, left, right = slots(place, order, sections)
-    half = width // 2
-
-    def fill(out, fresh):
+    targets = ((to_right, own < right), (to_left, own < left))
+    copies[4].wait()
+
+    def old_copies(n, out):
+        return [
+            pltpu.make_async_copy(
+                held.at[i * rows : (i + 1) * rows],
+                out.at[:, i * half : (i + 1) * half],
+                out_sems.at[2 * n + i],
+            )
+            for i in range(2)
+        ]
+
+    def new_copy(n, out):
+        return pltpu.make_async_copy(normed, out, out_sems.at[4 + n])
+
+    for n, (out, fresh) in enumerate(targets):
+
+        @pl.when(jnp.logical_not(fresh))
+        def _():
+            for copy in old_copies(n, out):
+                copy.start()
+
+    norm(1)
+    for n, (out, fresh) in enumerate(targets):
+
         @pl.when(fresh)
         def _():
-            out[...] = normed[...]
+            new_copy(n, out).start()
+
+    last = [pltpu.make_async_copy(normed, normed_out, out_sems.at[6])]
+    last[0].start()
+    copies[5].wait()
+    last.append(pltpu.make_async_copy(values, values_out, out_sems.at[7]))
+    last[1].start()
+    for n, (out, fresh) in enumerate(targets):
 
         @pl.when(jnp.logical_not(fresh))
         def _():
-            out[:, :half] = held[:rows, :]
-            out[:, half:] = held[rows:, :]
-
-    fill(to_right, own < right)
-    fill(to_left, own < left)
-    copies[4].wait()
+            for copy in old_copies(n, out):
+                copy.wait()
+
+        @pl.when(fresh)
+        def _():
+            new_copy(n, out).wait()
+
+    for copy in last:
+        copy.wait()
 
 
 def attend(queries, keys, vbuf):
@@ -114,33 +146,12 @@
     return jnp.dot(jnp.exp2(s).astype(bf16), vbuf, preferred_element_type=f32)
 
 
-def project_kernel(
-    place,
-    side,
-    count,
-    own_half,
-    other_half,
-    weight,
-    gains,
-    text,
-    keep,
-    cache,
-    queries,
-    total,
-    key_weight,
-    value_weight,
-    query_weight,
-    keys,
-    vbuf,
-    sems,
-):
-    rows = own_half.shape[0]
-    patch, width = queries.shape
-    text_rows = text.shape[1]
-    size = gains.shape[1]
-    block = 2 * size
-    buffers = {2: value_weight, 1: key_weight, 0: query_weight}
-    pieces = ((2, 0, block), (2, block, width), (1, 0, width), (0, 0, width))
+def own_rows_kernel(half, weight, gains, cache, keys, key_weight, value_weight, sems):
+    width = keys.shape[1]
+    block = 2 * gains.shape[1]
+    gain = gain_row(gains, 1)
+    buffers = {2: value_weight, 1: key_weight}
+    pieces = ((2, 0, block), (2, block, width), (1, 0, width))
     copies = []
     for n, (c, low, high) in enumerate(pieces):
         copy = pltpu.make_async_copy(
@@ -148,45 +159,79 @@
         )
         copy.start()
         copies.append(copy)
-    own_mask = mask_columns((keep[pl.ds(place[0], 1), :] > 0).astype(f32), size)
-    live = lax.broadcasted_iota(jnp.int32, (text_rows, size), 0) < count[0]
-    text_mask = live.astype(f32).astype(bf16)
-    heads = width // size
-    text_gain = gain_row(gains, 2)
-    for i in range(heads):
-        cols = slice(i * size, (i + 1) * size)
-        keys[patch:, cols] = head_normed(text[0, :, cols].astype(f32), text_gain)
-        vbuf[i, :patch, size:] = own_mask
-        vbuf[i, patch:, size:] = text_mask
-        vbuf[i, patch:, :size] = text[1, :, cols] * text_mask
-    h = side[0]
-    places = (
-        (own_half, pl.multiple_of(h * rows, rows)),
-        (other_half, pl.multiple_of((1 - h) * rows, rows)),
-    )
-    factor = math.log2(math.e) * size**-0.5
-    query_gain = gain_row(gains, 0) * factor
-    key_gain = gain_row(gains, 1)
     for n, (c, low, high) in enumerate(pieces):
         copies[n].wait()
         for j in range(low, high, block):
             cols = slice(j, j + block)
-            for half, at in places:
-                y = jnp.dot(half[...], buffers[c][:, cols], preferred_element_type=f32)
-                at = pl.ds(at, rows)
-                if c == 0:
-                    queries[at, cols] = heads_normed(y, query_gain)
-                else:
-                    rounded = y.astype(bf16)
-                    cache[c - 1, at, cols] = rounded
-                    if c == 1:
-                        keys[at, cols] = heads_normed(rounded.astype(f32), key_gain)
+            y = jnp.dot(half[...], buffers[c][:, cols], preferred_element_type=f32)
+            y = y.astype(bf16)
+            cache[c - 1, :, cols] = y
+            if c == 1:
+                keys[:, cols] = heads_normed(y.astype(f32), gain)
+
+
+def other_rows_kernel(
+    place, side, own_half, half, own_cache, own_keys, key_weight, value_weight, weight, gains,
+    keep, cache, queries, keys, vbuf, query_weight, sem,
+):
+    load = pltpu.make_async_copy(weight.at[0], query_weight, sem)
+    load.start()
+    rows = half.shape[0]
+    width = keys.shape[1]
+    size = gains.shape[1]
+    block = 2 * size
+    h = side[0]
+    at = pl.ds(pl.multiple_of((1 - h) * rows, rows), rows)
+    own_at = pl.ds(pl.multiple_of(h * rows, rows), rows)
+    mask = mask_columns((keep[pl.ds(place[0], 1), :] > 0).astype(f32), size)
+    for i in range(width // size):
+        vbuf[i, :, size:] = mask
+    cache[:, own_at, :] = own_cache[...]
+    keys[own_at, :] = own_keys[...]
+    gain = gain_row(gains, 1)
+    for j in range(0, width, block):
+        cols = slice(j, j + block)
+        y = jnp.dot(half[...], value_weight[:, cols], preferred_element_type=f32).astype(bf16)
+        cache[1, at, cols] = y
+        for low in range(0, block, size):
+            i = (j + low) // size
+            vbuf[i, at, :size] = y[:, low : low + size] * vbuf[0, at, size:]
+            vbuf[i, own_at, :size] = (
+                own_cache[1, :, i * size : (i + 1) * size] * vbuf[0, own_at, size:]
+            )
+    for j in range(0, width, block):
+        cols = slice(j, j + block)
+        y = jnp.dot(half[...], key_weight[:, cols], preferred_element_type=f32).astype(bf16)
+        cache[0, at, cols] = y
+        keys[at, cols] = heads_normed(y.astype(f32), gain)
+    gain = gain_row(gains, 0) * (math.log2(math.e) * size**-0.5)
+    load.wait()
+    for j in range(0, width, block):
+        cols = slice(j, j + block)
+        for source, rows_at in ((own_half, own_at), (half, at)):
+            y = jnp.dot(source[...], query_weight[:, cols], preferred_element_type=f32)
+            queries[rows_at, cols] = heads_normed(y, gain)
+
+
+def own_kernel(count, queries, keys, vbuf, text_in, gains, total, text, text_keys, tbuf, sem):
+    load = pltpu.make_async_copy(text_in, text, sem)
+    load.start()
+    heads, _, wide = vbuf.shape
+    size = wide // 2
+    text_rows = text.shape[1]
     for i in range(heads):
         cols = slice(i * size, (i + 1) * size)
-        vbuf[i, :patch, :size] = cache[1, :, cols] * own_mask
-        total[:, 2 * i * size : 2 * (i + 1) * size] = attend(
-            queries[:, cols], keys[:, cols], vbuf[i]
-        )
+        total[:, wide * i : wide * (i + 1)] = attend(queries[:, cols], keys[:, cols], vbuf[i])
+    live = lax.broadcasted_iota(jnp.int32, (text_rows, size), 0) < count[0]
+    mask = live.astype(f32).astype(bf16)
+    gain = gain_row(gains, 2)
+    load.wait()
+    for i in range(heads):
+        cols = slice(i * size, (i + 1) * size)
+        text_keys[:, cols] = head_normed(text[0, :, cols].astype(f32), gain)
+        tbuf[i, :, :size] = text[1, :, cols] * mask
+        tbuf[i, :, size:] = mask
+        total[:, wide * i : wide * (i + 1)] += attend(queries[:, cols], text_keys[:, cols], tbuf[i])
 
 
 def side_mask(keep, place, sections, by, size):
@@ -272,7 +317,7 @@
     total_in,
     weight,
     sent,
-    kept,
+    mine,
     keys,
     vbuf,
     total,
@@ -309,9 +354,13 @@
         att[:, i * size : (i + 1) * size] = (
             total[:, low : low + size] / total[:, low + size : low + 2 * size]
         ).astype(bf16)
-    for out, at in ((sent, 1 - h), (kept, h)):
-        at = pl.ds(pl.multiple_of(at * rows, rows), rows)
-        out[...] = jnp.dot(att[at, :], weight[...], preferred_element_type=f32).astype(bf16)
+    at = pl.ds(pl.multiple_of((1 - h) * rows, rows), rows)
+    sent[...] = jnp.dot(att[at, :], weight[...], preferred_element_type=f32).astype(bf16)
+    mine[...] = att[pl.ds(pl.multiple_of(h * rows, rows), rows), :]
+
+
+def kept_kernel(mine, weight, kept):
+    kept[...] = jnp.dot(mine[...], weight[...], preferred_element_type=f32).astype(bf16)
 
 
 def swapped(array):
@@ -348,31 +397,29 @@
     keep = video_keep.reshape(sections, patch)
     half_shape = jax.ShapeDtypeStruct((rows, model), bf16)
     side_shape = jax.ShapeDtypeStruct((patch, width), bf16)
-    weight_shape = jax.ShapeDtypeStruct((model, width), bf16)
+    part_shape = jax.ShapeDtypeStruct((rows, width), bf16)
     total_shape = jax.ShapeDtypeStruct((patch, 2 * width), f32)
+    stale_cache = in_hbm(stale_cache)
 
     normed, to_right, to_left, values = pl.pallas_call(
         functools.partial(first_kernel, sections),
         out_shape=(half_shape, half_shape, half_shape, side_shape),
         in_specs=[SMEM, HBM, HBM, HBM, HBM],
-        out_specs=(VMEM,) * 4,
+        out_specs=(HBM,) * 4,
         scratch_shapes=[
             pltpu.SMEM(patch_order.shape, jnp.int32),
             pltpu.VMEM((rows, model), bf16),
             pltpu.VMEM(modulation.shape, f32),
             pltpu.VMEM((patch, width), bf16),
-            pltpu.SemaphoreType.DMA((5,)),
+            pltpu.VMEM((patch, width), bf16),
+            pltpu.VMEM((rows, model), bf16),
+            pltpu.SemaphoreType.DMA((6,)),
+            pltpu.SemaphoreType.DMA((8,)),
         ],
         compiler_params=params(10),
         cost_estimate=cost(10 * rows * model, 10 * rows * model),
         name="first",
-    )(
-        place,
-        in_hbm(patch_order),
-        in_hbm(video_tokens),
-        in_hbm(modulation),
-        in_hbm(stale_cache),
-    )
+    )(place, in_hbm(patch_order), in_hbm(video_tokens), in_hbm(modulation), stale_cache)
 
     left_own = from_behind(to_right, "section", 1)
     right_own = from_behind(to_left, "section", -1)
@@ -380,41 +427,71 @@
     right_values = from_behind(values, "section", -1)
     other = swapped(normed)
 
-    fresh_cache, queries, total, key_weight, value_weight = pl.pallas_call(
-        project_kernel,
+    weight_shape = jax.ShapeDtypeStruct((model, width), bf16)
+    project_weight = in_hbm(project_weight)
+    own_cache, own_keys, key_weight, value_weight = pl.pallas_call(
+        own_rows_kernel,
+        out_shape=(
+            jax.ShapeDtypeStruct((2, rows, width), bf16),
+            part_shape,
+            weight_shape,
+            weight_shape,
+        ),
+        in_specs=[VMEM, HBM, VMEM],
+        out_specs=(VMEM,) * 4,
+        scratch_shapes=[pltpu.SemaphoreType.DMA((3,))],
+        compiler_params=params(10),
+        cost_estimate=cost(4 * rows * model * width, 4 * rows * width),
+        name="own_rows",
+    )(normed, project_weight, norm_gains)
+
+    fresh_cache, queries, keys, vbuf = pl.pallas_call(
+        other_rows_kernel,
         out_shape=(
             jax.ShapeDtypeStruct((2, patch, width), bf16),
             side_shape,
-            total_shape,
-            weight_shape,
-            weight_shape,
+            side_shape,
+            jax.ShapeDtypeStruct((heads, patch, 2 * size), bf16),
         ),
-        in_specs=[SMEM, SMEM, SMEM, VMEM, VMEM, HBM, VMEM, VMEM, VMEM],
-        out_specs=(VMEM,) * 5,
-        scratch_shapes=[
-            pltpu.VMEM((model, width), bf16),
-            pltpu.VMEM((patch + text_rows, width), bf16),
-            pltpu.VMEM((heads, patch + text_rows, 2 * size), bf16),
-            pltpu.SemaphoreType.DMA((4,)),
-        ],
-        compiler_params=params(28),
-        cost_estimate=cost(2 * patch * model * 3 * width, 6 * model * width),
-        name="project",
+        in_specs=[SMEM, SMEM] + [VMEM] * 6 + [HBM, VMEM, VMEM],
+        out_specs=(VMEM,) * 4,
+        scratch_shapes=[pltpu.VMEM((model, width), bf16), pltpu.SemaphoreType.DMA],
+        compiler_params=params(16),
+        cost_estimate=cost(8 * rows * model * width, 4 * rows * width),
+        name="other_rows",
     )(
         place,
         side,
-        text_count,
         normed,
         other,
-        in_hbm(project_weight),
+        own_cache,
+        own_keys,
+        key_weight,
+        value_weight,
+        project_weight,
         norm_gains,
-        text_cache,
         keep,
     )
 
     left_own, right_own, queries = lax.optimization_barrier((left_own, right_own, queries))
     left_other = swapped(left_own)
     right_other = swapped(right_own)
+
+    total = pl.pallas_call(
+        own_kernel,
+        out_shape=total_shape,
+        in_specs=[SMEM, VMEM, VMEM, VMEM, HBM, VMEM],
+        out_specs=VMEM,
+        scratch_shapes=[
+            pltpu.VMEM((2, text_rows, width), bf16),
+            pltpu.VMEM((text_rows, width), bf16),
+            pltpu.VMEM((heads, text_rows, 2 * size), bf16),
+            pltpu.SemaphoreType.DMA,
+        ],
+        compiler_params=params(12),
+        cost_estimate=cost(6 * patch * (patch + text_rows) * width, 6 * patch * width),
+        name="own",
+    )(text_count, queries, keys, vbuf, in_hbm(text_cache), norm_gains)
 
     total = pl.pallas_call(
         functools.partial(fresh_kernel, sections),
@@ -445,9 +522,9 @@
         total,
     )
 
-    sent, kept = pl.pallas_call(
+    sent, mine = pl.pallas_call(
         functools.partial(stale_kernel, sections),
-        out_shape=(half_shape, half_shape),
+        out_shape=(half_shape, part_shape),
         in_specs=[SMEM] * 3 + [VMEM] * 9,
         out_specs=(VMEM, VMEM),
         scratch_shapes=[
@@ -474,6 +551,15 @@
         output_weight,
     )
     received = swapped(sent)
+    kept = pl.pallas_call(
+        kept_kernel,
+        out_shape=half_shape,
+        in_specs=[VMEM, VMEM],
+        out_specs=VMEM,
+        compiler_params=params(8),
+        cost_estimate=cost(2 * rows * width * model, 4 * rows * model),
+        name="kept",
+    )(mine, output_weight)
     mixed = kept.astype(f32) + received.astype(f32)
     updated = (video_tokens.astype(f32) + modulation[2] * mixed).astype(bf16)
     return (updated, fresh_cache)

time: 79.6 us -> 79.2 us (level)
  waiting for transfers between devices: 28 us -> 25.3 us
  Pallas kernels: 19.3 us -> 20.8 us
  local copies, waits for them, and re-layouts: 0.81 us -> 1.73 us
    pallas_call x1 -> x4, Pallas kernels: 10.1 us -> 12.8 us  [the longest x1 5.35 us: on_device(): pl.pallas_call(other_rows_kernel, out_shape=(jax.ShapeDtypeStruct((2, pat...]
    ppermute x4, waiting for transfers between devices: 26.5 us -> 24.9 us  [from_behind(): return lax.ppermute(array, axis, pairs)]
    ppermute x4, waiting for transfers between devices: 1.51 us -> 0.36 us  [swapped(): return lax.ppermute(array, 'head', [(0, 1), (1, 0)])]
    unnamed x12 -> x14, local copies, waits for them, and re-layouts: 0.03 us -> 0.94 us
  transfers between devices with their start and end apart: 8 -> 8, of which waited for: 6 -> 5; matrix products, arithmetic and copies ran while one was open for 1% -> 1% of each run, Pallas kernels for 14% -> 18%
where the time goes in v3:
time: 79.2 us; the launch traced here: 78.9 us
  starting transfers between devices  28.3 us (36%)
  waiting for transfers between devices  25.3 us (32%)
  Pallas kernels  20.8 us (26%)
  local copies, waits for them, and re-layouts  1.73 us (2%)
  between operations  1.49 us (2%)
  other arithmetic  1.21 us (2%)
    ppermute x4, waiting for transfers between devices, from_behind(): return lax.ppermute(array, axis, pairs)  24.9 us
    ppermute x4, starting transfers between devices, swapped(): return lax.ppermute(array, 'head', [(0, 1), (1, 0)])  23 us
    pallas_call x1, Pallas kernels, on_device(): pl.pallas_call(other_rows_kernel, out_shape=(jax.ShapeDtypeStruct((2, pat...  5.35 us
    ppermute x4, starting transfers between devices, from_behind(): return lax.ppermute(array, axis, pairs)  5.3 us
    pallas_call x1, Pallas kernels, on_device(): pl.pallas_call(functools.partial(stale_kernel, sections), out_shape=(half...  4.16 us
    pallas_call x1, Pallas kernels, on_device(): pl.pallas_call(own_rows_kernel, out_shape=(jax.ShapeDtypeStruct((2, rows,...  3.5 us
    pallas_call x1, Pallas kernels, on_device(): pl.pallas_call(own_kernel, out_shape=total_shape, in_specs=[SMEM, VMEM, V...  3.13 us
    pallas_call x1, Pallas kernels, on_device(): pl.pallas_call(functools.partial(first_kernel, sections), out_shape=(half...  2.76 us
  transfers between devices with their start and end apart: 8, of which 5 were waited for; matrix products, arithmetic and copies ran while one was open for 1% of the time, Pallas kernels for 18%

profile of v3, /device:TPU:513, one launch (start us, length us, event | category | flops | bytes accessed | tf_op | source)
XLA Modules:
  0.0 78.9 jit_solution(17658202442309330486)
XLA Ops:
  0.6 0.0 copy-start.6
  0.6 0.0 copy-start.1
  0.7 2.8 %first.1 = (bf16[256,1536]{1,0:T(8,128)(2,1)S(1)}, bf16[256,1536]{1,0:T(8,128)(2,1)}, bf16[256,1536]{1,0:T(8,128)(2,1)}, bf16[512,768]{1,0:T(8,128)(2,1)S(1)}) custom-call(s32[1]{0:T(128)} %bitcast.place, s32[64]{0:T(128)} %order.3, bf16[256,1536]{1,0:T(8,128)(2,1)} %x_in.1, f32[3,1536]{1,0:T(4,128)} %mod_in.1, bf16[2,512,768]{2,1,0:T(8,128)(2,1)} %stale.2), custom_call_target="tpu_custom_call" | custom-call | flops 3932160 | bytes 3932160 | tf_op jit(solution)/shard_map/first/pallas_call | solution.py:404
  3.4 0.0 copy-start.3
  3.4 0.9 %copy-done.3 = bf16[512,768]{1,0:T(8,128)(2,1)} copy-done((bf16[512,768]{1,0:T(8,128)(2,1)}, bf16[512,768]{1,0:T(8,128)(2,1)S(1)}, u32[]{:S(2)}) %copy-start.3) | copy-done | bytes 786456
  4.3 20.4 %collective-permute-start.2 = (bf16[256,1536]{1,0:T(8,128)(2,1)S(1)}, bf16[256,1536]{1,0:T(8,128)(2,1)S(1)}, u32[]{:S(2)}, u32[]{:S(2)}) collective-permute-start(bf16[256,1536]{1,0:T(8,128)(2,1)S(1)} %get-tuple-element.21.half.own_half), channel_id=1, source_target_pairs={{0,1},{1,0},{2,3},{3,2},{4,5},{5,4},{6,7},{7,6},{8,9},{9,8},{10,11... | collective-permute-start | bytes 2359304 | tf_op jit(solution)/shard_map/ppermute | solution.py:367
  24.8 1.3 %collective-permute-start = (bf16[256,1536]{1,0:T(8,128)(2,1)}, bf16[256,1536]{1,0:T(8,128)(2,1)S(1)}, u32[]{:S(2)}, u32[]{:S(2)}) collective-permute-start(bf16[256,1536]{1,0:T(8,128)(2,1)} %get-tuple-element.19), channel_id=1, source_target_pairs={{0,2},{2,4},{4,6},{6,8},{8,10},{10,12},{12,14},{14,16},{16,18},{18... | collective-permute-start | bytes 2359304 | tf_op jit(solution)/shard_map/ppermute | solution.py:373
  26.1 1.3 %collective-permute-start.1 = (bf16[256,1536]{1,0:T(8,128)(2,1)}, bf16[256,1536]{1,0:T(8,128)(2,1)S(1)}, u32[]{:S(2)}, u32[]{:S(2)}) collective-permute-start(bf16[256,1536]{1,0:T(8,128)(2,1)} %get-tuple-element.20), channel_id=1, source_target_pairs={{2,0},{4,2},{6,4},{8,6},{10,8},{12,10},{14,12},{16,14},{18,16},{20... | collective-permute-start | bytes 2359304 | tf_op jit(solution)/shard_map/ppermute | solution.py:373
  27.5 3.5 %own_rows.1 = (bf16[2,256,768]{2,1,0:T(8,128)(2,1)S(1)}, bf16[256,768]{1,0:T(8,128)(2,1)S(1)}, bf16[1536,768]{1,0:T(8,128)(2,1)S(1)}, bf16[1536,768]{1,0:T(8,128)(2,1)S(1)}) custom-call(bf16[256,1536]{1,0:T(8,128)(2,1)S(1)} %get-tuple-element.21.half.own_half, bf16[3,1536,768]{2,1,0:T(8,128)(2,1)} %weight.5, f32[3,128]{1,0:T(4,128)S(1)} %copy-done.1), custom_call_target="tpu_custom_call" | custom-call | flops 1207959552 | bytes 786432 | tf_op jit(solution)/shard_map/own_rows/pallas_call | solution.py:432
  31.0 0.0 collective-permute-done.2.half
  31.0 5.3 %other_rows.1 = (bf16[2,512,768]{2,1,0:T(8,128)(2,1)}, bf16[512,768]{1,0:T(8,128)(2,1)S(1)}, bf16[512,768]{1,0:T(8,128)(2,1)S(1)}, bf16[6,512,256]{2,1,0:T(8,128)(2,1)S(1)}) custom-call(s32[1]{0:T(128)} %bitcast.place, s32[1]{0:T(128)} %bitcast.1.side, bf16[256,1536]{1,0:T(8,128)(2,1)S(1)} %get-tuple-element.21.half.own_half, ...), custom_call_target="tpu_custom_call" | custom-call | flops 2415919104 | bytes 786432 | tf_op jit(solution)/shard_map/other_rows/pallas_call | solution.py:448
  36.4 7.2 %collective-permute-done.left_own.left_keys = bf16[256,1536]{1,0:T(8,128)(2,1)S(1)} collective-permute-done((bf16[256,1536]{1,0:T(8,128)(2,1)}, bf16[256,1536]{1,0:T(8,128)(2,1)S(1)}, u32[]{:S(2)}, u32[]{:S(2)}) %collective-permute-start) | collective-permute-done | bytes 786464 | tf_op jit(solution)/shard_map/ppermute | solution.py:373
  43.5 3.8 %collective-permute-done.1.right_own.right_keys = bf16[256,1536]{1,0:T(8,128)(2,1)S(1)} collective-permute-done((bf16[256,1536]{1,0:T(8,128)(2,1)}, bf16[256,1536]{1,0:T(8,128)(2,1)S(1)}, u32[]{:S(2)}, u32[]{:S(2)}) %collective-permute-start.1) | collective-permute-done | bytes 786464 | tf_op jit(solution)/shard_map/ppermute | solution.py:373
  47.3 0.9 %collective-permute-start.5 = (bf16[256,1536]{1,0:T(8,128)(2,1)S(1)}, bf16[256,1536]{1,0:T(8,128)(2,1)S(1)}, u32[]{:S(2)}, u32[]{:S(2)}) collective-permute-start(bf16[256,1536]{1,0:T(8,128)(2,1)S(1)} %collective-permute-done.left_own.left_keys), channel_id=1, source_target_pairs={{0,1},{1,0},{2,3},{3,2},{4,5},{5,4},{6,7},{7,6},{8,9},{9,8},{10,11... | collective-permute-start | bytes 2359304 | tf_op jit(solution)/shard_map/ppermute | solution.py:367
  48.2 0.0 collective-permute-start.6
  48.2 1.3 %collective-permute-start.3 = (bf16[512,768]{1,0:T(8,128)(2,1)S(1)}, bf16[512,768]{1,0:T(8,128)(2,1)S(1)}, u32[]{:S(2)}, u32[]{:S(2)}) collective-permute-start(bf16[512,768]{1,0:T(8,128)(2,1)S(1)} %copy-done.4), channel_id=1, source_target_pairs={{0,2},{2,4},{4,6},{6,8},{8,10},{10,12},{12,14},{14,16},{16,18},{18... | collective-permute-start | bytes 2359304 | tf_op jit(solution)/shard_map/ppermute | solution.py:373
  49.6 1.3 %collective-permute-start.4 = (bf16[512,768]{1,0:T(8,128)(2,1)S(1)}, bf16[512,768]{1,0:T(8,128)(2,1)S(1)}, u32[]{:S(2)}, u32[]{:S(2)}) collective-permute-start(bf16[512,768]{1,0:T(8,128)(2,1)S(1)} %copy-done.4), channel_id=1, source_target_pairs={{2,0},{4,2},{6,4},{8,6},{10,8},{12,10},{14,12},{16,14},{18,16},{20... | collective-permute-start | bytes 2359304 | tf_op jit(solution)/shard_map/ppermute | solution.py:373
  51.5 0.0 copy-start.2
  51.5 3.1 %own.1.total_in = f32[512,1536]{1,0:T(8,128)S(1)} custom-call(s32[1]{0:T(128)S(6)} %copy.14.count, bf16[512,768]{1,0:T(8,128)(2,1)S(1)} %get-tuple-element.30.queries, bf16[512,768]{1,0:T(8,128)(2,1)S(1)} %get-tuple-element.31.keys, bf16[6,512,256]{2,1,0:T(8,128)(2,1)S(1)} %get-tuple-element.32.vbuf, bf16[2,256,768]{2,1,0:T(8,128)(2,1)} %text_in.1, ...), custom_call_target="tpu_custom_call" | custom-call | flops 1811939328 | bytes 2359296 | tf_op jit(solution)/shard_map/own/pallas_call | solution.py:480
  54.7 0.0 collective-permute-done.5.left_other
  54.7 0.0 collective-permute-done.6.right_other
  54.7 0.0 copy-start
  54.7 1.1 %fresh.1.total_in = f32[512,1536]{1,0:T(8,128)S(1)} custom-call(s32[1]{0:T(128)} %bitcast.place, s32[1]{0:T(128)} %bitcast.1.side, s32[64]{0:T(128)S(1)} %copy-done.2, bf16[256,1536]{1,0:T(8,128)(2,1)S(1)} %collective-permute-done.left_own.left_keys, bf16[256,1536]{1,0:T(8,128)(2,1)S(1)} %collective-permute-done.5.left_other, ...), custom_call_target="tpu_custom_call", output_to_operand_aliasing={{}: (12, {})} | custom-call | flops 2415919104 | bytes 2359296 | tf_op jit(solution)/shard_map/fresh/pallas_call | solution.py:496
  55.9 10.0 %collective-permute-done.3.left_values = bf16[512,768]{1,0:T(8,128)(2,1)S(1)} collective-permute-done((bf16[512,768]{1,0:T(8,128)(2,1)S(1)}, bf16[512,768]{1,0:T(8,128)(2,1)S(1)}, u32[]{:S(2)}, u32[]{:S(2)}) %collective-permute-start.3) | collective-permute-done | bytes 786464 | tf_op jit(solution)/shard_map/ppermute | solution.py:373
  65.9 3.9 %collective-permute-done.4.right_values = bf16[512,768]{1,0:T(8,128)(2,1)S(1)} collective-permute-done((bf16[512,768]{1,0:T(8,128)(2,1)S(1)}, bf16[512,768]{1,0:T(8,128)(2,1)S(1)}, u32[]{:S(2)}, u32[]{:S(2)}) %collective-permute-start.4) | collective-permute-done | bytes 786464 | tf_op jit(solution)/shard_map/ppermute | solution.py:373
  69.8 4.2 %stale.3 = (bf16[256,1536]{1,0:T(8,128)(2,1)S(1)}, bf16[256,768]{1,0:T(8,128)(2,1)S(1)}) custom-call(s32[1]{0:T(128)} %bitcast.place, s32[1]{0:T(128)} %bitcast.1.side, s32[64]{0:T(128)S(1)} %copy-done.2, bf16[256,1536]{1,0:T(8,128)(2,1)S(1)} %collective-permute-done.left_own.left_keys, bf16[512,768]{1,0:T(8,128)(2,1)S(1)} %collective-permute-done.3.left_values, ...), custom_call_target="tpu_custom_call" | custom-call | flops 1207959552 | bytes 2359296 | tf_op jit(solution)/shard_map/stale/pallas_call | solution.py:525
  74.0 1.8 %collective-permute-start.7 = (bf16[256,1536]{1,0:T(8,128)(2,1)S(1)}, bf16[256,1536]{1,0:T(8,128)(2,1)S(1)}, u32[]{:S(2)}, u32[]{:S(2)}) collective-permute-start(bf16[256,1536]{1,0:T(8,128)(2,1)S(1)} %get-tuple-element.34), channel_id=1, source_target_pairs={{0,1},{1,0},{2,3},{3,2},{4,5},{5,4},{6,7},{7,6},{8,9},{9,8},{10,11... | collective-permute-start | bytes 2359304 | tf_op jit(solution)/shard_map/ppermute | solution.py:367
  75.7 0.8 slice_reduce_fusion
  76.5 0.0 copy-start.5
  76.5 0.8 kept.1
  77.3 0.4 collective-permute-done.7
  77.6 1.2 %add_convert_fusion = bf16[256,1536]{1,0:T(8,128)(2,1)} fusion(bf16[256,1536]{1,0:T(8,128)(2,1)S(1)} %collective-permute-done.7, bf16[256,1536]{1,0:T(8,128)(2,1)S(1)} %kept.1, bf16[256,1536]{1,0:T(8,128)(2,1)S(1)} %copy-done.5, f32[1536]{0:T(1024)S(1)} %slice_reduce_fusion), kind=kLoop, calls=%fused_computation | loop fusion | flops 2752512 | bytes 3151872 | tf_op jit(solution)/shard_map/convert_element_type | solution.py:564
  (8 shorter events, 0.0 us)
Async XLA Ops:
  0.6 26.8 %copy-start.6 = (s32[32768]{0:T(1024)S(1)}, s32[32768]{0:T(1024)}, u32[]{:S(2)}) copy-start(s32[32768]{0:T(1024)} %param.17) | copy-start | bytes 393220
  0.6 26.8 %copy-start.1 = (f32[3,128]{1,0:T(4,128)S(1)}, f32[3,128]{1,0:T(4,128)}, u32[]{:S(2)}) copy-start(f32[3,128]{1,0:T(4,128)} %gains.9) | copy-start | bytes 4612
  3.4 0.9 %copy-start.3 = (bf16[512,768]{1,0:T(8,128)(2,1)}, bf16[512,768]{1,0:T(8,128)(2,1)S(1)}, u32[]{:S(2)}) copy-start(bf16[512,768]{1,0:T(8,128)(2,1)S(1)} %get-tuple-element.28) | copy-start | bytes 2359300
  4.3 26.6 %collective-permute-start.2 = (bf16[256,1536]{1,0:T(8,128)(2,1)S(1)}, bf16[256,1536]{1,0:T(8,128)(2,1)S(1)}, u32[]{:S(2)}, u32[]{:S(2)}) collective-permute-start(bf16[256,1536]{1,0:T(8,128)(2,1)S(1)} %get-tuple-element.21.half.own_half), channel_id=1, source_target_pairs={{0,1},{1,0},{2,3},{3,2},{4,5},{5,4},{6,7},{7,6},{8,9},{9,8},{10,11... | collective-permute-start | bytes 2359304 | tf_op jit(solution)/shard_map/ppermute | solution.py:367
  24.8 18.8 %collective-permute-start = (bf16[256,1536]{1,0:T(8,128)(2,1)}, bf16[256,1536]{1,0:T(8,128)(2,1)S(1)}, u32[]{:S(2)}, u32[]{:S(2)}) collective-permute-start(bf16[256,1536]{1,0:T(8,128)(2,1)} %get-tuple-element.19), channel_id=1, source_target_pairs={{0,2},{2,4},{4,6},{6,8},{8,10},{10,12},{12,14},{14,16},{16,18},{18... | collective-permute-start | bytes 2359304 | tf_op jit(solution)/shard_map/ppermute | solution.py:373
  26.1 21.2 %collective-permute-start.1 = (bf16[256,1536]{1,0:T(8,128)(2,1)}, bf16[256,1536]{1,0:T(8,128)(2,1)S(1)}, u32[]{:S(2)}, u32[]{:S(2)}) collective-permute-start(bf16[256,1536]{1,0:T(8,128)(2,1)} %get-tuple-element.20), channel_id=1, source_target_pairs={{2,0},{4,2},{6,4},{8,6},{10,8},{12,10},{14,12},{16,14},{18,16},{20... | collective-permute-start | bytes 2359304 | tf_op jit(solution)/shard_map/ppermute | solution.py:373
  31.0 17.2 %copy-start.4 = (bf16[512,768]{1,0:T(8,128)(2,1)S(1)}, bf16[512,768]{1,0:T(8,128)(2,1)}, u32[]{:S(2)}) copy-start(bf16[512,768]{1,0:T(8,128)(2,1)} %copy-done.3) | copy-start | bytes 2359300
  47.3 7.3 %collective-permute-start.5 = (bf16[256,1536]{1,0:T(8,128)(2,1)S(1)}, bf16[256,1536]{1,0:T(8,128)(2,1)S(1)}, u32[]{:S(2)}, u32[]{:S(2)}) collective-permute-start(bf16[256,1536]{1,0:T(8,128)(2,1)S(1)} %collective-permute-done.left_own.left_keys), channel_id=1, source_target_pairs={{0,1},{1,0},{2,3},{3,2},{4,5},{5,4},{6,7},{7,6},{8,9},{9,8},{10,11... | collective-permute-start | bytes 2359304 | tf_op jit(solution)/shard_map/ppermute | solution.py:367
  48.2 6.5 %collective-permute-start.6 = (bf16[256,1536]{1,0:T(8,128)(2,1)S(1)}, bf16[256,1536]{1,0:T(8,128)(2,1)S(1)}, u32[]{:S(2)}, u32[]{:S(2)}) collective-permute-start(bf16[256,1536]{1,0:T(8,128)(2,1)S(1)} %collective-permute-done.1.right_own.right_keys), channel_id=1, source_target_pairs={{0,1},{1,0},{2,3},{3,2},{4,5},{5,4},{6,7},{7,6},{8,9},{9,8},{10,11... | collective-permute-start | bytes 2359304 | tf_op jit(solution)/shard_map/ppermute | solution.py:367
  48.2 17.7 %collective-permute-start.3 = (bf16[512,768]{1,0:T(8,128)(2,1)S(1)}, bf16[512,768]{1,0:T(8,128)(2,1)S(1)}, u32[]{:S(2)}, u32[]{:S(2)}) collective-permute-start(bf16[512,768]{1,0:T(8,128)(2,1)S(1)} %copy-done.4), channel_id=1, source_target_pairs={{0,2},{2,4},{4,6},{6,8},{8,10},{10,12},{12,14},{14,16},{16,18},{18... | collective-permute-start | bytes 2359304 | tf_op jit(solution)/shard_map/ppermute | solution.py:373
  49.6 20.2 %collective-permute-start.4 = (bf16[512,768]{1,0:T(8,128)(2,1)S(1)}, bf16[512,768]{1,0:T(8,128)(2,1)S(1)}, u32[]{:S(2)}, u32[]{:S(2)}) collective-permute-start(bf16[512,768]{1,0:T(8,128)(2,1)S(1)} %copy-done.4), channel_id=1, source_target_pairs={{2,0},{4,2},{6,4},{8,6},{10,8},{12,10},{14,12},{16,14},{18,16},{20... | collective-permute-start | bytes 2359304 | tf_op jit(solution)/shard_map/ppermute | solution.py:373
  51.5 3.2 %copy-start.2 = (s32[64]{0:T(128)S(1)}, s32[64]{0:T(128)}, u32[]{:S(2)}) copy-start(s32[64]{0:T(128)} %order.3) | copy-start | bytes 772
  54.7 15.1 %copy-start = (bf16[768,1536]{1,0:T(8,128)(2,1)S(1)}, bf16[768,1536]{1,0:T(8,128)(2,1)}, u32[]{:S(2)}) copy-start(bf16[768,1536]{1,0:T(8,128)(2,1)} %weight.7) | copy-start | bytes 7077892
  74.0 3.7 %collective-permute-start.7 = (bf16[256,1536]{1,0:T(8,128)(2,1)S(1)}, bf16[256,1536]{1,0:T(8,128)(2,1)S(1)}, u32[]{:S(2)}, u32[]{:S(2)}) collective-permute-start(bf16[256,1536]{1,0:T(8,128)(2,1)S(1)} %get-tuple-element.34), channel_id=1, source_target_pairs={{0,1},{1,0},{2,3},{3,2},{4,5},{5,4},{6,7},{7,6},{8,9},{9,8},{10,11... | collective-permute-start | bytes 2359304 | tf_op jit(solution)/shard_map/ppermute | solution.py:367
  76.5 1.2 %copy-start.5 = (bf16[256,1536]{1,0:T(8,128)(2,1)S(1)}, bf16[256,1536]{1,0:T(8,128)(2,1)}, u32[]{:S(2)}) copy-start(bf16[256,1536]{1,0:T(8,128)(2,1)} %x_in.1) | copy-start | bytes 2359300

commit v4 on v3

--- a/solution.py
+++ b/solution.py
@@ -31,11 +31,10 @@
     return pl.CostEstimate(flops=flops, bytes_accessed=nbytes, transcendentals=0)
 
 
-def slots(place, order, sections):
+def partners(place, sections):
     p = place[0]
-    left = jnp.maximum(p - 1, 0)
-    right = jnp.minimum(p + 1, sections - 1)
-    return order[p], order[left], order[right]
+    by = 2 * lax.rem(p, 2) - 1
+    return tuple(jnp.clip(q, 0, sections - 1) for q in (p + by, p - by))
 
 
 def gain_row(gains, which):
@@ -60,7 +59,7 @@
 
 
 def first_kernel(
-    sections, place, order_in, x_in, mod_in, stale, normed_out, to_right, to_left, values_out,
+    sections, place, order_in, x_in, mod_in, stale, normed_out, to_odd, to_even, values_out,
     order, x, mod, held, values, normed, sems, out_sems,
 ):
     rows, width = x.shape
@@ -90,8 +89,10 @@
 
     norm(0)
     copies[3].wait()
-    own, left, right = slots(place, order, sections)
-    targets = ((to_right, own < right), (to_left, own < left))
+    own = order[place[0]]
+    targets = tuple(
+        (out, own < order[q]) for out, q in zip((to_odd, to_even), partners(place, sections))
+    )
     copies[4].wait()
 
     def old_copies(n, out):
@@ -171,11 +172,13 @@
 
 
 def other_rows_kernel(
-    place, side, own_half, half, own_cache, own_keys, key_weight, value_weight, weight, gains,
-    keep, cache, queries, keys, vbuf, query_weight, sem,
+    place, side, own_half, half_in, own_cache, own_keys, key_weight, value_weight, weight, gains,
+    keep, cache, queries, keys, vbuf, half, raw, query_weight, sems,
 ):
-    load = pltpu.make_async_copy(weight.at[0], query_weight, sem)
-    load.start()
+    load_half = pltpu.make_async_copy(half_in, half, sems.at[0])
+    load_half.start()
+    load_weight = pltpu.make_async_copy(weight.at[0], query_weight, sems.at[1])
+    load_weight.start()
     rows = half.shape[0]
     width = keys.shape[1]
     size = gains.shape[1]
@@ -183,34 +186,44 @@
     h = side[0]
     at = pl.ds(pl.multiple_of((1 - h) * rows, rows), rows)
     own_at = pl.ds(pl.multiple_of(h * rows, rows), rows)
+    stores = [
+        pltpu.make_async_copy(own_cache, cache.at[:, own_at, :], sems.at[2]),
+        pltpu.make_async_copy(raw.at[1], cache.at[1, at, :], sems.at[3]),
+        pltpu.make_async_copy(raw.at[0], cache.at[0, at, :], sems.at[4]),
+    ]
+    stores[0].start()
     mask = mask_columns((keep[pl.ds(place[0], 1), :] > 0).astype(f32), size)
     for i in range(width // size):
         vbuf[i, :, size:] = mask
-    cache[:, own_at, :] = own_cache[...]
     keys[own_at, :] = own_keys[...]
+    for i in range(width // size):
+        vbuf[i, own_at, :size] = (
+            own_cache[1, :, i * size : (i + 1) * size] * vbuf[0, own_at, size:]
+        )
     gain = gain_row(gains, 1)
+    load_half.wait()
     for j in range(0, width, block):
         cols = slice(j, j + block)
         y = jnp.dot(half[...], value_weight[:, cols], preferred_element_type=f32).astype(bf16)
-        cache[1, at, cols] = y
+        raw[1, :, cols] = y
         for low in range(0, block, size):
-            i = (j + low) // size
-            vbuf[i, at, :size] = y[:, low : low + size] * vbuf[0, at, size:]
-            vbuf[i, own_at, :size] = (
-                own_cache[1, :, i * size : (i + 1) * size] * vbuf[0, own_at, size:]
-            )
+            vbuf[(j + low) // size, at, :size] = y[:, low : low + size] * vbuf[0, at, size:]
     for j in range(0, width, block):
         cols = slice(j, j + block)
         y = jnp.dot(half[...], key_weight[:, cols], preferred_element_type=f32).astype(bf16)
-        cache[0, at, cols] = y
+        raw[0, :, cols] = y
         keys[at, cols] = heads_normed(y.astype(f32), gain)
     gain = gain_row(gains, 0) * (math.log2(math.e) * size**-0.5)
-    load.wait()
+    load_weight.wait()
+    stores[1].start()
+    stores[2].start()
     for j in range(0, width, block):
         cols = slice(j, j + block)
         for source, rows_at in ((own_half, own_at), (half, at)):
             y = jnp.dot(source[...], query_weight[:, cols], preferred_element_type=f32)
             queries[rows_at, cols] = heads_normed(y, gain)
+    for store in stores:
+        store.wait()
 
 
 def own_kernel(count, queries, keys, vbuf, text_in, gains, total, text, text_keys, tbuf, sem):
@@ -234,29 +247,19 @@
         total[:, wide * i : wide * (i + 1)] += attend(queries[:, cols], text_keys[:, cols], tbuf[i])
 
 
-def side_mask(keep, place, sections, by, size):
-    wanted = place[0] + by
-    there = (wanted >= 0) & (wanted < sections)
-    row = keep[pl.ds(jnp.clip(wanted, 0, sections - 1), 1), :]
-    return mask_columns(((row > 0) & there).astype(f32), size)
-
-
-def add_side(queries, keys, vbuf, total, size):
-    for i in range(queries.shape[1] // size):
-        cols = slice(i * size, (i + 1) * size)
-        wide = slice(2 * i * size, 2 * (i + 1) * size)
-        total[:, wide] += attend(queries[:, cols], keys[:, cols], vbuf[i])
-
-
-def fresh_kernel(
+def side_mask(keep, wanted, size):
+    return mask_columns((keep[pl.ds(wanted, 1), :] > 0).astype(f32), size)
+
+
+def near_kernel(
     sections,
     place,
     side,
     order,
-    left_own,
-    left_other,
-    right_own,
-    right_other,
+    odd_own,
+    odd_other,
+    even_own,
+    even_other,
     key_weight,
     value_weight,
     gains,
@@ -264,26 +267,26 @@
     keep,
     total_in,
     total,
+    weights,
     keys,
     vbuf,
 ):
-    rows = left_own.shape[0]
-    _, width = queries.shape
+    rows = odd_own.shape[0]
+    patch, width = queries.shape
     size = gains.shape[1]
     block = 2 * size
+    heads = width // size
     h = side[0]
-    own, left, right = slots(place, order, sections)
+    own = order[place[0]]
     gain = gain_row(gains, 1)
     total[...] = total_in[...]
-    for mine, other, fresh, by in (
-        (left_own, left_other, left < own, -1),
-        (right_own, right_other, right < own, 1),
-    ):
-
-        @pl.when(fresh)
-        def _():
-            mask = side_mask(keep, place, sections, by, size)
-            for i in range(width // size):
+    sources = ((odd_own, odd_other), (even_own, even_other))
+    for n, ((mine, other), q) in enumerate(zip(sources, partners(place, sections))):
+
+        @pl.when(order[q] < own)
+        def _():
+            mask = side_mask(keep, q, size)
+            for i in range(heads):
                 vbuf[i, :, size:] = mask
             for half, at in ((mine, h), (other, 1 - h)):
                 at = pl.ds(pl.multiple_of(at * rows, rows), rows)
@@ -295,82 +298,84 @@
                     cols = slice(j, j + block)
                     y = jnp.dot(half[...], value_weight[:, cols], preferred_element_type=f32)
                     y = y.astype(bf16)
-                    for i in range(block // size):
-                        vbuf[j // size + i, at, :size] = (
-                            y[:, i * size : (i + 1) * size] * vbuf[0, at, size:]
+                    for low in range(0, block, size):
+                        vbuf[(j + low) // size, at, :size] = (
+                            y[:, low : low + size] * vbuf[0, at, size:]
                         )
-            add_side(queries, keys, vbuf, total, size)
-
-
-def stale_kernel(
+            for i in range(heads):
+                cols = slice(i * size, (i + 1) * size)
+                wide = slice(2 * i * size, 2 * (i + 1) * size)
+                total[:, wide] += attend(queries[:, cols], keys[:, cols], vbuf[i])
+
+        @pl.when(order[q] > own)
+        def _():
+            for r in range(patch // rows):
+                keys[r * rows : (r + 1) * rows, :] = heads_normed(
+                    mine[:, r * width : (r + 1) * width].astype(f32), gain
+                )
+            for i in range(heads):
+                cols = slice(i * size, (i + 1) * size)
+                s = lax.dot_general(
+                    queries[:, cols],
+                    keys[:, cols],
+                    (((1,), (1,)), ((), ())),
+                    preferred_element_type=f32,
+                )
+                weights[n, i] = jnp.exp2(s).astype(bf16)
+
+
+def finish_kernel(
     sections,
+    flip,
     place,
     side,
     order,
-    left_keys,
-    left_values,
-    right_keys,
-    right_values,
-    gains,
-    queries,
+    weights,
+    odd_values,
+    even_values,
     keep,
-    total_in,
+    total,
     weight,
-    sent,
-    mine,
-    keys,
+    out,
     vbuf,
-    total,
+    sums,
     att,
 ):
-    rows = sent.shape[0]
-    patch, width = queries.shape
-    size = gains.shape[1]
-    p = place[0]
+    rows = out.shape[0]
+    heads = vbuf.shape[0]
+    size = vbuf.shape[2] // 2
     h = side[0]
-    own, left, right = slots(place, order, sections)
-    gain = gain_row(gains, 1)
-    total[...] = total_in[...]
-    for raw, values, wanted, by in (
-        (left_keys, left_values, (left > own) & (p > 0), -1),
-        (right_keys, right_values, (right > own) & (p < sections - 1), 1),
-    ):
-
-        @pl.when(wanted)
-        def _():
-            mask = side_mask(keep, place, sections, by, size)
-            for r in range(patch // rows):
-                keys[r * rows : (r + 1) * rows, :] = heads_normed(
-                    raw[:, r * width : (r + 1) * width].astype(f32), gain
+    at = pl.ds(pl.multiple_of((1 - h if flip else h) * rows, rows), rows)
+    own = order[place[0]]
+    sums[...] = total[at, :]
+    for n, (values, q) in enumerate(zip((odd_values, even_values), partners(place, sections))):
+
+        @pl.when(order[q] > own)
+        def _():
+            mask = side_mask(keep, q, size)
+            for i in range(heads):
+                vbuf[i, :, size:] = mask
+                vbuf[i, :, :size] = values[:, i * size : (i + 1) * size] * mask
+                sums[:, 2 * i * size : 2 * (i + 1) * size] += jnp.dot(
+                    weights[n, i, at, :], vbuf[i], preferred_element_type=f32
                 )
-            for i in range(width // size):
-                cols = slice(i * size, (i + 1) * size)
-                vbuf[i, :, size:] = mask
-                vbuf[i, :, :size] = values[:, cols] * mask
-            add_side(queries, keys, vbuf, total, size)
-
-    for i in range(width // size):
+
+    for i in range(heads):
         low = 2 * i * size
         att[:, i * size : (i + 1) * size] = (
-            total[:, low : low + size] / total[:, low + size : low + 2 * size]
+            sums[:, low : low + size] / sums[:, low + size : low + 2 * size]
         ).astype(bf16)
-    at = pl.ds(pl.multiple_of((1 - h) * rows, rows), rows)
-    sent[...] = jnp.dot(att[at, :], weight[...], preferred_element_type=f32).astype(bf16)
-    mine[...] = att[pl.ds(pl.multiple_of(h * rows, rows), rows), :]
-
-
-def kept_kernel(mine, weight, kept):
-    kept[...] = jnp.dot(mine[...], weight[...], preferred_element_type=f32).astype(bf16)
+    out[...] = jnp.dot(att[...], weight[...], preferred_element_type=f32).astype(bf16)
 
 
 def swapped(array):
     return lax.ppermute(array, "head", [(0, 1), (1, 0)])
 
 
-def from_behind(array, axis, by):
-    count = lax.axis_size(axis)
-    pairs = [(i, i + by) for i in range(count) if 0 <= i + by < count]
-    return lax.ppermute(array, axis, pairs)
+def across(array, first):
+    count = lax.axis_size("section")
+    edges = [(i, i + 1) for i in range(first, count - 1, 2)]
+    return lax.ppermute(array, "section", edges + [(j, i) for i, j in edges])
 
 
 def on_device(
@@ -401,7 +406,7 @@
     total_shape = jax.ShapeDtypeStruct((patch, 2 * width), f32)
     stale_cache = in_hbm(stale_cache)
 
-    normed, to_right, to_left, values = pl.pallas_call(
+    normed, to_odd, to_even, values = pl.pallas_call(
         functools.partial(first_kernel, sections),
         out_shape=(half_shape, half_shape, half_shape, side_shape),
         in_specs=[SMEM, HBM, HBM, HBM, HBM],
@@ -421,10 +426,10 @@
         name="first",
     )(place, in_hbm(patch_order), in_hbm(video_tokens), in_hbm(modulation), stale_cache)
 
-    left_own = from_behind(to_right, "section", 1)
-    right_own = from_behind(to_left, "section", -1)
-    left_values = from_behind(values, "section", 1)
-    right_values = from_behind(values, "section", -1)
+    odd_own = across(to_odd, 1)
+    odd_values = across(values, 1)
+    even_own = across(to_even, 0)
+    even_values = across(values, 0)
     other = swapped(normed)
 
     weight_shape = jax.ShapeDtypeStruct((model, width), bf16)
@@ -453,9 +458,14 @@
             side_shape,
             jax.ShapeDtypeStruct((heads, patch, 2 * size), bf16),
         ),
-        in_specs=[SMEM, SMEM] + [VMEM] * 6 + [HBM, VMEM, VMEM],
-        out_specs=(VMEM,) * 4,
-        scratch_shapes=[pltpu.VMEM((model, width), bf16), pltpu.SemaphoreType.DMA],
+        in_specs=[SMEM, SMEM, VMEM, HBM] + [VMEM] * 4 + [HBM, VMEM, VMEM],
+        out_specs=(HBM,) + (VMEM,) * 3,
+        scratch_shapes=[
+            pltpu.VMEM((rows, model), bf16),
+            pltpu.VMEM((2, rows, width), bf16),
+            pltpu.VMEM((model, width), bf16),
+            pltpu.SemaphoreType.DMA((5,)),
+        ],
         compiler_params=params(16),
         cost_estimate=cost(8 * rows * model * width, 4 * rows * width),
         name="other_rows",
@@ -463,7 +473,7 @@
         place,
         side,
         normed,
-        other,
+        in_hbm(other),
         own_cache,
         own_keys,
         key_weight,
@@ -473,9 +483,9 @@
         keep,
     )
 
-    left_own, right_own, queries = lax.optimization_barrier((left_own, right_own, queries))
-    left_other = swapped(left_own)
-    right_other = swapped(right_own)
+    odd_own, even_own, queries = lax.optimization_barrier((odd_own, even_own, queries))
+    odd_other = swapped(odd_own)
+    even_other = swapped(even_own)
 
     total = pl.pallas_call(
         own_kernel,
@@ -493,11 +503,11 @@
         name="own",
     )(text_count, queries, keys, vbuf, in_hbm(text_cache), norm_gains)
 
-    total = pl.pallas_call(
-        functools.partial(fresh_kernel, sections),
-        out_shape=total_shape,
+    total, weights = pl.pallas_call(
+        functools.partial(near_kernel, sections),
+        out_shape=(total_shape, jax.ShapeDtypeStruct((2, heads, patch, patch), bf16)),
         in_specs=[SMEM] * 3 + [VMEM] * 10,
-        out_specs=VMEM,
+        out_specs=(VMEM, VMEM),
         scratch_shapes=[
             pltpu.VMEM((patch, width), bf16),
             pltpu.VMEM((heads, patch, 2 * size), bf16),
@@ -505,15 +515,15 @@
         input_output_aliases={12: 0},
         compiler_params=params(24),
         cost_estimate=cost(4 * patch * model * width, 6 * patch * width),
-        name="fresh",
+        name="near",
     )(
         place,
         side,
         patch_order,
-        left_own,
-        left_other,
-        right_own,
-        right_other,
+        odd_own,
+        odd_other,
+        even_own,
+        even_other,
         key_weight,
         value_weight,
         norm_gains,
@@ -522,44 +532,25 @@
         total,
     )
 
-    sent, mine = pl.pallas_call(
-        functools.partial(stale_kernel, sections),
-        out_shape=(half_shape, part_shape),
-        in_specs=[SMEM] * 3 + [VMEM] * 9,
-        out_specs=(VMEM, VMEM),
-        scratch_shapes=[
-            pltpu.VMEM((patch, width), bf16),
-            pltpu.VMEM((heads, patch, 2 * size), bf16),
-            pltpu.VMEM((patch, 2 * width), f32),
-            pltpu.VMEM((patch, width), bf16),
-        ],
-        compiler_params=params(24),
-        cost_estimate=cost(2 * patch * width * model, 6 * patch * width),
-        name="stale",
-    )(
-        place,
-        side,
-        patch_order,
-        left_own,
-        left_values,
-        right_own,
-        right_values,
-        norm_gains,
-        queries,
-        keep,
-        total,
-        output_weight,
-    )
+    def finish(flip):
+        return pl.pallas_call(
+            functools.partial(finish_kernel, sections, flip),
+            out_shape=half_shape,
+            in_specs=[SMEM] * 3 + [VMEM] * 6,
+            out_specs=VMEM,
+            scratch_shapes=[
+                pltpu.VMEM((heads, patch, 2 * size), bf16),
+                pltpu.VMEM((rows, 2 * width), f32),
+                pltpu.VMEM((rows, width), bf16),
+            ],
+            compiler_params=params(20),
+            cost_estimate=cost(2 * rows * width * model, 4 * rows * model),
+            name="finish_sent" if flip else "finish_kept",
+        )(place, side, patch_order, weights, odd_values, even_values, keep, total, output_weight)
+
+    sent = finish(True)
     received = swapped(sent)
-    kept = pl.pallas_call(
-        kept_kernel,
-        out_shape=half_shape,
-        in_specs=[VMEM, VMEM],
-        out_specs=VMEM,
-        compiler_params=params(8),
-        cost_estimate=cost(2 * rows * width * model, 4 * rows * model),
-        name="kept",
-    )(mine, output_weight)
+    kept = finish(False)
     mixed = kept.astype(f32) + received.astype(f32)
     updated = (video_tokens.astype(f32) + modulation[2] * mixed).astype(bf16)
     return (updated, fresh_cache)

time: 79.2 us -> 73.7 us (0.931)
  waiting for transfers between devices: 25.3 us -> 21.5 us
  starting transfers between devices: 28.3 us -> 25.8 us
  Pallas kernels: 20.8 us -> 21.8 us
  local copies, waits for them, and re-layouts: 1.73 us -> 0.81 us
    ppermute x4, waiting for transfers between devices: 24.9 us -> 21.5 us  [across(): return lax.ppermute(array, 'section', edges + [(j, i) for i, j in edges])]
    ppermute x4, starting transfers between devices: 5.3 us -> 2.92 us  [across(): return lax.ppermute(array, 'section', edges + [(j, i) for i, j in edges])]
    pallas_call x3, Pallas kernels: 6.08 us -> 7.29 us  [the longest x2 4.75 us: finish(): pl.pallas_call(functools.partial(finish_kernel, sections, flip), out_shap...]
    unnamed x14 -> x10, local copies, waits for them, and re-layouts: 0.94 us -> 0.03 us
  transfers between devices with their start and end apart: 8 -> 8, of which waited for: 5 -> 2; matrix products, arithmetic and copies ran while one was open for 1% -> 1% of each run, Pallas kernels for 18% -> 23%
where the time goes in v4:
time: 73.7 us; the launch traced here: 72.7 us
  starting transfers between devices  25.8 us (35%)
  Pallas kernels  21.8 us (30%)
  waiting for transfers between devices  21.5 us (29%)
  between operations  1.5 us (2%)
  other arithmetic  1.22 us (2%)
  local copies, waits for them, and re-layouts  0.81 us (1%)
    ppermute x4, starting transfers between devices, swapped(): return lax.ppermute(array, 'head', [(0, 1), (1, 0)])  22.9 us
    ppermute x4, waiting for transfers between devices, across(): return lax.ppermute(array, 'section', edges + [(j, i) for i, j in edges])  21.5 us
    pallas_call x1, Pallas kernels, on_device(): pl.pallas_call(other_rows_kernel, out_shape=(jax.ShapeDtypeStruct((2, pat...  5.09 us
    pallas_call x2, Pallas kernels, finish(): pl.pallas_call(functools.partial(finish_kernel, sections, flip), out_shap...  4.75 us
    pallas_call x1, Pallas kernels, on_device(): pl.pallas_call(own_rows_kernel, out_shape=(jax.ShapeDtypeStruct((2, rows,...  3.5 us
    pallas_call x1, Pallas kernels, on_device(): pl.pallas_call(own_kernel, out_shape=total_shape, in_specs=[SMEM, VMEM, V...  3.13 us
    ppermute x4, starting transfers between devices, across(): return lax.ppermute(array, 'section', edges + [(j, i) for i, j in edges])  2.92 us
    pallas_call x1, Pallas kernels, on_device(): pl.pallas_call(functools.partial(first_kernel, sections), out_shape=(half...  2.79 us
  transfers between devices with their start and end apart: 8, of which 2 were waited for; matrix products, arithmetic and copies ran while one was open for 1% of the time, Pallas kernels for 23%

profile of v4, /device:TPU:513, one launch (start us, length us, event | category | flops | bytes accessed | tf_op | source)
XLA Modules:
  0.0 72.7 jit_solution(11102750399255034404)
XLA Ops:
  0.6 0.0 copy-start.4
  0.6 0.0 copy-start.1
  0.7 2.8 %first.1 = (bf16[256,1536]{1,0:T(8,128)(2,1)S(1)}, bf16[256,1536]{1,0:T(8,128)(2,1)}, bf16[256,1536]{1,0:T(8,128)(2,1)}, bf16[512,768]{1,0:T(8,128)(2,1)S(1)}) custom-call(s32[1]{0:T(128)} %bitcast.place, s32[64]{0:T(128)} %order.5, bf16[256,1536]{1,0:T(8,128)(2,1)} %x_in.1, f32[3,1536]{1,0:T(4,128)} %mod_in.1, bf16[2,512,768]{2,1,0:T(8,128)(2,1)} %stale.1), custom_call_target="tpu_custom_call" | custom-call | flops 3932160 | bytes 3932160 | tf_op jit(solution)/shard_map/first/pallas_call | solution.py:409
  3.4 20.5 %collective-permute-start.2 = (bf16[256,1536]{1,0:T(8,128)(2,1)S(1)}, bf16[256,1536]{1,0:T(8,128)(2,1)}, u32[]{:S(2)}, u32[]{:S(2)}) collective-permute-start(bf16[256,1536]{1,0:T(8,128)(2,1)S(1)} %get-tuple-element.21.half.own_half), channel_id=1, source_target_pairs={{0,1},{1,0},{2,3},{3,2},{4,5},{5,4},{6,7},{7,6},{8,9},{9,8},{10,11... | collective-permute-start | bytes 2359304 | tf_op jit(solution)/shard_map/ppermute | solution.py:372
  24.0 0.7 collective-permute-start
  24.7 0.1 collective-permute-start.1
  24.8 0.0 copy-done.4
  24.9 3.5 %own_rows.1 = (bf16[2,256,768]{2,1,0:T(8,128)(2,1)S(1)}, bf16[256,768]{1,0:T(8,128)(2,1)S(1)}, bf16[1536,768]{1,0:T(8,128)(2,1)S(1)}, bf16[1536,768]{1,0:T(8,128)(2,1)S(1)}) custom-call(bf16[256,1536]{1,0:T(8,128)(2,1)S(1)} %get-tuple-element.21.half.own_half, bf16[3,1536,768]{2,1,0:T(8,128)(2,1)} %weight.5, f32[3,128]{1,0:T(4,128)S(1)} %copy-done.1), custom_call_target="tpu_custom_call" | custom-call | flops 1207959552 | bytes 786432 | tf_op jit(solution)/shard_map/own_rows/pallas_call | solution.py:437
  28.4 0.0 collective-permute-done.2.half_in
  28.4 5.1 %other_rows.1 = (bf16[2,512,768]{2,1,0:T(8,128)(2,1)}, bf16[512,768]{1,0:T(8,128)(2,1)S(1)}, bf16[512,768]{1,0:T(8,128)(2,1)S(1)}, bf16[6,512,256]{2,1,0:T(8,128)(2,1)S(1)}) custom-call(s32[1]{0:T(128)} %bitcast.place, s32[1]{0:T(128)} %bitcast.1.side, bf16[256,1536]{1,0:T(8,128)(2,1)S(1)} %get-tuple-element.21.half.own_half, ...), custom_call_target="tpu_custom_call" | custom-call | flops 2415919104 | bytes 786432 | tf_op jit(solution)/shard_map/other_rows/pallas_call | solution.py:453
  33.5 0.0 collective-permute-done.odd_own
  33.5 10.6 %collective-permute-done.1.even_own = bf16[256,1536]{1,0:T(8,128)(2,1)S(1)} collective-permute-done((bf16[256,1536]{1,0:T(8,128)(2,1)}, bf16[256,1536]{1,0:T(8,128)(2,1)S(1)}, u32[]{:S(2)}, u32[]{:S(2)}) %collective-permute-start.1) | collective-permute-done | bytes 786464 | tf_op jit(solution)/shard_map/ppermute | solution.py:378
  44.1 0.9 %collective-permute-start.3 = (bf16[256,1536]{1,0:T(8,128)(2,1)S(1)}, bf16[256,1536]{1,0:T(8,128)(2,1)S(1)}, u32[]{:S(2)}, u32[]{:S(2)}) collective-permute-start(bf16[256,1536]{1,0:T(8,128)(2,1)S(1)} %collective-permute-done.odd_own), channel_id=1, source_target_pairs={{0,1},{1,0},{2,3},{3,2},{4,5},{5,4},{6,7},{7,6},{8,9},{9,8},{10,11... | collective-permute-start | bytes 2359304 | tf_op jit(solution)/shard_map/ppermute | solution.py:372
  45.0 0.0 collective-permute-start.4
  45.0 0.7 collective-permute-start.5
  45.7 1.4 %collective-permute-start.6 = (bf16[512,768]{1,0:T(8,128)(2,1)S(1)}, bf16[512,768]{1,0:T(8,128)(2,1)S(1)}, u32[]{:S(2)}, u32[]{:S(2)}) collective-permute-start(bf16[512,768]{1,0:T(8,128)(2,1)S(1)} %get-tuple-element.33), channel_id=1, source_target_pairs={{0,2},{4,6},{8,10},{12,14},{16,18},{20,22},{24,26},{28,30},{32,34}... | collective-permute-start | bytes 2359304 | tf_op jit(solution)/shard_map/ppermute | solution.py:378
  47.7 0.0 copy-start.2
  47.7 3.1 %own.1.total_in = f32[512,1536]{1,0:T(8,128)S(1)} custom-call(s32[1]{0:T(128)S(6)} %copy.14.count, bf16[512,768]{1,0:T(8,128)(2,1)S(1)} %get-tuple-element.29.queries, bf16[512,768]{1,0:T(8,128)(2,1)S(1)} %get-tuple-element.30.keys, bf16[6,512,256]{2,1,0:T(8,128)(2,1)S(1)} %get-tuple-element.31.vbuf, bf16[2,256,768]{2,1,0:T(8,128)(2,1)} %text_in.1, ...), custom_call_target="tpu_custom_call" | custom-call | flops 1811939328 | bytes 2359296 | tf_op jit(solution)/shard_map/own/pallas_call | solution.py:490
  50.9 0.0 collective-permute-done.3.odd_other
  50.9 0.0 collective-permute-done.4.even_other
  50.9 0.0 copy-start
  50.9 2.5 %near.1 = (f32[512,1536]{1,0:T(8,128)S(1)}, bf16[2,6,512,512]{3,2,1,0:T(8,128)(2,1)S(1)}) custom-call(s32[1]{0:T(128)} %bitcast.place, s32[1]{0:T(128)} %bitcast.1.side, s32[64]{0:T(128)S(1)} %copy-done.2, bf16[256,1536]{1,0:T(8,128)(2,1)S(1)} %collective-permute-done.odd_own, ...), custom_call_target="tpu_custom_call", output_to_operand_aliasing={{0}: (12, {})} | custom-call | flops 2415919104 | bytes 2359296 | tf_op jit(solution)/shard_map/near/pallas_call | solution.py:506
  53.5 0.0 collective-permute-done.5.odd_values
  53.5 10.9 %collective-permute-done.6.even_values = bf16[512,768]{1,0:T(8,128)(2,1)S(1)} collective-permute-done((bf16[512,768]{1,0:T(8,128)(2,1)S(1)}, bf16[512,768]{1,0:T(8,128)(2,1)S(1)}, u32[]{:S(2)}, u32[]{:S(2)}) %collective-permute-start.6) | collective-permute-done | bytes 786464 | tf_op jit(solution)/shard_map/ppermute | solution.py:378
  64.4 2.5 %finish_sent.1 = bf16[256,1536]{1,0:T(8,128)(2,1)S(1)} custom-call(s32[1]{0:T(128)} %bitcast.place, s32[1]{0:T(128)} %bitcast.1.side, s32[64]{0:T(128)S(1)} %copy-done.2, bf16[2,6,512,512]{3,2,1,0:T(8,128)(2,1)S(1)} %get-tuple-element.32.weights, bf16[512,768]{1,0:T(8,128)(2,1)S(1)} %collective-permute-done.5.odd_values, ...), custom_call_target="tpu_custom_call" | custom-call | flops 603979776 | bytes 1572864 | tf_op jit(solution)/shard_map/finish_sent/pallas_call | solution.py:536
  66.9 1.5 %collective-permute-start.7 = (bf16[256,1536]{1,0:T(8,128)(2,1)S(1)}, bf16[256,1536]{1,0:T(8,128)(2,1)S(1)}, u32[]{:S(2)}, u32[]{:S(2)}) collective-permute-start(bf16[256,1536]{1,0:T(8,128)(2,1)S(1)} %finish_sent.1), channel_id=1, source_target_pairs={{0,1},{1,0},{2,3},{3,2},{4,5},{5,4},{6,7},{7,6},{8,9},{9,8},{10,11... | collective-permute-start | bytes 2359304 | tf_op jit(solution)/shard_map/ppermute | solution.py:372
  68.4 0.8 %slice_reduce_fusion = f32[1536]{0:T(1024)S(1)} fusion(f32[3,1536]{1,0:T(4,128)} %mod_in.1), kind=kLoop, calls=%fused_computation.1 | loop fusion | bytes 12288 | tf_op jit(solution)/shard_map/slice | solution.py:555
  69.1 0.0 copy-start.3
  69.2 2.3 %finish_kept.1 = bf16[256,1536]{1,0:T(8,128)(2,1)S(1)} custom-call(s32[1]{0:T(128)} %bitcast.place, s32[1]{0:T(128)} %bitcast.1.side, s32[64]{0:T(128)S(1)} %copy-done.2, bf16[2,6,512,512]{3,2,1,0:T(8,128)(2,1)S(1)} %get-tuple-element.32.weights, bf16[512,768]{1,0:T(8,128)(2,1)S(1)} %collective-permute-done.5.odd_values, ...), custom_call_target="tpu_custom_call" | custom-call | flops 603979776 | bytes 1572864 | tf_op jit(solution)/shard_map/finish_kept/pallas_call | solution.py:536
  71.4 0.0 collective-permute-done.7
  71.4 0.0 copy-done.3
  71.5 1.2 %add_convert_fusion = bf16[256,1536]{1,0:T(8,128)(2,1)} fusion(bf16[256,1536]{1,0:T(8,128)(2,1)S(1)} %collective-permute-done.7, bf16[256,1536]{1,0:T(8,128)(2,1)S(1)} %finish_kept.1, bf16[256,1536]{1,0:T(8,128)(2,1)S(1)} %copy-done.3, f32[1536]{0:T(1024)S(1)} %slice_reduce_fusion), kind=kLoop, calls=%fused_computation | loop fusion | flops 2752512 | bytes 3151872 | tf_op jit(solution)/shard_map/convert_element_type | solution.py:555
  (4 shorter events, 0.0 us)
Async XLA Ops:
  0.6 24.2 %copy-start.4 = (s32[32768]{0:T(1024)S(1)}, s32[32768]{0:T(1024)}, u32[]{:S(2)}) copy-start(s32[32768]{0:T(1024)} %param.17) | copy-start | bytes 393220
  0.6 24.2 %copy-start.1 = (f32[3,128]{1,0:T(4,128)S(1)}, f32[3,128]{1,0:T(4,128)}, u32[]{:S(2)}) copy-start(f32[3,128]{1,0:T(4,128)} %gains.7) | copy-start | bytes 4612
  3.4 25.0 %collective-permute-start.2 = (bf16[256,1536]{1,0:T(8,128)(2,1)S(1)}, bf16[256,1536]{1,0:T(8,128)(2,1)}, u32[]{:S(2)}, u32[]{:S(2)}) collective-permute-start(bf16[256,1536]{1,0:T(8,128)(2,1)S(1)} %get-tuple-element.21.half.own_half), channel_id=1, source_target_pairs={{0,1},{1,0},{2,3},{3,2},{4,5},{5,4},{6,7},{7,6},{8,9},{9,8},{10,11... | collective-permute-start | bytes 2359304 | tf_op jit(solution)/shard_map/ppermute | solution.py:372
  24.0 9.5 %collective-permute-start = (bf16[256,1536]{1,0:T(8,128)(2,1)}, bf16[256,1536]{1,0:T(8,128)(2,1)S(1)}, u32[]{:S(2)}, u32[]{:S(2)}) collective-permute-start(bf16[256,1536]{1,0:T(8,128)(2,1)} %get-tuple-element.19), channel_id=1, source_target_pairs={{2,4},{6,8},{10,12},{14,16},{18,20},{22,24},{26,28},{30,32},{34,36... | collective-permute-start | bytes 2359304 | tf_op jit(solution)/shard_map/ppermute | solution.py:378
  24.7 19.4 %collective-permute-start.1 = (bf16[256,1536]{1,0:T(8,128)(2,1)}, bf16[256,1536]{1,0:T(8,128)(2,1)S(1)}, u32[]{:S(2)}, u32[]{:S(2)}) collective-permute-start(bf16[256,1536]{1,0:T(8,128)(2,1)} %get-tuple-element.20), channel_id=1, source_target_pairs={{0,2},{4,6},{8,10},{12,14},{16,18},{20,22},{24,26},{28,30},{32,34}... | collective-permute-start | bytes 2359304 | tf_op jit(solution)/shard_map/ppermute | solution.py:378
  44.1 6.8 %collective-permute-start.3 = (bf16[256,1536]{1,0:T(8,128)(2,1)S(1)}, bf16[256,1536]{1,0:T(8,128)(2,1)S(1)}, u32[]{:S(2)}, u32[]{:S(2)}) collective-permute-start(bf16[256,1536]{1,0:T(8,128)(2,1)S(1)} %collective-permute-done.odd_own), channel_id=1, source_target_pairs={{0,1},{1,0},{2,3},{3,2},{4,5},{5,4},{6,7},{7,6},{8,9},{9,8},{10,11... | collective-permute-start | bytes 2359304 | tf_op jit(solution)/shard_map/ppermute | solution.py:372
  45.0 5.9 %collective-permute-start.4 = (bf16[256,1536]{1,0:T(8,128)(2,1)S(1)}, bf16[256,1536]{1,0:T(8,128)(2,1)S(1)}, u32[]{:S(2)}, u32[]{:S(2)}) collective-permute-start(bf16[256,1536]{1,0:T(8,128)(2,1)S(1)} %collective-permute-done.1.even_own), channel_id=1, source_target_pairs={{0,1},{1,0},{2,3},{3,2},{4,5},{5,4},{6,7},{7,6},{8,9},{9,8},{10,11... | collective-permute-start | bytes 2359304 | tf_op jit(solution)/shard_map/ppermute | solution.py:372
  45.0 8.5 %collective-permute-start.5 = (bf16[512,768]{1,0:T(8,128)(2,1)S(1)}, bf16[512,768]{1,0:T(8,128)(2,1)S(1)}, u32[]{:S(2)}, u32[]{:S(2)}) collective-permute-start(bf16[512,768]{1,0:T(8,128)(2,1)S(1)} %get-tuple-element.33), channel_id=1, source_target_pairs={{2,4},{6,8},{10,12},{14,16},{18,20},{22,24},{26,28},{30,32},{34,36... | collective-permute-start | bytes 2359304 | tf_op jit(solution)/shard_map/ppermute | solution.py:378
  45.7 18.7 %collective-permute-start.6 = (bf16[512,768]{1,0:T(8,128)(2,1)S(1)}, bf16[512,768]{1,0:T(8,128)(2,1)S(1)}, u32[]{:S(2)}, u32[]{:S(2)}) collective-permute-start(bf16[512,768]{1,0:T(8,128)(2,1)S(1)} %get-tuple-element.33), channel_id=1, source_target_pairs={{0,2},{4,6},{8,10},{12,14},{16,18},{20,22},{24,26},{28,30},{32,34}... | collective-permute-start | bytes 2359304 | tf_op jit(solution)/shard_map/ppermute | solution.py:378
  47.7 3.2 %copy-start.2 = (s32[64]{0:T(128)S(1)}, s32[64]{0:T(128)}, u32[]{:S(2)}) copy-start(s32[64]{0:T(128)} %order.5) | copy-start | bytes 772
  50.9 13.5 %copy-start = (bf16[768,1536]{1,0:T(8,128)(2,1)S(1)}, bf16[768,1536]{1,0:T(8,128)(2,1)}, u32[]{:S(2)}) copy-start(bf16[768,1536]{1,0:T(8,128)(2,1)} %weight.7) | copy-start | bytes 7077892
  66.9 4.5 %collective-permute-start.7 = (bf16[256,1536]{1,0:T(8,128)(2,1)S(1)}, bf16[256,1536]{1,0:T(8,128)(2,1)S(1)}, u32[]{:S(2)}, u32[]{:S(2)}) collective-permute-start(bf16[256,1536]{1,0:T(8,128)(2,1)S(1)} %finish_sent.1), channel_id=1, source_target_pairs={{0,1},{1,0},{2,3},{3,2},{4,5},{5,4},{6,7},{7,6},{8,9},{9,8},{10,11... | collective-permute-start | bytes 2359304 | tf_op jit(solution)/shard_map/ppermute | solution.py:372
  69.1 2.3 %copy-start.3 = (bf16[256,1536]{1,0:T(8,128)(2,1)S(1)}, bf16[256,1536]{1,0:T(8,128)(2,1)}, u32[]{:S(2)}) copy-start(bf16[256,1536]{1,0:T(8,128)(2,1)} %x_in.1) | copy-start | bytes 2359300

commit v5 on v4

--- a/solution.py
+++ b/solution.py
@@ -147,10 +147,13 @@
     return jnp.dot(jnp.exp2(s).astype(bf16), vbuf, preferred_element_type=f32)
 
 
-def own_rows_kernel(half, weight, gains, cache, keys, key_weight, value_weight, sems):
+def own_rows_kernel(
+    half, weight, gains_in, cache, keys, key_weight, value_weight, gains, sems, gains_sem
+):
+    load_gains = pltpu.make_async_copy(gains_in, gains, gains_sem)
+    load_gains.start()
     width = keys.shape[1]
     block = 2 * gains.shape[1]
-    gain = gain_row(gains, 1)
     buffers = {2: value_weight, 1: key_weight}
     pieces = ((2, 0, block), (2, block, width), (1, 0, width))
     copies = []
@@ -160,6 +163,8 @@
         )
         copy.start()
         copies.append(copy)
+    load_gains.wait()
+    gain = gain_row(gains, 1)
     for n, (c, low, high) in enumerate(pieces):
         copies[n].wait()
         for j in range(low, high, block):
@@ -253,13 +258,12 @@
 
 def near_kernel(
     sections,
+    edge,
     place,
     side,
     order,
-    odd_own,
-    odd_other,
-    even_own,
-    even_other,
+    mine,
+    other,
     key_weight,
     value_weight,
     gains,
@@ -271,57 +275,56 @@
     keys,
     vbuf,
 ):
-    rows = odd_own.shape[0]
+    rows = mine.shape[0]
     patch, width = queries.shape
     size = gains.shape[1]
     block = 2 * size
     heads = width // size
     h = side[0]
     own = order[place[0]]
+    q = partners(place, sections)[edge]
     gain = gain_row(gains, 1)
     total[...] = total_in[...]
-    sources = ((odd_own, odd_other), (even_own, even_other))
-    for n, ((mine, other), q) in enumerate(zip(sources, partners(place, sections))):
-
-        @pl.when(order[q] < own)
-        def _():
-            mask = side_mask(keep, q, size)
-            for i in range(heads):
-                vbuf[i, :, size:] = mask
-            for half, at in ((mine, h), (other, 1 - h)):
-                at = pl.ds(pl.multiple_of(at * rows, rows), rows)
-                for j in range(0, width, block):
-                    cols = slice(j, j + block)
-                    y = jnp.dot(half[...], key_weight[:, cols], preferred_element_type=f32)
-                    keys[at, cols] = heads_normed(y.astype(bf16).astype(f32), gain)
-                for j in range(0, width, block):
-                    cols = slice(j, j + block)
-                    y = jnp.dot(half[...], value_weight[:, cols], preferred_element_type=f32)
-                    y = y.astype(bf16)
-                    for low in range(0, block, size):
-                        vbuf[(j + low) // size, at, :size] = (
-                            y[:, low : low + size] * vbuf[0, at, size:]
-                        )
-            for i in range(heads):
-                cols = slice(i * size, (i + 1) * size)
-                wide = slice(2 * i * size, 2 * (i + 1) * size)
-                total[:, wide] += attend(queries[:, cols], keys[:, cols], vbuf[i])
-
-        @pl.when(order[q] > own)
-        def _():
-            for r in range(patch // rows):
-                keys[r * rows : (r + 1) * rows, :] = heads_normed(
-                    mine[:, r * width : (r + 1) * width].astype(f32), gain
-                )
-            for i in range(heads):
-                cols = slice(i * size, (i + 1) * size)
-                s = lax.dot_general(
-                    queries[:, cols],
-                    keys[:, cols],
-                    (((1,), (1,)), ((), ())),
-                    preferred_element_type=f32,
-                )
-                weights[n, i] = jnp.exp2(s).astype(bf16)
+
+    @pl.when(order[q] < own)
+    def _():
+        mask = side_mask(keep, q, size)
+        for i in range(heads):
+            vbuf[i, :, size:] = mask
+        for half, at in ((mine, h), (other, 1 - h)):
+            at = pl.ds(pl.multiple_of(at * rows, rows), rows)
+            for j in range(0, width, block):
+                cols = slice(j, j + block)
+                y = jnp.dot(half[...], key_weight[:, cols], preferred_element_type=f32)
+                keys[at, cols] = heads_normed(y.astype(bf16).astype(f32), gain)
+            for j in range(0, width, block):
+                cols = slice(j, j + block)
+                y = jnp.dot(half[...], value_weight[:, cols], preferred_element_type=f32)
+                y = y.astype(bf16)
+                for low in range(0, block, size):
+                    vbuf[(j + low) // size, at, :size] = (
+                        y[:, low : low + size] * vbuf[0, at, size:]
+                    )
+        for i in range(heads):
+            cols = slice(i * size, (i + 1) * size)
+            wide = slice(2 * i * size, 2 * (i + 1) * size)
+            total[:, wide] += attend(queries[:, cols], keys[:, cols], vbuf[i])
+
+    @pl.when(order[q] > own)
+    def _():
+        for r in range(patch // rows):
+            keys[r * rows : (r + 1) * rows, :] = heads_normed(
+                mine[:, r * width : (r + 1) * width].astype(f32), gain
+            )
+        for i in range(heads):
+            cols = slice(i * size, (i + 1) * size)
+            s = lax.dot_general(
+                queries[:, cols],
+                keys[:, cols],
+                (((1,), (1,)), ((), ())),
+                preferred_element_type=f32,
+            )
+            weights[i] = jnp.exp2(s).astype(bf16)
 
 
 def finish_kernel(
@@ -330,7 +333,8 @@
     place,
     side,
     order,
-    weights,
+    odd_weights,
+    even_weights,
     odd_values,
     even_values,
     keep,
@@ -348,7 +352,8 @@
     at = pl.ds(pl.multiple_of((1 - h if flip else h) * rows, rows), rows)
     own = order[place[0]]
     sums[...] = total[at, :]
-    for n, (values, q) in enumerate(zip((odd_values, even_values), partners(place, sections))):
+    odd, even = partners(place, sections)
+    for weights, values, q in ((odd_weights, odd_values, odd), (even_weights, even_values, even)):
 
         @pl.when(order[q] > own)
         def _():
@@ -357,7 +362,7 @@
                 vbuf[i, :, size:] = mask
                 vbuf[i, :, :size] = values[:, i * size : (i + 1) * size] * mask
                 sums[:, 2 * i * size : 2 * (i + 1) * size] += jnp.dot(
-                    weights[n, i, at, :], vbuf[i], preferred_element_type=f32
+                    weights[i, at, :], vbuf[i], preferred_element_type=f32
                 )
 
     for i in range(heads):
@@ -366,6 +371,15 @@
             sums[:, low : low + size] / sums[:, low + size : low + 2 * size]
         ).astype(bf16)
     out[...] = jnp.dot(att[...], weight[...], preferred_element_type=f32).astype(bf16)
+
+
+def add_kernel(tokens, mod, kept, received, out):
+    gate = mod[2:3, :]
+    step = 64
+    for r in range(0, tokens.shape[0], step):
+        at = slice(r, r + step)
+        mixed = kept[at, :].astype(f32) + received[at, :].astype(f32)
+        out[at, :] = (tokens[at, :].astype(f32) + gate * mixed).astype(bf16)
 
 
 def swapped(array):
@@ -427,8 +441,8 @@
     )(place, in_hbm(patch_order), in_hbm(video_tokens), in_hbm(modulation), stale_cache)
 
     odd_own = across(to_odd, 1)
+    even_own = across(to_even, 0)
     odd_values = across(values, 1)
-    even_own = across(to_even, 0)
     even_values = across(values, 0)
     other = swapped(normed)
 
@@ -442,13 +456,17 @@
             weight_shape,
             weight_shape,
         ),
-        in_specs=[VMEM, HBM, VMEM],
+        in_specs=[VMEM, HBM, HBM],
         out_specs=(VMEM,) * 4,
-        scratch_shapes=[pltpu.SemaphoreType.DMA((3,))],
+        scratch_shapes=[
+            pltpu.VMEM(norm_gains.shape, f32),
+            pltpu.SemaphoreType.DMA((3,)),
+            pltpu.SemaphoreType.DMA,
+        ],
         compiler_params=params(10),
         cost_estimate=cost(4 * rows * model * width, 4 * rows * width),
         name="own_rows",
-    )(normed, project_weight, norm_gains)
+    )(normed, project_weight, in_hbm(norm_gains))
 
     fresh_cache, queries, keys, vbuf = pl.pallas_call(
         other_rows_kernel,
@@ -483,10 +501,6 @@
         keep,
     )
 
-    odd_own, even_own, queries = lax.optimization_barrier((odd_own, even_own, queries))
-    odd_other = swapped(odd_own)
-    even_other = swapped(even_own)
-
     total = pl.pallas_call(
         own_kernel,
         out_shape=total_shape,
@@ -503,40 +517,46 @@
         name="own",
     )(text_count, queries, keys, vbuf, in_hbm(text_cache), norm_gains)
 
-    total, weights = pl.pallas_call(
-        functools.partial(near_kernel, sections),
-        out_shape=(total_shape, jax.ShapeDtypeStruct((2, heads, patch, patch), bf16)),
-        in_specs=[SMEM] * 3 + [VMEM] * 10,
-        out_specs=(VMEM, VMEM),
-        scratch_shapes=[
-            pltpu.VMEM((patch, width), bf16),
-            pltpu.VMEM((heads, patch, 2 * size), bf16),
-        ],
-        input_output_aliases={12: 0},
-        compiler_params=params(24),
-        cost_estimate=cost(4 * patch * model * width, 6 * patch * width),
-        name="near",
-    )(
-        place,
-        side,
-        patch_order,
-        odd_own,
-        odd_other,
-        even_own,
-        even_other,
-        key_weight,
-        value_weight,
-        norm_gains,
-        queries,
-        keep,
-        total,
-    )
+    odd_own, even_own, total = lax.optimization_barrier((odd_own, even_own, total))
+    odd_other = swapped(odd_own)
+    even_other = swapped(even_own)
+
+    def near(edge, mine, other, total):
+        return pl.pallas_call(
+            functools.partial(near_kernel, sections, edge),
+            out_shape=(total_shape, jax.ShapeDtypeStruct((heads, patch, patch), bf16)),
+            in_specs=[SMEM] * 3 + [VMEM] * 8,
+            out_specs=(VMEM, VMEM),
+            scratch_shapes=[
+                pltpu.VMEM((patch, width), bf16),
+                pltpu.VMEM((heads, patch, 2 * size), bf16),
+            ],
+            input_output_aliases={10: 0},
+            compiler_params=params(16),
+            cost_estimate=cost(4 * patch * model * width, 6 * patch * width),
+            name="near_even" if edge else "near_odd",
+        )(
+            place,
+            side,
+            patch_order,
+            mine,
+            other,
+            key_weight,
+            value_weight,
+            norm_gains,
+            queries,
+            keep,
+            total,
+        )
+
+    total, odd_weights = near(0, odd_own, odd_other, total)
+    total, even_weights = near(1, even_own, even_other, total)
 
     def finish(flip):
         return pl.pallas_call(
             functools.partial(finish_kernel, sections, flip),
             out_shape=half_shape,
-            in_specs=[SMEM] * 3 + [VMEM] * 6,
+            in_specs=[SMEM] * 3 + [VMEM] * 7,
             out_specs=VMEM,
             scratch_shapes=[
                 pltpu.VMEM((heads, patch, 2 * size), bf16),
@@ -546,13 +566,31 @@
             compiler_params=params(20),
             cost_estimate=cost(2 * rows * width * model, 4 * rows * model),
             name="finish_sent" if flip else "finish_kept",
-        )(place, side, patch_order, weights, odd_values, even_values, keep, total, output_weight)
+        )(
+            place,
+            side,
+            patch_order,
+            odd_weights,
+            even_weights,
+            odd_values,
+            even_values,
+            keep,
+            total,
+            output_weight,
+        )
 
     sent = finish(True)
     received = swapped(sent)
     kept = finish(False)
-    mixed = kept.astype(f32) + received.astype(f32)
-    updated = (video_tokens.astype(f32) + modulation[2] * mixed).astype(bf16)
+    updated = pl.pallas_call(
+        add_kernel,
+        out_shape=half_shape,
+        in_specs=[VMEM] * 4,
+        out_specs=VMEM,
+        compiler_params=params(8),
+        cost_estimate=cost(6 * rows * model, 8 * rows * model),
+        name="add",
+    )(video_tokens, modulation, kept, received)
     return (updated, fresh_cache)
 
 

time: 73.7 us -> 72.9 us (0.989)
  Pallas kernels: 21.8 us -> 24.6 us
  waiting for transfers between devices: 21.5 us -> 18.9 us
  other arithmetic: 1.22 us -> 0 us
    ppermute x4, waiting for transfers between devices: 21.5 us -> 18.9 us  [across(): return lax.ppermute(array, 'section', edges + [(j, i) for i, j in edges])]
    pallas_call x1 -> x3, Pallas kernels: 2.54 us -> 4.7 us  [the longest x2 3.49 us: near(): pl.pallas_call(functools.partial(near_kernel, sections, edge), out_shape=...]
    convert_element_type x1 -> x0, other arithmetic: 1.22 us -> none  [on_device(): updated = (video_tokens.astype(f32) + modulation[2] * mixed).astype(bf16)]
    reshape x1, local copies, waits for them, and re-layouts: 0.02 us -> 0.93 us  [on_device(): keep = video_keep.reshape(sections, patch)]
    slice x1 -> x0, local copies, waits for them, and re-layouts: 0.76 us -> none  [on_device(): updated = (video_tokens.astype(f32) + modulation[2] * mixed).astype(bf16)]
  transfers between devices with their start and end apart: 8 -> 8, of which waited for: 2 -> 2; matrix products, arithmetic and copies ran while one was open for 1% -> 1% of each run, Pallas kernels for 23% -> 25%
where the time goes in v5:
time: 72.9 us; the launch traced here: 71.8 us
  starting transfers between devices  25.8 us (35%)
  Pallas kernels  24.6 us (34%)
  waiting for transfers between devices  18.9 us (26%)
  between operations  1.48 us (2%)
  local copies, waits for them, and re-layouts  0.96 us (1%)
    ppermute x4, starting transfers between devices, swapped(): return lax.ppermute(array, 'head', [(0, 1), (1, 0)])  22.9 us
    ppermute x4, waiting for transfers between devices, across(): return lax.ppermute(array, 'section', edges + [(j, i) for i, j in edges])  18.9 us
    pallas_call x1, Pallas kernels, on_device(): pl.pallas_call(other_rows_kernel, out_shape=(jax.ShapeDtypeStruct((2, pat...  5.09 us
    pallas_call x2, Pallas kernels, finish(): pl.pallas_call(functools.partial(finish_kernel, sections, flip), out_shap...  4.74 us
    pallas_call x1, Pallas kernels, on_device(): pl.pallas_call(own_rows_kernel, out_shape=(jax.ShapeDtypeStruct((2, rows,...  4.24 us
    pallas_call x2, Pallas kernels, near(): pl.pallas_call(functools.partial(near_kernel, sections, edge), out_shape=...  3.49 us
    pallas_call x1, Pallas kernels, on_device(): pl.pallas_call(own_kernel, out_shape=total_shape, in_specs=[SMEM, VMEM, V...  3.15 us
    ppermute x4, starting transfers between devices, across(): return lax.ppermute(array, 'section', edges + [(j, i) for i, j in edges])  2.92 us
  transfers between devices with their start and end apart: 8, of which 2 were waited for; matrix products, arithmetic and copies ran while one was open for 1% of the time, Pallas kernels for 25%

profile of v5, /device:TPU:513, one launch (start us, length us, event | category | flops | bytes accessed | tf_op | source)
XLA Modules:
  0.0 71.8 jit_solution(14484493834398883274)
XLA Ops:
  0.6 2.7 %first.1 = (bf16[256,1536]{1,0:T(8,128)(2,1)S(1)}, bf16[256,1536]{1,0:T(8,128)(2,1)}, bf16[256,1536]{1,0:T(8,128)(2,1)}, bf16[512,768]{1,0:T(8,128)(2,1)S(1)}) custom-call(s32[1]{0:T(128)} %bitcast.place, s32[64]{0:T(128)} %order.7, bf16[256,1536]{1,0:T(8,128)(2,1)} %tokens.1, f32[3,1536]{1,0:T(4,128)} %mod.1, bf16[2,512,768]{2,1,0:T(8,128)(2,1)} %stale.1), custom_call_target="tpu_custom_call" | custom-call | flops 3932160 | bytes 3932160 | tf_op jit(solution)/shard_map/first/pallas_call | solution.py:423
  3.4 20.5 %collective-permute-start.2 = (bf16[256,1536]{1,0:T(8,128)(2,1)S(1)}, bf16[256,1536]{1,0:T(8,128)(2,1)}, u32[]{:S(2)}, u32[]{:S(2)}) collective-permute-start(bf16[256,1536]{1,0:T(8,128)(2,1)S(1)} %get-tuple-element.23.half.own_half), channel_id=1, source_target_pairs={{0,1},{1,0},{2,3},{3,2},{4,5},{5,4},{6,7},{7,6},{8,9},{9,8},{10,11... | collective-permute-start | bytes 2359304 | tf_op jit(solution)/shard_map/ppermute | solution.py:386
  23.9 0.7 collective-permute-start
  24.6 0.1 collective-permute-start.1
  25.4 0.9 %reshape.15.keep = s32[64,512]{1,0:T(8,128)S(1)} reshape(s32[32768]{0:T(1024)} %param.17) | data formatting | bytes 262144 | tf_op jit(solution)/shard_map/reshape | solution.py:416
  26.3 0.0 copy-start.3
  26.4 4.2 %own_rows.1 = (bf16[2,256,768]{2,1,0:T(8,128)(2,1)S(1)}, bf16[256,768]{1,0:T(8,128)(2,1)S(1)}, bf16[1536,768]{1,0:T(8,128)(2,1)S(1)}, bf16[1536,768]{1,0:T(8,128)(2,1)S(1)}) custom-call(bf16[256,1536]{1,0:T(8,128)(2,1)S(1)} %get-tuple-element.23.half.own_half, bf16[3,1536,768]{2,1,0:T(8,128)(2,1)} %weight.5, f32[3,128]{1,0:T(4,128)} %gains.7), custom_call_target="tpu_custom_call" | custom-call | flops 1207959552 | bytes 786432 | tf_op jit(solution)/shard_map/own_rows/pallas_call | solution.py:451
  30.6 0.0 collective-permute-done.2.half_in
  30.6 0.0 copy-done.3
  30.6 5.1 %other_rows.1 = (bf16[2,512,768]{2,1,0:T(8,128)(2,1)}, bf16[512,768]{1,0:T(8,128)(2,1)S(1)}, bf16[512,768]{1,0:T(8,128)(2,1)S(1)}, bf16[6,512,256]{2,1,0:T(8,128)(2,1)S(1)}) custom-call(s32[1]{0:T(128)} %bitcast.place, s32[1]{0:T(128)} %bitcast.1.side, bf16[256,1536]{1,0:T(8,128)(2,1)S(1)} %get-tuple-element.23.half.own_half, ...), custom_call_target="tpu_custom_call" | custom-call | flops 2415919104 | bytes 786432 | tf_op jit(solution)/shard_map/other_rows/pallas_call | solution.py:471
  35.7 0.0 copy-start.4
  35.7 3.2 %own.1.total_in = f32[512,1536]{1,0:T(8,128)S(1)} custom-call(s32[1]{0:T(128)S(6)} %copy.16.count, bf16[512,768]{1,0:T(8,128)(2,1)S(1)} %get-tuple-element.28.queries, bf16[512,768]{1,0:T(8,128)(2,1)S(1)} %get-tuple-element.29.keys, bf16[6,512,256]{2,1,0:T(8,128)(2,1)S(1)} %get-tuple-element.30.vbuf, bf16[2,256,768]{2,1,0:T(8,128)(2,1)} %text_in.1, ...), custom_call_target="tpu_custom_call" | custom-call | flops 1811939328 | bytes 2359296 | tf_op jit(solution)/shard_map/own/pallas_call | solution.py:504
  38.9 0.0 collective-permute-done.mine
  38.9 5.1 %collective-permute-done.1.mine = bf16[256,1536]{1,0:T(8,128)(2,1)S(1)} collective-permute-done((bf16[256,1536]{1,0:T(8,128)(2,1)}, bf16[256,1536]{1,0:T(8,128)(2,1)S(1)}, u32[]{:S(2)}, u32[]{:S(2)}) %collective-permute-start.1) | collective-permute-done | bytes 786464 | tf_op jit(solution)/shard_map/ppermute | solution.py:392
  44.0 0.9 %collective-permute-start.3 = (bf16[256,1536]{1,0:T(8,128)(2,1)S(1)}, bf16[256,1536]{1,0:T(8,128)(2,1)S(1)}, u32[]{:S(2)}, u32[]{:S(2)}) collective-permute-start(bf16[256,1536]{1,0:T(8,128)(2,1)S(1)} %collective-permute-done.mine), channel_id=1, source_target_pairs={{0,1},{1,0},{2,3},{3,2},{4,5},{5,4},{6,7},{7,6},{8,9},{9,8},{10,11... | collective-permute-start | bytes 2359304 | tf_op jit(solution)/shard_map/ppermute | solution.py:386
  44.9 0.0 collective-permute-start.4
  44.9 0.7 collective-permute-start.5
  45.6 1.4 %collective-permute-start.6 = (bf16[512,768]{1,0:T(8,128)(2,1)S(1)}, bf16[512,768]{1,0:T(8,128)(2,1)S(1)}, u32[]{:S(2)}, u32[]{:S(2)}) collective-permute-start(bf16[512,768]{1,0:T(8,128)(2,1)S(1)} %get-tuple-element.37), channel_id=1, source_target_pairs={{0,2},{4,6},{8,10},{12,14},{16,18},{20,22},{24,26},{28,30},{32,34}... | collective-permute-start | bytes 2359304 | tf_op jit(solution)/shard_map/ppermute | solution.py:392
  47.0 0.0 collective-permute-done.3.other
  47.0 1.1 %near_odd.1 = (f32[512,1536]{1,0:T(8,128)S(1)}, bf16[6,512,512]{2,1,0:T(8,128)(2,1)S(1)}) custom-call(s32[1]{0:T(128)} %bitcast.place, s32[1]{0:T(128)} %bitcast.1.side, s32[64]{0:T(128)S(1)} %copy-done.4, bf16[256,1536]{1,0:T(8,128)(2,1)S(1)} %collective-permute-done.mine, ...), custom_call_target="tpu_custom_call", output_to_operand_aliasing={{0}: (10, {})} | custom-call | flops 2415919104 | bytes 2359296 | tf_op jit(solution)/shard_map/near_odd/pallas_call | solution.py:525
  48.1 0.0 collective-permute-done.4.other
  48.2 0.0 copy-start
  48.2 2.3 %near_even.1 = (f32[512,1536]{1,0:T(8,128)S(1)}, bf16[6,512,512]{2,1,0:T(8,128)(2,1)S(1)}) custom-call(s32[1]{0:T(128)} %bitcast.place, s32[1]{0:T(128)} %bitcast.1.side, s32[64]{0:T(128)S(1)} %copy-done.4, bf16[256,1536]{1,0:T(8,128)(2,1)S(1)} %collective-permute-done.1.mine, ...), custom_call_target="tpu_custom_call", output_to_operand_aliasing={{0}: (10, {})} | custom-call | flops 2415919104 | bytes 2359296 | tf_op jit(solution)/shard_map/near_even/pallas_call | solution.py:525
  50.5 0.0 collective-permute-done.5.odd_values
  50.5 13.8 %collective-permute-done.6.even_values = bf16[512,768]{1,0:T(8,128)(2,1)S(1)} collective-permute-done((bf16[512,768]{1,0:T(8,128)(2,1)S(1)}, bf16[512,768]{1,0:T(8,128)(2,1)S(1)}, u32[]{:S(2)}, u32[]{:S(2)}) %collective-permute-start.6) | collective-permute-done | bytes 786464 | tf_op jit(solution)/shard_map/ppermute | solution.py:392
  64.3 2.5 %finish_sent.1 = bf16[256,1536]{1,0:T(8,128)(2,1)S(1)} custom-call(s32[1]{0:T(128)} %bitcast.place, s32[1]{0:T(128)} %bitcast.1.side, s32[64]{0:T(128)S(1)} %copy-done.4, bf16[6,512,512]{2,1,0:T(8,128)(2,1)S(1)} %get-tuple-element.33.odd_weights, bf16[6,512,512]{2,1,0:T(8,128)(2,1)S(1)} %get-tuple-element.36.even_weights, ...), custom_call_target="tpu_custom_call" | custom-call | flops 603979776 | bytes 1572864 | tf_op jit(solution)/shard_map/finish_sent/pallas_call | solution.py:556
  66.8 0.0 copy-start.1
  66.8 0.0 copy-start.2
  66.8 1.5 %collective-permute-start.7 = (bf16[256,1536]{1,0:T(8,128)(2,1)S(1)}, bf16[256,1536]{1,0:T(8,128)(2,1)S(1)}, u32[]{:S(2)}, u32[]{:S(2)}) collective-permute-start(bf16[256,1536]{1,0:T(8,128)(2,1)S(1)} %finish_sent.1), channel_id=1, source_target_pairs={{0,1},{1,0},{2,3},{3,2},{4,5},{5,4},{6,7},{7,6},{8,9},{9,8},{10,11... | collective-permute-start | bytes 2359304 | tf_op jit(solution)/shard_map/ppermute | solution.py:386
  68.3 2.3 %finish_kept.1.kept = bf16[256,1536]{1,0:T(8,128)(2,1)S(1)} custom-call(s32[1]{0:T(128)} %bitcast.place, s32[1]{0:T(128)} %bitcast.1.side, s32[64]{0:T(128)S(1)} %copy-done.4, bf16[6,512,512]{2,1,0:T(8,128)(2,1)S(1)} %get-tuple-element.33.odd_weights, bf16[6,512,512]{2,1,0:T(8,128)(2,1)S(1)} %get-tuple-element.36.even_weights, ...), custom_call_target="tpu_custom_call" | custom-call | flops 603979776 | bytes 1572864 | tf_op jit(solution)/shard_map/finish_kept/pallas_call | solution.py:556
  70.6 0.0 collective-permute-done.7.received
  70.6 1.2 %add.1 = bf16[256,1536]{1,0:T(8,128)(2,1)} custom-call(bf16[256,1536]{1,0:T(8,128)(2,1)S(1)} %copy-done.1, f32[3,1536]{1,0:T(4,128)S(1)} %copy-done.2, bf16[256,1536]{1,0:T(8,128)(2,1)S(1)} %finish_kept.1.kept, bf16[256,1536]{1,0:T(8,128)(2,1)S(1)} %collective-permute-done.7.received), custom_call_target="tpu_custom_call" | custom-call | flops 2359296 | bytes 3145728 | tf_op jit(solution)/shard_map/add/pallas_call | solution.py:585
  (4 shorter events, 0.0 us)
Async XLA Ops:
  3.4 27.2 %collective-permute-start.2 = (bf16[256,1536]{1,0:T(8,128)(2,1)S(1)}, bf16[256,1536]{1,0:T(8,128)(2,1)}, u32[]{:S(2)}, u32[]{:S(2)}) collective-permute-start(bf16[256,1536]{1,0:T(8,128)(2,1)S(1)} %get-tuple-element.23.half.own_half), channel_id=1, source_target_pairs={{0,1},{1,0},{2,3},{3,2},{4,5},{5,4},{6,7},{7,6},{8,9},{9,8},{10,11... | collective-permute-start | bytes 2359304 | tf_op jit(solution)/shard_map/ppermute | solution.py:386
  23.9 15.0 %collective-permute-start = (bf16[256,1536]{1,0:T(8,128)(2,1)}, bf16[256,1536]{1,0:T(8,128)(2,1)S(1)}, u32[]{:S(2)}, u32[]{:S(2)}) collective-permute-start(bf16[256,1536]{1,0:T(8,128)(2,1)} %get-tuple-element.21), channel_id=1, source_target_pairs={{2,4},{6,8},{10,12},{14,16},{18,20},{22,24},{26,28},{30,32},{34,36... | collective-permute-start | bytes 2359304 | tf_op jit(solution)/shard_map/ppermute | solution.py:392
  24.6 19.4 %collective-permute-start.1 = (bf16[256,1536]{1,0:T(8,128)(2,1)}, bf16[256,1536]{1,0:T(8,128)(2,1)S(1)}, u32[]{:S(2)}, u32[]{:S(2)}) collective-permute-start(bf16[256,1536]{1,0:T(8,128)(2,1)} %get-tuple-element.22), channel_id=1, source_target_pairs={{0,2},{4,6},{8,10},{12,14},{16,18},{20,22},{24,26},{28,30},{32,34}... | collective-permute-start | bytes 2359304 | tf_op jit(solution)/shard_map/ppermute | solution.py:392
  26.3 4.3 %copy-start.3 = (f32[3,128]{1,0:T(4,128)S(1)}, f32[3,128]{1,0:T(4,128)}, u32[]{:S(2)}) copy-start(f32[3,128]{1,0:T(4,128)} %gains.7) | copy-start | bytes 4612
  35.7 11.3 %copy-start.4 = (s32[64]{0:T(128)S(1)}, s32[64]{0:T(128)}, u32[]{:S(2)}) copy-start(s32[64]{0:T(128)} %order.7) | copy-start | bytes 772
  44.0 3.0 %collective-permute-start.3 = (bf16[256,1536]{1,0:T(8,128)(2,1)S(1)}, bf16[256,1536]{1,0:T(8,128)(2,1)S(1)}, u32[]{:S(2)}, u32[]{:S(2)}) collective-permute-start(bf16[256,1536]{1,0:T(8,128)(2,1)S(1)} %collective-permute-done.mine), channel_id=1, source_target_pairs={{0,1},{1,0},{2,3},{3,2},{4,5},{5,4},{6,7},{7,6},{8,9},{9,8},{10,11... | collective-permute-start | bytes 2359304 | tf_op jit(solution)/shard_map/ppermute | solution.py:386
  44.9 3.3 %collective-permute-start.4 = (bf16[256,1536]{1,0:T(8,128)(2,1)S(1)}, bf16[256,1536]{1,0:T(8,128)(2,1)S(1)}, u32[]{:S(2)}, u32[]{:S(2)}) collective-permute-start(bf16[256,1536]{1,0:T(8,128)(2,1)S(1)} %collective-permute-done.1.mine), channel_id=1, source_target_pairs={{0,1},{1,0},{2,3},{3,2},{4,5},{5,4},{6,7},{7,6},{8,9},{9,8},{10,11... | collective-permute-start | bytes 2359304 | tf_op jit(solution)/shard_map/ppermute | solution.py:386
  44.9 5.6 %collective-permute-start.5 = (bf16[512,768]{1,0:T(8,128)(2,1)S(1)}, bf16[512,768]{1,0:T(8,128)(2,1)S(1)}, u32[]{:S(2)}, u32[]{:S(2)}) collective-permute-start(bf16[512,768]{1,0:T(8,128)(2,1)S(1)} %get-tuple-element.37), channel_id=1, source_target_pairs={{2,4},{6,8},{10,12},{14,16},{18,20},{22,24},{26,28},{30,32},{34,36... | collective-permute-start | bytes 2359304 | tf_op jit(solution)/shard_map/ppermute | solution.py:392
  45.6 18.7 %collective-permute-start.6 = (bf16[512,768]{1,0:T(8,128)(2,1)S(1)}, bf16[512,768]{1,0:T(8,128)(2,1)S(1)}, u32[]{:S(2)}, u32[]{:S(2)}) collective-permute-start(bf16[512,768]{1,0:T(8,128)(2,1)S(1)} %get-tuple-element.37), channel_id=1, source_target_pairs={{0,2},{4,6},{8,10},{12,14},{16,18},{20,22},{24,26},{28,30},{32,34}... | collective-permute-start | bytes 2359304 | tf_op jit(solution)/shard_map/ppermute | solution.py:392
  48.2 16.2 %copy-start = (bf16[768,1536]{1,0:T(8,128)(2,1)S(1)}, bf16[768,1536]{1,0:T(8,128)(2,1)}, u32[]{:S(2)}) copy-start(bf16[768,1536]{1,0:T(8,128)(2,1)} %weight.7) | copy-start | bytes 7077892
  66.8 3.8 %copy-start.1 = (bf16[256,1536]{1,0:T(8,128)(2,1)S(1)}, bf16[256,1536]{1,0:T(8,128)(2,1)}, u32[]{:S(2)}) copy-start(bf16[256,1536]{1,0:T(8,128)(2,1)} %tokens.1) | copy-start | bytes 2359300
  66.8 3.8 %copy-start.2 = (f32[3,1536]{1,0:T(4,128)S(1)}, f32[3,1536]{1,0:T(4,128)}, u32[]{:S(2)}) copy-start(f32[3,1536]{1,0:T(4,128)} %mod.1) | copy-start | bytes 55300
  66.8 3.8 %collective-permute-start.7 = (bf16[256,1536]{1,0:T(8,128)(2,1)S(1)}, bf16[256,1536]{1,0:T(8,128)(2,1)S(1)}, u32[]{:S(2)}, u32[]{:S(2)}) collective-permute-start(bf16[256,1536]{1,0:T(8,128)(2,1)S(1)} %finish_sent.1), channel_id=1, source_target_pairs={{0,1},{1,0},{2,3},{3,2},{4,5},{5,4},{6,7},{7,6},{8,9},{9,8},{10,11... | collective-permute-start | bytes 2359304 | tf_op jit(solution)/shard_map/ppermute | solution.py:386

commit v6 on v5

--- a/solution.py
+++ b/solution.py
@@ -56,6 +56,15 @@
 
 def mask_columns(row, lanes):
     return jnp.broadcast_to(row, (lanes, row.shape[1])).T.astype(bf16)
+
+
+def patch_mask(keep, wanted, patch):
+    lanes = keep.shape[1]
+    count = patch // lanes
+    rows = (keep[pl.ds(wanted * count, count), :] > 0).astype(f32)
+    return jnp.concatenate(
+        [mask_columns(rows[r : r + 1, :], lanes) for r in range(count)], axis=0
+    )
 
 
 def first_kernel(
@@ -150,8 +159,6 @@
 def own_rows_kernel(
     half, weight, gains_in, cache, keys, key_weight, value_weight, gains, sems, gains_sem
 ):
-    load_gains = pltpu.make_async_copy(gains_in, gains, gains_sem)
-    load_gains.start()
     width = keys.shape[1]
     block = 2 * gains.shape[1]
     buffers = {2: value_weight, 1: key_weight}
@@ -163,10 +170,13 @@
         )
         copy.start()
         copies.append(copy)
-    load_gains.wait()
-    gain = gain_row(gains, 1)
+    load_gains = pltpu.make_async_copy(gains_in, gains, gains_sem)
+    load_gains.start()
     for n, (c, low, high) in enumerate(pieces):
         copies[n].wait()
+        if c == 1:
+            load_gains.wait()
+            gain = gain_row(gains, 1)
         for j in range(low, high, block):
             cols = slice(j, j + block)
             y = jnp.dot(half[...], buffers[c][:, cols], preferred_element_type=f32)
@@ -183,7 +193,6 @@
     load_half = pltpu.make_async_copy(half_in, half, sems.at[0])
     load_half.start()
     load_weight = pltpu.make_async_copy(weight.at[0], query_weight, sems.at[1])
-    load_weight.start()
     rows = half.shape[0]
     width = keys.shape[1]
     size = gains.shape[1]
@@ -196,8 +205,7 @@
         pltpu.make_async_copy(raw.at[1], cache.at[1, at, :], sems.at[3]),
         pltpu.make_async_copy(raw.at[0], cache.at[0, at, :], sems.at[4]),
     ]
-    stores[0].start()
-    mask = mask_columns((keep[pl.ds(place[0], 1), :] > 0).astype(f32), size)
+    mask = patch_mask(keep, place[0], keys.shape[0])
     for i in range(width // size):
         vbuf[i, :, size:] = mask
     keys[own_at, :] = own_keys[...]
@@ -207,6 +215,7 @@
         )
     gain = gain_row(gains, 1)
     load_half.wait()
+    load_weight.start()
     for j in range(0, width, block):
         cols = slice(j, j + block)
         y = jnp.dot(half[...], value_weight[:, cols], preferred_element_type=f32).astype(bf16)
@@ -220,8 +229,8 @@
         keys[at, cols] = heads_normed(y.astype(f32), gain)
     gain = gain_row(gains, 0) * (math.log2(math.e) * size**-0.5)
     load_weight.wait()
-    stores[1].start()
-    stores[2].start()
+    for store in stores:
+        store.start()
     for j in range(0, width, block):
         cols = slice(j, j + block)
         for source, rows_at in ((own_half, own_at), (half, at)):
@@ -250,10 +259,6 @@
         tbuf[i, :, :size] = text[1, :, cols] * mask
         tbuf[i, :, size:] = mask
         total[:, wide * i : wide * (i + 1)] += attend(queries[:, cols], text_keys[:, cols], tbuf[i])
-
-
-def side_mask(keep, wanted, size):
-    return mask_columns((keep[pl.ds(wanted, 1), :] > 0).astype(f32), size)
 
 
 def near_kernel(
@@ -288,7 +293,7 @@
 
     @pl.when(order[q] < own)
     def _():
-        mask = side_mask(keep, q, size)
+        mask = patch_mask(keep, q, vbuf.shape[1])
         for i in range(heads):
             vbuf[i, :, size:] = mask
         for half, at in ((mine, h), (other, 1 - h)):
@@ -357,7 +362,7 @@
 
         @pl.when(order[q] > own)
         def _():
-            mask = side_mask(keep, q, size)
+            mask = patch_mask(keep, q, vbuf.shape[1])
             for i in range(heads):
                 vbuf[i, :, size:] = mask
                 vbuf[i, :, :size] = values[:, i * size : (i + 1) * size] * mask
@@ -413,7 +418,7 @@
     heads = width // size
     patch = stale_cache.shape[1]
     text_rows = text_cache.shape[1]
-    keep = video_keep.reshape(sections, patch)
+    keep = video_keep.reshape(-1, size)
     half_shape = jax.ShapeDtypeStruct((rows, model), bf16)
     side_shape = jax.ShapeDtypeStruct((patch, width), bf16)
     part_shape = jax.ShapeDtypeStruct((rows, width), bf16)
@@ -442,8 +447,8 @@
 
     odd_own = across(to_odd, 1)
     even_own = across(to_even, 0)
+    even_values = across(values, 0)
     odd_values = across(values, 1)
-    even_values = across(values, 0)
     other = swapped(normed)
 
     weight_shape = jax.ShapeDtypeStruct((model, width), bf16)
@@ -501,6 +506,9 @@
         keep,
     )
 
+    odd_own, queries, keys = lax.optimization_barrier((odd_own, queries, keys))
+    odd_other = swapped(odd_own)
+
     total = pl.pallas_call(
         own_kernel,
         out_shape=total_shape,
@@ -517,8 +525,7 @@
         name="own",
     )(text_count, queries, keys, vbuf, in_hbm(text_cache), norm_gains)
 
-    odd_own, even_own, total = lax.optimization_barrier((odd_own, even_own, total))
-    odd_other = swapped(odd_own)
+    even_own, total = lax.optimization_barrier((even_own, total))
     even_other = swapped(even_own)
 
     def near(edge, mine, other, total):

time: 72.9 us -> 72.9 us (level)
  local copies, waits for them, and re-layouts: 0.96 us -> 0.04 us
    pallas_call x1, Pallas kernels: 5.09 us -> 6.33 us  [on_device(): pl.pallas_call(other_rows_kernel, out_shape=(jax.ShapeDtypeStruct((2, pat...]
    reshape x1 -> x0, local copies, waits for them, and re-layouts: 0.93 us -> none  [on_device(): keep = video_keep.reshape(sections, patch)]
  transfers between devices with their start and end apart: 8 -> 8, of which waited for: 2 -> 2; matrix products, arithmetic and copies ran while one was open for 1% -> 0% of each run, Pallas kernels for 25% -> 26%
where the time goes in v6:
time: 72.9 us; the launch traced here: 71.8 us
  starting transfers between devices  25.5 us (35%)
  Pallas kernels  25.2 us (35%)
  waiting for transfers between devices  19.6 us (27%)
  between operations  1.5 us (2%)
    ppermute x4, starting transfers between devices, swapped(): return lax.ppermute(array, 'head', [(0, 1), (1, 0)])  22.6 us
    ppermute x4, waiting for transfers between devices, across(): return lax.ppermute(array, 'section', edges + [(j, i) for i, j in edges])  19.6 us
    pallas_call x1, Pallas kernels, on_device(): pl.pallas_call(other_rows_kernel, out_shape=(jax.ShapeDtypeStruct((2, pat...  6.33 us
    pallas_call x2, Pallas kernels, finish(): pl.pallas_call(functools.partial(finish_kernel, sections, flip), out_shap...  4.74 us
    pallas_call x1, Pallas kernels, on_device(): pl.pallas_call(own_rows_kernel, out_shape=(jax.ShapeDtypeStruct((2, rows,...  3.54 us
    pallas_call x2, Pallas kernels, near(): pl.pallas_call(functools.partial(near_kernel, sections, edge), out_shape=...  3.49 us
    pallas_call x1, Pallas kernels, on_device(): pl.pallas_call(own_kernel, out_shape=total_shape, in_specs=[SMEM, VMEM, V...  3.15 us
    ppermute x4, starting transfers between devices, across(): return lax.ppermute(array, 'section', edges + [(j, i) for i, j in edges])  2.92 us
  transfers between devices with their start and end apart: 8, of which 2 were waited for; matrix products, arithmetic and copies ran while one was open for 0% of the time, Pallas kernels for 26%

profile of v6, /device:TPU:513, one launch (start us, length us, event | category | flops | bytes accessed | tf_op | source)
XLA Modules:
  0.0 71.8 jit_solution(2561366583463851936)
XLA Ops:
  0.6 2.7 %first.1 = (bf16[256,1536]{1,0:T(8,128)(2,1)S(1)}, bf16[256,1536]{1,0:T(8,128)(2,1)}, bf16[256,1536]{1,0:T(8,128)(2,1)}, bf16[512,768]{1,0:T(8,128)(2,1)S(1)}) custom-call(s32[1]{0:T(128)} %bitcast.place, s32[64]{0:T(128)} %order.7, bf16[256,1536]{1,0:T(8,128)(2,1)} %tokens.1, f32[3,1536]{1,0:T(4,128)} %mod.1, bf16[2,512,768]{2,1,0:T(8,128)(2,1)} %stale.1), custom_call_target="tpu_custom_call" | custom-call | flops 3932160 | bytes 3932160 | tf_op jit(solution)/shard_map/first/pallas_call | solution.py:428
  3.4 20.5 %collective-permute-start.1 = (bf16[256,1536]{1,0:T(8,128)(2,1)S(1)}, bf16[256,1536]{1,0:T(8,128)(2,1)}, u32[]{:S(2)}, u32[]{:S(2)}) collective-permute-start(bf16[256,1536]{1,0:T(8,128)(2,1)S(1)} %get-tuple-element.24.half.own_half), channel_id=1, source_target_pairs={{0,1},{1,0},{2,3},{3,2},{4,5},{5,4},{6,7},{7,6},{8,9},{9,8},{10,11... | collective-permute-start | bytes 2359304 | tf_op jit(solution)/shard_map/ppermute | solution.py:391
  23.9 0.7 collective-permute-start
  24.6 0.1 collective-permute-start.3
  24.8 0.0 copy-start.1
  24.8 0.0 copy-start.4
  24.8 3.5 %own_rows.1 = (bf16[2,256,768]{2,1,0:T(8,128)(2,1)S(1)}, bf16[256,768]{1,0:T(8,128)(2,1)S(1)}, bf16[1536,768]{1,0:T(8,128)(2,1)S(1)}, bf16[1536,768]{1,0:T(8,128)(2,1)S(1)}) custom-call(bf16[256,1536]{1,0:T(8,128)(2,1)S(1)} %get-tuple-element.24.half.own_half, bf16[3,1536,768]{2,1,0:T(8,128)(2,1)} %weight.5, f32[3,128]{1,0:T(4,128)} %gains.7), custom_call_target="tpu_custom_call" | custom-call | flops 1207959552 | bytes 786432 | tf_op jit(solution)/shard_map/own_rows/pallas_call | solution.py:456
  28.3 0.0 collective-permute-done.1.half_in
  28.3 0.0 copy-done.1
  28.4 6.3 %other_rows.1 = (bf16[2,512,768]{2,1,0:T(8,128)(2,1)}, bf16[512,768]{1,0:T(8,128)(2,1)S(1)}, bf16[512,768]{1,0:T(8,128)(2,1)S(1)}, bf16[6,512,256]{2,1,0:T(8,128)(2,1)S(1)}) custom-call(s32[1]{0:T(128)} %bitcast.place, s32[1]{0:T(128)} %bitcast.1.side, bf16[256,1536]{1,0:T(8,128)(2,1)S(1)} %get-tuple-element.24.half.own_half, ...), custom_call_target="tpu_custom_call" | custom-call | flops 2415919104 | bytes 786432 | tf_op jit(solution)/shard_map/other_rows/pallas_call | solution.py:476
  34.7 0.0 collective-permute-done.mine
  34.7 0.2 collective-permute-start.2
  35.5 0.0 copy-start.5
  35.5 3.2 %own.1.total_in = f32[512,1536]{1,0:T(8,128)S(1)} custom-call(s32[1]{0:T(128)S(6)} %copy.16.count, bf16[512,768]{1,0:T(8,128)(2,1)S(1)} %get-tuple-element.32.queries, bf16[512,768]{1,0:T(8,128)(2,1)S(1)} %get-tuple-element.34.keys, bf16[6,512,256]{2,1,0:T(8,128)(2,1)S(1)} %get-tuple-element.35.vbuf, bf16[2,256,768]{2,1,0:T(8,128)(2,1)} %text_in.1, ...), custom_call_target="tpu_custom_call" | custom-call | flops 1811939328 | bytes 2359296 | tf_op jit(solution)/shard_map/own/pallas_call | solution.py:512
  38.7 5.3 %collective-permute-done.3.mine = bf16[256,1536]{1,0:T(8,128)(2,1)S(1)} collective-permute-done((bf16[256,1536]{1,0:T(8,128)(2,1)}, bf16[256,1536]{1,0:T(8,128)(2,1)S(1)}, u32[]{:S(2)}, u32[]{:S(2)}) %collective-permute-start.3) | collective-permute-done | bytes 786464 | tf_op jit(solution)/shard_map/ppermute | solution.py:397
  44.0 0.9 %collective-permute-start.4 = (bf16[256,1536]{1,0:T(8,128)(2,1)S(1)}, bf16[256,1536]{1,0:T(8,128)(2,1)S(1)}, u32[]{:S(2)}, u32[]{:S(2)}) collective-permute-start(bf16[256,1536]{1,0:T(8,128)(2,1)S(1)} %collective-permute-done.3.mine), channel_id=1, source_target_pairs={{0,1},{1,0},{2,3},{3,2},{4,5},{5,4},{6,7},{7,6},{8,9},{9,8},{10,11... | collective-permute-start | bytes 2359304 | tf_op jit(solution)/shard_map/ppermute | solution.py:391
  44.9 0.7 collective-permute-start.5
  45.6 1.4 %collective-permute-start.6 = (bf16[512,768]{1,0:T(8,128)(2,1)S(1)}, bf16[512,768]{1,0:T(8,128)(2,1)S(1)}, u32[]{:S(2)}, u32[]{:S(2)}) collective-permute-start(bf16[512,768]{1,0:T(8,128)(2,1)S(1)} %get-tuple-element.41), channel_id=1, source_target_pairs={{0,2},{4,6},{8,10},{12,14},{16,18},{20,22},{24,26},{28,30},{32,34}... | collective-permute-start | bytes 2359304 | tf_op jit(solution)/shard_map/ppermute | solution.py:397
  47.0 0.0 collective-permute-done.2.other
  47.0 1.1 %near_odd.1 = (f32[512,1536]{1,0:T(8,128)S(1)}, bf16[6,512,512]{2,1,0:T(8,128)(2,1)S(1)}) custom-call(s32[1]{0:T(128)} %bitcast.place, s32[1]{0:T(128)} %bitcast.1.side, s32[64]{0:T(128)S(1)} %copy-done.5, bf16[256,1536]{1,0:T(8,128)(2,1)S(1)} %collective-permute-done.mine, ...), custom_call_target="tpu_custom_call", output_to_operand_aliasing={{0}: (10, {})} | custom-call | flops 2415919104 | bytes 2359296 | tf_op jit(solution)/shard_map/near_odd/pallas_call | solution.py:532
  48.1 0.0 collective-permute-done.4.other
  48.1 0.0 copy-start
  48.2 2.3 %near_even.1 = (f32[512,1536]{1,0:T(8,128)S(1)}, bf16[6,512,512]{2,1,0:T(8,128)(2,1)S(1)}) custom-call(s32[1]{0:T(128)} %bitcast.place, s32[1]{0:T(128)} %bitcast.1.side, s32[64]{0:T(128)S(1)} %copy-done.5, bf16[256,1536]{1,0:T(8,128)(2,1)S(1)} %collective-permute-done.3.mine, ...), custom_call_target="tpu_custom_call", output_to_operand_aliasing={{0}: (10, {})} | custom-call | flops 2415919104 | bytes 2359296 | tf_op jit(solution)/shard_map/near_even/pallas_call | solution.py:532
  50.5 0.0 collective-permute-done.5.odd_values
  50.5 14.3 %collective-permute-done.6.even_values = bf16[512,768]{1,0:T(8,128)(2,1)S(1)} collective-permute-done((bf16[512,768]{1,0:T(8,128)(2,1)S(1)}, bf16[512,768]{1,0:T(8,128)(2,1)S(1)}, u32[]{:S(2)}, u32[]{:S(2)}) %collective-permute-start.6) | collective-permute-done | bytes 786464 | tf_op jit(solution)/shard_map/ppermute | solution.py:397
  64.8 2.5 %finish_sent.1 = bf16[256,1536]{1,0:T(8,128)(2,1)S(1)} custom-call(s32[1]{0:T(128)} %bitcast.place, s32[1]{0:T(128)} %bitcast.1.side, s32[64]{0:T(128)S(1)} %copy-done.5, bf16[6,512,512]{2,1,0:T(8,128)(2,1)S(1)} %get-tuple-element.37.odd_weights, bf16[6,512,512]{2,1,0:T(8,128)(2,1)S(1)} %get-tuple-element.40.even_weights, ...), custom_call_target="tpu_custom_call" | custom-call | flops 603979776 | bytes 1572864 | tf_op jit(solution)/shard_map/finish_sent/pallas_call | solution.py:563
  67.3 0.0 copy-start.2
  67.3 0.0 copy-start.3
  67.3 1.0 %collective-permute-start.7 = (bf16[256,1536]{1,0:T(8,128)(2,1)S(1)}, bf16[256,1536]{1,0:T(8,128)(2,1)S(1)}, u32[]{:S(2)}, u32[]{:S(2)}) collective-permute-start(bf16[256,1536]{1,0:T(8,128)(2,1)S(1)} %finish_sent.1), channel_id=1, source_target_pairs={{0,1},{1,0},{2,3},{3,2},{4,5},{5,4},{6,7},{7,6},{8,9},{9,8},{10,11... | collective-permute-start | bytes 2359304 | tf_op jit(solution)/shard_map/ppermute | solution.py:391
  68.3 2.3 %finish_kept.1.kept = bf16[256,1536]{1,0:T(8,128)(2,1)S(1)} custom-call(s32[1]{0:T(128)} %bitcast.place, s32[1]{0:T(128)} %bitcast.1.side, s32[64]{0:T(128)S(1)} %copy-done.5, bf16[6,512,512]{2,1,0:T(8,128)(2,1)S(1)} %get-tuple-element.37.odd_weights, bf16[6,512,512]{2,1,0:T(8,128)(2,1)S(1)} %get-tuple-element.40.even_weights, ...), custom_call_target="tpu_custom_call" | custom-call | flops 603979776 | bytes 1572864 | tf_op jit(solution)/shard_map/finish_kept/pallas_call | solution.py:563
  70.6 0.0 collective-permute-done.7.received
  70.6 1.2 %add.1 = bf16[256,1536]{1,0:T(8,128)(2,1)} custom-call(bf16[256,1536]{1,0:T(8,128)(2,1)S(1)} %copy-done.2, f32[3,1536]{1,0:T(4,128)S(1)} %copy-done.3, bf16[256,1536]{1,0:T(8,128)(2,1)S(1)} %finish_kept.1.kept, bf16[256,1536]{1,0:T(8,128)(2,1)S(1)} %collective-permute-done.7.received), custom_call_target="tpu_custom_call" | custom-call | flops 2359296 | bytes 3145728 | tf_op jit(solution)/shard_map/add/pallas_call | solution.py:592
  (5 shorter events, 0.0 us)
Async XLA Ops:
  3.4 25.0 %collective-permute-start.1 = (bf16[256,1536]{1,0:T(8,128)(2,1)S(1)}, bf16[256,1536]{1,0:T(8,128)(2,1)}, u32[]{:S(2)}, u32[]{:S(2)}) collective-permute-start(bf16[256,1536]{1,0:T(8,128)(2,1)S(1)} %get-tuple-element.24.half.own_half), channel_id=1, source_target_pairs={{0,1},{1,0},{2,3},{3,2},{4,5},{5,4},{6,7},{7,6},{8,9},{9,8},{10,11... | collective-permute-start | bytes 2359304 | tf_op jit(solution)/shard_map/ppermute | solution.py:391
  23.9 10.8 %collective-permute-start = (bf16[256,1536]{1,0:T(8,128)(2,1)}, bf16[256,1536]{1,0:T(8,128)(2,1)S(1)}, u32[]{:S(2)}, u32[]{:S(2)}) collective-permute-start(bf16[256,1536]{1,0:T(8,128)(2,1)} %get-tuple-element.23), channel_id=1, source_target_pairs={{2,4},{6,8},{10,12},{14,16},{18,20},{22,24},{26,28},{30,32},{34,36... | collective-permute-start | bytes 2359304 | tf_op jit(solution)/shard_map/ppermute | solution.py:397
  24.6 19.4 %collective-permute-start.3 = (bf16[256,1536]{1,0:T(8,128)(2,1)}, bf16[256,1536]{1,0:T(8,128)(2,1)S(1)}, u32[]{:S(2)}, u32[]{:S(2)}) collective-permute-start(bf16[256,1536]{1,0:T(8,128)(2,1)} %get-tuple-element.33), channel_id=1, source_target_pairs={{0,2},{4,6},{8,10},{12,14},{16,18},{20,22},{24,26},{28,30},{32,34}... | collective-permute-start | bytes 2359304 | tf_op jit(solution)/shard_map/ppermute | solution.py:397
  24.8 3.6 %copy-start.1 = (s32[32768]{0:T(1024)S(1)}, s32[32768]{0:T(1024)}, u32[]{:S(2)}) copy-start(s32[32768]{0:T(1024)} %param.17) | copy-start | bytes 393220
  24.8 3.6 %copy-start.4 = (f32[3,128]{1,0:T(4,128)S(1)}, f32[3,128]{1,0:T(4,128)}, u32[]{:S(2)}) copy-start(f32[3,128]{1,0:T(4,128)} %gains.7) | copy-start | bytes 4612
  34.7 12.3 %collective-permute-start.2 = (bf16[256,1536]{1,0:T(8,128)(2,1)S(1)}, bf16[256,1536]{1,0:T(8,128)(2,1)S(1)}, u32[]{:S(2)}, u32[]{:S(2)}) collective-permute-start(bf16[256,1536]{1,0:T(8,128)(2,1)S(1)} %collective-permute-done.mine), channel_id=1, source_target_pairs={{0,1},{1,0},{2,3},{3,2},{4,5},{5,4},{6,7},{7,6},{8,9},{9,8},{10,11... | collective-permute-start | bytes 2359304 | tf_op jit(solution)/shard_map/ppermute | solution.py:391
  35.5 11.5 %copy-start.5 = (s32[64]{0:T(128)S(1)}, s32[64]{0:T(128)}, u32[]{:S(2)}) copy-start(s32[64]{0:T(128)} %order.7) | copy-start | bytes 772
  44.0 4.1 %collective-permute-start.4 = (bf16[256,1536]{1,0:T(8,128)(2,1)S(1)}, bf16[256,1536]{1,0:T(8,128)(2,1)S(1)}, u32[]{:S(2)}, u32[]{:S(2)}) collective-permute-start(bf16[256,1536]{1,0:T(8,128)(2,1)S(1)} %collective-permute-done.3.mine), channel_id=1, source_target_pairs={{0,1},{1,0},{2,3},{3,2},{4,5},{5,4},{6,7},{7,6},{8,9},{9,8},{10,11... | collective-permute-start | bytes 2359304 | tf_op jit(solution)/shard_map/ppermute | solution.py:391
  44.9 5.6 %collective-permute-start.5 = (bf16[512,768]{1,0:T(8,128)(2,1)S(1)}, bf16[512,768]{1,0:T(8,128)(2,1)S(1)}, u32[]{:S(2)}, u32[]{:S(2)}) collective-permute-start(bf16[512,768]{1,0:T(8,128)(2,1)S(1)} %get-tuple-element.41), channel_id=1, source_target_pairs={{2,4},{6,8},{10,12},{14,16},{18,20},{22,24},{26,28},{30,32},{34,36... | collective-permute-start | bytes 2359304 | tf_op jit(solution)/shard_map/ppermute | solution.py:397
  45.6 19.2 %collective-permute-start.6 = (bf16[512,768]{1,0:T(8,128)(2,1)S(1)}, bf16[512,768]{1,0:T(8,128)(2,1)S(1)}, u32[]{:S(2)}, u32[]{:S(2)}) collective-permute-start(bf16[512,768]{1,0:T(8,128)(2,1)S(1)} %get-tuple-element.41), channel_id=1, source_target_pairs={{0,2},{4,6},{8,10},{12,14},{16,18},{20,22},{24,26},{28,30},{32,34}... | collective-permute-start | bytes 2359304 | tf_op jit(solution)/shard_map/ppermute | solution.py:397
  48.1 16.7 %copy-start = (bf16[768,1536]{1,0:T(8,128)(2,1)S(1)}, bf16[768,1536]{1,0:T(8,128)(2,1)}, u32[]{:S(2)}) copy-start(bf16[768,1536]{1,0:T(8,128)(2,1)} %weight.7) | copy-start | bytes 7077892
  67.3 3.3 %copy-start.2 = (bf16[256,1536]{1,0:T(8,128)(2,1)S(1)}, bf16[256,1536]{1,0:T(8,128)(2,1)}, u32[]{:S(2)}) copy-start(bf16[256,1536]{1,0:T(8,128)(2,1)} %tokens.1) | copy-start | bytes 2359300
  67.3 3.3 %copy-start.3 = (f32[3,1536]{1,0:T(4,128)S(1)}, f32[3,1536]{1,0:T(4,128)}, u32[]{:S(2)}) copy-start(f32[3,1536]{1,0:T(4,128)} %mod.1) | copy-start | bytes 55300
  67.3 3.3 %collective-permute-start.7 = (bf16[256,1536]{1,0:T(8,128)(2,1)S(1)}, bf16[256,1536]{1,0:T(8,128)(2,1)S(1)}, u32[]{:S(2)}, u32[]{:S(2)}) collective-permute-start(bf16[256,1536]{1,0:T(8,128)(2,1)S(1)} %finish_sent.1), channel_id=1, source_target_pairs={{0,1},{1,0},{2,3},{3,2},{4,5},{5,4},{6,7},{7,6},{8,9},{9,8},{10,11... | collective-permute-start | bytes 2359304 | tf_op jit(solution)/shard_map/ppermute | solution.py:391

commit v7 on v6

--- a/solution.py
+++ b/solution.py
@@ -65,6 +65,18 @@
     return jnp.concatenate(
         [mask_columns(rows[r : r + 1, :], lanes) for r in range(count)], axis=0
     )
+
+
+def row_copies(source, target, sems, base, pieces):
+    step = source.shape[0] // pieces
+    return [
+        pltpu.make_async_copy(
+            source.at[i * step : (i + 1) * step],
+            target.at[i * step : (i + 1) * step],
+            sems.at[base + i],
+        )
+        for i in range(pieces)
+    ]
 
 
 def first_kernel(
@@ -162,37 +174,39 @@
     width = keys.shape[1]
     block = 2 * gains.shape[1]
     buffers = {2: value_weight, 1: key_weight}
-    pieces = ((2, 0, block), (2, block, width), (1, 0, width))
-    copies = []
-    for n, (c, low, high) in enumerate(pieces):
-        copy = pltpu.make_async_copy(
+    pieces = [(c, low, low + block) for c in (2, 1) for low in range(0, width, block)]
+    copies = [
+        pltpu.make_async_copy(
             weight.at[c, :, low:high], buffers[c].at[:, low:high], sems.at[n]
         )
+        for n, (c, low, high) in enumerate(pieces)
+    ]
+    for copy in copies:
         copy.start()
-        copies.append(copy)
     load_gains = pltpu.make_async_copy(gains_in, gains, gains_sem)
     load_gains.start()
+    waits = {0: copies[:1], 1: copies[1 : width // block], width // block: copies[width // block :]}
     for n, (c, low, high) in enumerate(pieces):
-        copies[n].wait()
-        if c == 1:
+        for copy in waits.get(n, ()):
+            copy.wait()
+        if n == width // block:
             load_gains.wait()
             gain = gain_row(gains, 1)
-        for j in range(low, high, block):
-            cols = slice(j, j + block)
-            y = jnp.dot(half[...], buffers[c][:, cols], preferred_element_type=f32)
-            y = y.astype(bf16)
-            cache[c - 1, :, cols] = y
-            if c == 1:
-                keys[:, cols] = heads_normed(y.astype(f32), gain)
+        cols = slice(low, high)
+        y = jnp.dot(half[...], buffers[c][:, cols], preferred_element_type=f32).astype(bf16)
+        cache[c - 1, :, cols] = y
+        if c == 1:
+            keys[:, cols] = heads_normed(y.astype(f32), gain)
 
 
 def other_rows_kernel(
     place, side, own_half, half_in, own_cache, own_keys, key_weight, value_weight, weight, gains,
     keep, cache, queries, keys, vbuf, half, raw, query_weight, sems,
 ):
-    load_half = pltpu.make_async_copy(half_in, half, sems.at[0])
-    load_half.start()
-    load_weight = pltpu.make_async_copy(weight.at[0], query_weight, sems.at[1])
+    load_half = row_copies(half_in, half, sems, 0, 2)
+    load_weight = row_copies(weight.at[0], query_weight, sems, 2, 6)
+    for copy in load_half + load_weight:
+        copy.start()
     rows = half.shape[0]
     width = keys.shape[1]
     size = gains.shape[1]
@@ -201,9 +215,10 @@
     at = pl.ds(pl.multiple_of((1 - h) * rows, rows), rows)
     own_at = pl.ds(pl.multiple_of(h * rows, rows), rows)
     stores = [
-        pltpu.make_async_copy(own_cache, cache.at[:, own_at, :], sems.at[2]),
-        pltpu.make_async_copy(raw.at[1], cache.at[1, at, :], sems.at[3]),
-        pltpu.make_async_copy(raw.at[0], cache.at[0, at, :], sems.at[4]),
+        pltpu.make_async_copy(own_cache.at[0], cache.at[0, own_at, :], sems.at[8]),
+        pltpu.make_async_copy(own_cache.at[1], cache.at[1, own_at, :], sems.at[9]),
+        pltpu.make_async_copy(raw.at[0], cache.at[0, at, :], sems.at[10]),
+        pltpu.make_async_copy(raw.at[1], cache.at[1, at, :], sems.at[11]),
     ]
     mask = patch_mask(keep, place[0], keys.shape[0])
     for i in range(width // size):
@@ -214,8 +229,8 @@
             own_cache[1, :, i * size : (i + 1) * size] * vbuf[0, own_at, size:]
         )
     gain = gain_row(gains, 1)
-    load_half.wait()
-    load_weight.start()
+    for copy in load_half:
+        copy.wait()
     for j in range(0, width, block):
         cols = slice(j, j + block)
         y = jnp.dot(half[...], value_weight[:, cols], preferred_element_type=f32).astype(bf16)
@@ -228,7 +243,8 @@
         raw[0, :, cols] = y
         keys[at, cols] = heads_normed(y.astype(f32), gain)
     gain = gain_row(gains, 0) * (math.log2(math.e) * size**-0.5)
-    load_weight.wait()
+    for copy in load_weight:
+        copy.wait()
     for store in stores:
         store.start()
     for j in range(0, width, block):
@@ -267,7 +283,7 @@
     place,
     side,
     order,
-    mine,
+    mine_in,
     other,
     key_weight,
     value_weight,
@@ -279,7 +295,15 @@
     weights,
     keys,
     vbuf,
+    *buffers,
 ):
+    loads = []
+    mine = mine_in
+    if buffers:
+        mine, sems = buffers
+        loads = row_copies(mine_in, mine, sems, 0, 2)
+    for copy in loads:
+        copy.start()
     rows = mine.shape[0]
     patch, width = queries.shape
     size = gains.shape[1]
@@ -289,14 +313,23 @@
     own = order[place[0]]
     q = partners(place, sections)[edge]
     gain = gain_row(gains, 1)
-    total[...] = total_in[...]
-
-    @pl.when(order[q] < own)
+    fresh = order[q] < own
+
+    @pl.when(jnp.logical_not(fresh))
+    def _():
+        total[...] = total_in[...]
+        for copy in loads:
+            copy.wait()
+
+    @pl.when(fresh)
     def _():
         mask = patch_mask(keep, q, vbuf.shape[1])
         for i in range(heads):
             vbuf[i, :, size:] = mask
-        for half, at in ((mine, h), (other, 1 - h)):
+        for half, at in ((other, 1 - h), (mine, h)):
+            if half is mine:
+                for copy in loads:
+                    copy.wait()
             at = pl.ds(pl.multiple_of(at * rows, rows), rows)
             for j in range(0, width, block):
                 cols = slice(j, j + block)
@@ -313,7 +346,7 @@
         for i in range(heads):
             cols = slice(i * size, (i + 1) * size)
             wide = slice(2 * i * size, 2 * (i + 1) * size)
-            total[:, wide] += attend(queries[:, cols], keys[:, cols], vbuf[i])
+            total[:, wide] = total_in[:, wide] + attend(queries[:, cols], keys[:, cols], vbuf[i])
 
     @pl.when(order[q] > own)
     def _():
@@ -378,13 +411,17 @@
     out[...] = jnp.dot(att[...], weight[...], preferred_element_type=f32).astype(bf16)
 
 
-def add_kernel(tokens, mod, kept, received, out):
+def add_kernel(tokens, mod, kept, received, out, held, sems):
     gate = mod[2:3, :]
-    step = 64
-    for r in range(0, tokens.shape[0], step):
-        at = slice(r, r + step)
+    copies = row_copies(held, out, sems, 0, 4)
+    step = held.shape[0] // len(copies)
+    for n, copy in enumerate(copies):
+        at = slice(n * step, (n + 1) * step)
         mixed = kept[at, :].astype(f32) + received[at, :].astype(f32)
-        out[at, :] = (tokens[at, :].astype(f32) + gate * mixed).astype(bf16)
+        held[at, :] = (tokens[at, :].astype(f32) + gate * mixed).astype(bf16)
+        copy.start()
+    for copy in copies:
+        copy.wait()
 
 
 def swapped(array):
@@ -465,7 +502,7 @@
         out_specs=(VMEM,) * 4,
         scratch_shapes=[
             pltpu.VMEM(norm_gains.shape, f32),
-            pltpu.SemaphoreType.DMA((3,)),
+            pltpu.SemaphoreType.DMA((width // size,)),
             pltpu.SemaphoreType.DMA,
         ],
         compiler_params=params(10),
@@ -487,7 +524,7 @@
             pltpu.VMEM((rows, model), bf16),
             pltpu.VMEM((2, rows, width), bf16),
             pltpu.VMEM((model, width), bf16),
-            pltpu.SemaphoreType.DMA((5,)),
+            pltpu.SemaphoreType.DMA((12,)),
         ],
         compiler_params=params(16),
         cost_estimate=cost(8 * rows * model * width, 4 * rows * width),
@@ -529,15 +566,20 @@
     even_other = swapped(even_own)
 
     def near(edge, mine, other, total):
+        buffers = []
+        if edge == 0:
+            mine = in_hbm(mine)
+            buffers = [pltpu.VMEM((rows, model), bf16), pltpu.SemaphoreType.DMA((2,))]
         return pl.pallas_call(
             functools.partial(near_kernel, sections, edge),
             out_shape=(total_shape, jax.ShapeDtypeStruct((heads, patch, patch), bf16)),
-            in_specs=[SMEM] * 3 + [VMEM] * 8,
+            in_specs=[SMEM] * 3 + [VMEM if edge else HBM] + [VMEM] * 7,
             out_specs=(VMEM, VMEM),
             scratch_shapes=[
                 pltpu.VMEM((patch, width), bf16),
                 pltpu.VMEM((heads, patch, 2 * size), bf16),
-            ],
+            ]
+            + buffers,
             input_output_aliases={10: 0},
             compiler_params=params(16),
             cost_estimate=cost(4 * patch * model * width, 6 * patch * width),
@@ -593,7 +635,8 @@
         add_kernel,
         out_shape=half_shape,
         in_specs=[VMEM] * 4,
-        out_specs=VMEM,
+        out_specs=HBM,
+        scratch_shapes=[pltpu.VMEM((rows, model), bf16), pltpu.SemaphoreType.DMA((4,))],
         compiler_params=params(8),
         cost_estimate=cost(6 * rows * model, 8 * rows * model),
         name="add",

time: 72.9 us -> 73.1 us (level)
  Pallas kernels: 25.2 us -> 24 us
    pallas_call x1, Pallas kernels: 6.33 us -> 5.11 us  [on_device(): pl.pallas_call(other_rows_kernel, out_shape=(jax.ShapeDtypeStruct((2, pat...]
  transfers between devices with their start and end apart: 8 -> 8, of which waited for: 2 -> 2; matrix products, arithmetic and copies ran while one was open for 0% -> 0% of each run, Pallas kernels for 26% -> 25%
where the time goes in v7:
time: 73.1 us; the launch traced here: 72 us
  starting transfers between devices  26.2 us (36%)
  Pallas kernels  24 us (33%)
  waiting for transfers between devices  20.1 us (27%)
  between operations  1.65 us (2%)
    ppermute x4, starting transfers between devices, swapped(): return lax.ppermute(array, 'head', [(0, 1), (1, 0)])  22.6 us
    ppermute x4, waiting for transfers between devices, across(): return lax.ppermute(array, 'section', edges + [(j, i) for i, j in edges])  20.1 us
    pallas_call x1, Pallas kernels, on_device(): pl.pallas_call(other_rows_kernel, out_shape=(jax.ShapeDtypeStruct((2, pat...  5.11 us
    pallas_call x2, Pallas kernels, finish(): pl.pallas_call(functools.partial(finish_kernel, sections, flip), out_shap...  4.74 us
    pallas_call x2, Pallas kernels, near(): pl.pallas_call(functools.partial(near_kernel, sections, edge), out_shape=...  4.03 us
    ppermute x4, starting transfers between devices, across(): return lax.ppermute(array, 'section', edges + [(j, i) for i, j in edges])  3.62 us
    pallas_call x1, Pallas kernels, on_device(): pl.pallas_call(own_rows_kernel, out_shape=(jax.ShapeDtypeStruct((2, rows,...  3.55 us
    pallas_call x1, Pallas kernels, on_device(): pl.pallas_call(own_kernel, out_shape=total_shape, in_specs=[SMEM, VMEM, V...  3.15 us
  transfers between devices with their start and end apart: 8, of which 2 were waited for; matrix products, arithmetic and copies ran while one was open for 0% of the time, Pallas kernels for 25%

profile of v7, /device:TPU:513, one launch (start us, length us, event | category | flops | bytes accessed | tf_op | source)
XLA Modules:
  0.0 72.0 jit_solution(9861277190801312294)
XLA Ops:
  0.6 2.4 %first.1 = (bf16[256,1536]{1,0:T(8,128)(2,1)S(1)}, bf16[256,1536]{1,0:T(8,128)(2,1)}, bf16[256,1536]{1,0:T(8,128)(2,1)S(1)}, bf16[512,768]{1,0:T(8,128)(2,1)S(1)}) custom-call(s32[1]{0:T(128)} %bitcast.place, s32[64]{0:T(128)} %order.7, bf16[256,1536]{1,0:T(8,128)(2,1)} %tokens.1, f32[3,1536]{1,0:T(4,128)} %mod.1, bf16[2,512,768]{2,1,0:T(8,128)(2,1)} %stale.1), custom_call_target="tpu_custom_call" | custom-call | flops 3932160 | bytes 3932160 | tf_op jit(solution)/shard_map/first/pallas_call | solution.py:465
  3.0 20.5 %collective-permute-start.1 = (bf16[256,1536]{1,0:T(8,128)(2,1)S(1)}, bf16[256,1536]{1,0:T(8,128)(2,1)}, u32[]{:S(2)}, u32[]{:S(2)}) collective-permute-start(bf16[256,1536]{1,0:T(8,128)(2,1)S(1)} %get-tuple-element.24.half.own_half), channel_id=1, source_target_pairs={{0,1},{1,0},{2,3},{3,2},{4,5},{5,4},{6,7},{7,6},{8,9},{9,8},{10,11... | collective-permute-start | bytes 2359304 | tf_op jit(solution)/shard_map/ppermute | solution.py:428
  23.6 1.6 %collective-permute-start = (bf16[256,1536]{1,0:T(8,128)(2,1)}, bf16[256,1536]{1,0:T(8,128)(2,1)}, u32[]{:S(2)}, u32[]{:S(2)}) collective-permute-start(bf16[256,1536]{1,0:T(8,128)(2,1)} %get-tuple-element.23), channel_id=1, source_target_pairs={{2,4},{6,8},{10,12},{14,16},{18,20},{22,24},{26,28},{30,32},{34,36... | collective-permute-start | bytes 2359304 | tf_op jit(solution)/shard_map/ppermute | solution.py:434
  25.1 0.0 collective-permute-start.3
  25.1 3.5 %own_rows.1 = (bf16[2,256,768]{2,1,0:T(8,128)(2,1)S(1)}, bf16[256,768]{1,0:T(8,128)(2,1)S(1)}, bf16[1536,768]{1,0:T(8,128)(2,1)S(1)}, bf16[1536,768]{1,0:T(8,128)(2,1)S(1)}) custom-call(bf16[256,1536]{1,0:T(8,128)(2,1)S(1)} %get-tuple-element.24.half.own_half, bf16[3,1536,768]{2,1,0:T(8,128)(2,1)} %weight.5, f32[3,128]{1,0:T(4,128)} %gains.7), custom_call_target="tpu_custom_call" | custom-call | flops 1207959552 | bytes 786432 | tf_op jit(solution)/shard_map/own_rows/pallas_call | solution.py:493
  28.7 0.0 collective-permute-done.1.half_in
  28.7 0.0 copy-done.1
  28.7 0.0 copy-done.4
  28.7 5.1 %other_rows.1 = (bf16[2,512,768]{2,1,0:T(8,128)(2,1)}, bf16[512,768]{1,0:T(8,128)(2,1)S(1)}, bf16[512,768]{1,0:T(8,128)(2,1)S(1)}, bf16[6,512,256]{2,1,0:T(8,128)(2,1)S(1)}) custom-call(s32[1]{0:T(128)} %bitcast.place, s32[1]{0:T(128)} %bitcast.1.side, bf16[256,1536]{1,0:T(8,128)(2,1)S(1)} %get-tuple-element.24.half.own_half, ...), custom_call_target="tpu_custom_call" | custom-call | flops 2415919104 | bytes 786432 | tf_op jit(solution)/shard_map/other_rows/pallas_call | solution.py:513
  33.8 0.0 collective-permute-done.mine_in
  33.8 0.2 collective-permute-start.2
  34.7 0.0 copy-start.5
  34.7 3.2 %own.1.total_in = f32[512,1536]{1,0:T(8,128)S(1)} custom-call(s32[1]{0:T(128)S(6)} %copy.16.count, bf16[512,768]{1,0:T(8,128)(2,1)S(1)} %get-tuple-element.32.queries, bf16[512,768]{1,0:T(8,128)(2,1)S(1)} %get-tuple-element.34.keys, bf16[6,512,256]{2,1,0:T(8,128)(2,1)S(1)} %get-tuple-element.35.vbuf, bf16[2,256,768]{2,1,0:T(8,128)(2,1)} %text_in.1, ...), custom_call_target="tpu_custom_call" | custom-call | flops 1811939328 | bytes 2359296 | tf_op jit(solution)/shard_map/own/pallas_call | solution.py:549
  37.8 6.3 %collective-permute-done.3.mine_in = bf16[256,1536]{1,0:T(8,128)(2,1)S(1)} collective-permute-done((bf16[256,1536]{1,0:T(8,128)(2,1)S(1)}, bf16[256,1536]{1,0:T(8,128)(2,1)S(1)}, u32[]{:S(2)}, u32[]{:S(2)}) %collective-permute-start.3) | collective-permute-done | bytes 786464 | tf_op jit(solution)/shard_map/ppermute | solution.py:434
  44.2 0.9 %collective-permute-start.4 = (bf16[256,1536]{1,0:T(8,128)(2,1)S(1)}, bf16[256,1536]{1,0:T(8,128)(2,1)S(1)}, u32[]{:S(2)}, u32[]{:S(2)}) collective-permute-start(bf16[256,1536]{1,0:T(8,128)(2,1)S(1)} %collective-permute-done.3.mine_in), channel_id=1, source_target_pairs={{0,1},{1,0},{2,3},{3,2},{4,5},{5,4},{6,7},{7,6},{8,9},{9,8},{10,11... | collective-permute-start | bytes 2359304 | tf_op jit(solution)/shard_map/ppermute | solution.py:428
  45.1 0.7 collective-permute-start.5
  45.8 1.4 %collective-permute-start.6 = (bf16[512,768]{1,0:T(8,128)(2,1)S(1)}, bf16[512,768]{1,0:T(8,128)(2,1)S(1)}, u32[]{:S(2)}, u32[]{:S(2)}) collective-permute-start(bf16[512,768]{1,0:T(8,128)(2,1)S(1)} %get-tuple-element.41), channel_id=1, source_target_pairs={{0,2},{4,6},{8,10},{12,14},{16,18},{20,22},{24,26},{28,30},{32,34}... | collective-permute-start | bytes 2359304 | tf_op jit(solution)/shard_map/ppermute | solution.py:434
  47.2 0.0 collective-permute-done.2.other
  47.2 1.7 %near_odd.1 = (f32[512,1536]{1,0:T(8,128)S(1)}, bf16[6,512,512]{2,1,0:T(8,128)(2,1)S(1)}) custom-call(s32[1]{0:T(128)} %bitcast.place, s32[1]{0:T(128)} %bitcast.1.side, s32[64]{0:T(128)S(1)} %copy-done.5, bf16[256,1536]{1,0:T(8,128)(2,1)} %collective-permute-done.mine_in, ...), custom_call_target="tpu_custom_call", output_to_operand_aliasing={{0}: (10, {})} | custom-call | flops 2415919104 | bytes 2359296 | tf_op jit(solution)/shard_map/near_odd/pallas_call | solution.py:573
  48.8 0.0 collective-permute-done.4.other
  48.8 0.0 copy-start
  48.9 2.4 %near_even.1 = (f32[512,1536]{1,0:T(8,128)S(1)}, bf16[6,512,512]{2,1,0:T(8,128)(2,1)S(1)}) custom-call(s32[1]{0:T(128)} %bitcast.place, s32[1]{0:T(128)} %bitcast.1.side, s32[64]{0:T(128)S(1)} %copy-done.5, bf16[256,1536]{1,0:T(8,128)(2,1)S(1)} %collective-permute-done.3.mine_in, ...), custom_call_target="tpu_custom_call", output_to_operand_aliasing={{0}: (10, {})} | custom-call | flops 2415919104 | bytes 2359296 | tf_op jit(solution)/shard_map/near_even/pallas_call | solution.py:573
  51.2 0.0 collective-permute-done.5.odd_values
  51.2 13.8 %collective-permute-done.6.even_values = bf16[512,768]{1,0:T(8,128)(2,1)S(1)} collective-permute-done((bf16[512,768]{1,0:T(8,128)(2,1)S(1)}, bf16[512,768]{1,0:T(8,128)(2,1)S(1)}, u32[]{:S(2)}, u32[]{:S(2)}) %collective-permute-start.6) | collective-permute-done | bytes 786464 | tf_op jit(solution)/shard_map/ppermute | solution.py:434
  65.0 2.5 %finish_sent.1 = bf16[256,1536]{1,0:T(8,128)(2,1)S(1)} custom-call(s32[1]{0:T(128)} %bitcast.place, s32[1]{0:T(128)} %bitcast.1.side, s32[64]{0:T(128)S(1)} %copy-done.5, bf16[6,512,512]{2,1,0:T(8,128)(2,1)S(1)} %get-tuple-element.37.odd_weights, bf16[6,512,512]{2,1,0:T(8,128)(2,1)S(1)} %get-tuple-element.40.even_weights, ...), custom_call_target="tpu_custom_call" | custom-call | flops 603979776 | bytes 1572864 | tf_op jit(solution)/shard_map/finish_sent/pallas_call | solution.py:605
  67.5 0.0 copy-start.2
  67.5 0.0 copy-start.3
  67.5 1.0 %collective-permute-start.7 = (bf16[256,1536]{1,0:T(8,128)(2,1)S(1)}, bf16[256,1536]{1,0:T(8,128)(2,1)S(1)}, u32[]{:S(2)}, u32[]{:S(2)}) collective-permute-start(bf16[256,1536]{1,0:T(8,128)(2,1)S(1)} %finish_sent.1), channel_id=1, source_target_pairs={{0,1},{1,0},{2,3},{3,2},{4,5},{5,4},{6,7},{7,6},{8,9},{9,8},{10,11... | collective-permute-start | bytes 2359304 | tf_op jit(solution)/shard_map/ppermute | solution.py:428
  68.5 2.3 %finish_kept.1.kept = bf16[256,1536]{1,0:T(8,128)(2,1)S(1)} custom-call(s32[1]{0:T(128)} %bitcast.place, s32[1]{0:T(128)} %bitcast.1.side, s32[64]{0:T(128)S(1)} %copy-done.5, bf16[6,512,512]{2,1,0:T(8,128)(2,1)S(1)} %get-tuple-element.37.odd_weights, bf16[6,512,512]{2,1,0:T(8,128)(2,1)S(1)} %get-tuple-element.40.even_weights, ...), custom_call_target="tpu_custom_call" | custom-call | flops 603979776 | bytes 1572864 | tf_op jit(solution)/shard_map/finish_kept/pallas_call | solution.py:605
  70.8 0.0 collective-permute-done.7.received
  70.8 0.0 copy-done.2
  70.8 1.1 %add.1 = bf16[256,1536]{1,0:T(8,128)(2,1)} custom-call(bf16[256,1536]{1,0:T(8,128)(2,1)S(1)} %copy-done.2, f32[3,1536]{1,0:T(4,128)S(1)} %copy-done.3, bf16[256,1536]{1,0:T(8,128)(2,1)S(1)} %finish_kept.1.kept, bf16[256,1536]{1,0:T(8,128)(2,1)S(1)} %collective-permute-done.7.received), custom_call_target="tpu_custom_call" | custom-call | flops 2359296 | bytes 3145728 | tf_op jit(solution)/shard_map/add/pallas_call | solution.py:634
  (5 shorter events, 0.0 us)
Async XLA Ops:
  3.0 25.6 %collective-permute-start.1 = (bf16[256,1536]{1,0:T(8,128)(2,1)S(1)}, bf16[256,1536]{1,0:T(8,128)(2,1)}, u32[]{:S(2)}, u32[]{:S(2)}) collective-permute-start(bf16[256,1536]{1,0:T(8,128)(2,1)S(1)} %get-tuple-element.24.half.own_half), channel_id=1, source_target_pairs={{0,1},{1,0},{2,3},{3,2},{4,5},{5,4},{6,7},{7,6},{8,9},{9,8},{10,11... | collective-permute-start | bytes 2359304 | tf_op jit(solution)/shard_map/ppermute | solution.py:428
  23.6 10.3 %collective-permute-start = (bf16[256,1536]{1,0:T(8,128)(2,1)}, bf16[256,1536]{1,0:T(8,128)(2,1)}, u32[]{:S(2)}, u32[]{:S(2)}) collective-permute-start(bf16[256,1536]{1,0:T(8,128)(2,1)} %get-tuple-element.23), channel_id=1, source_target_pairs={{2,4},{6,8},{10,12},{14,16},{18,20},{22,24},{26,28},{30,32},{34,36... | collective-permute-start | bytes 2359304 | tf_op jit(solution)/shard_map/ppermute | solution.py:434
  25.1 19.1 %collective-permute-start.3 = (bf16[256,1536]{1,0:T(8,128)(2,1)S(1)}, bf16[256,1536]{1,0:T(8,128)(2,1)S(1)}, u32[]{:S(2)}, u32[]{:S(2)}) collective-permute-start(bf16[256,1536]{1,0:T(8,128)(2,1)S(1)} %get-tuple-element.33), channel_id=1, source_target_pairs={{0,2},{4,6},{8,10},{12,14},{16,18},{20,22},{24,26},{28,30},{32,34}... | collective-permute-start | bytes 2359304 | tf_op jit(solution)/shard_map/ppermute | solution.py:434
  25.1 3.6 %copy-start.1 = (s32[32768]{0:T(1024)S(1)}, s32[32768]{0:T(1024)}, u32[]{:S(2)}) copy-start(s32[32768]{0:T(1024)} %param.17) | copy-start | bytes 393220
  25.1 3.6 %copy-start.4 = (f32[3,128]{1,0:T(4,128)S(1)}, f32[3,128]{1,0:T(4,128)}, u32[]{:S(2)}) copy-start(f32[3,128]{1,0:T(4,128)} %gains.7) | copy-start | bytes 4612
  33.8 13.3 %collective-permute-start.2 = (bf16[256,1536]{1,0:T(8,128)(2,1)}, bf16[256,1536]{1,0:T(8,128)(2,1)S(1)}, u32[]{:S(2)}, u32[]{:S(2)}) collective-permute-start(bf16[256,1536]{1,0:T(8,128)(2,1)} %collective-permute-done.mine_in), channel_id=1, source_target_pairs={{0,1},{1,0},{2,3},{3,2},{4,5},{5,4},{6,7},{7,6},{8,9},{9,8},{10,11... | collective-permute-start | bytes 2359304 | tf_op jit(solution)/shard_map/ppermute | solution.py:428
  34.7 12.5 %copy-start.5 = (s32[64]{0:T(128)S(1)}, s32[64]{0:T(128)}, u32[]{:S(2)}) copy-start(s32[64]{0:T(128)} %order.7) | copy-start | bytes 772
  44.2 4.7 %collective-permute-start.4 = (bf16[256,1536]{1,0:T(8,128)(2,1)S(1)}, bf16[256,1536]{1,0:T(8,128)(2,1)S(1)}, u32[]{:S(2)}, u32[]{:S(2)}) collective-permute-start(bf16[256,1536]{1,0:T(8,128)(2,1)S(1)} %collective-permute-done.3.mine_in), channel_id=1, source_target_pairs={{0,1},{1,0},{2,3},{3,2},{4,5},{5,4},{6,7},{7,6},{8,9},{9,8},{10,11... | collective-permute-start | bytes 2359304 | tf_op jit(solution)/shard_map/ppermute | solution.py:428
  45.1 6.1 %collective-permute-start.5 = (bf16[512,768]{1,0:T(8,128)(2,1)S(1)}, bf16[512,768]{1,0:T(8,128)(2,1)S(1)}, u32[]{:S(2)}, u32[]{:S(2)}) collective-permute-start(bf16[512,768]{1,0:T(8,128)(2,1)S(1)} %get-tuple-element.41), channel_id=1, source_target_pairs={{2,4},{6,8},{10,12},{14,16},{18,20},{22,24},{26,28},{30,32},{34,36... | collective-permute-start | bytes 2359304 | tf_op jit(solution)/shard_map/ppermute | solution.py:434
  45.8 19.2 %collective-permute-start.6 = (bf16[512,768]{1,0:T(8,128)(2,1)S(1)}, bf16[512,768]{1,0:T(8,128)(2,1)S(1)}, u32[]{:S(2)}, u32[]{:S(2)}) collective-permute-start(bf16[512,768]{1,0:T(8,128)(2,1)S(1)} %get-tuple-element.41), channel_id=1, source_target_pairs={{0,2},{4,6},{8,10},{12,14},{16,18},{20,22},{24,26},{28,30},{32,34}... | collective-permute-start | bytes 2359304 | tf_op jit(solution)/shard_map/ppermute | solution.py:434
  48.8 16.2 %copy-start = (bf16[768,1536]{1,0:T(8,128)(2,1)S(1)}, bf16[768,1536]{1,0:T(8,128)(2,1)}, u32[]{:S(2)}) copy-start(bf16[768,1536]{1,0:T(8,128)(2,1)} %weight.7) | copy-start | bytes 7077892
  67.5 3.3 %copy-start.2 = (bf16[256,1536]{1,0:T(8,128)(2,1)S(1)}, bf16[256,1536]{1,0:T(8,128)(2,1)}, u32[]{:S(2)}) copy-start(bf16[256,1536]{1,0:T(8,128)(2,1)} %tokens.1) | copy-start | bytes 2359300
  67.5 3.3 %copy-start.3 = (f32[3,1536]{1,0:T(4,128)S(1)}, f32[3,1536]{1,0:T(4,128)}, u32[]{:S(2)}) copy-start(f32[3,1536]{1,0:T(4,128)} %mod.1) | copy-start | bytes 55300
  67.5 3.3 %collective-permute-start.7 = (bf16[256,1536]{1,0:T(8,128)(2,1)S(1)}, bf16[256,1536]{1,0:T(8,128)(2,1)S(1)}, u32[]{:S(2)}, u32[]{:S(2)}) collective-permute-start(bf16[256,1536]{1,0:T(8,128)(2,1)S(1)} %finish_sent.1), channel_id=1, source_target_pairs={{0,1},{1,0},{2,3},{3,2},{4,5},{5,4},{6,7},{7,6},{8,9},{9,8},{10,11... | collective-permute-start | bytes 2359304 | tf_op jit(solution)/shard_map/ppermute | solution.py:428

commit v8 on v7

--- a/solution.py
+++ b/solution.py
@@ -231,6 +231,8 @@
     gain = gain_row(gains, 1)
     for copy in load_half:
         copy.wait()
+    stores[0].start()
+    stores[1].start()
     for j in range(0, width, block):
         cols = slice(j, j + block)
         y = jnp.dot(half[...], value_weight[:, cols], preferred_element_type=f32).astype(bf16)
@@ -243,10 +245,10 @@
         raw[0, :, cols] = y
         keys[at, cols] = heads_normed(y.astype(f32), gain)
     gain = gain_row(gains, 0) * (math.log2(math.e) * size**-0.5)
+    stores[2].start()
+    stores[3].start()
     for copy in load_weight:
         copy.wait()
-    for store in stores:
-        store.start()
     for j in range(0, width, block):
         cols = slice(j, j + block)
         for source, rows_at in ((own_half, own_at), (half, at)):

time: 73.1 us -> 73.1 us (level)
  Pallas kernels: 24 us -> 23.2 us
  waiting for transfers between devices: 20.1 us -> 20.9 us
    pallas_call x1, Pallas kernels: 5.11 us -> 4.34 us  [on_device(): pl.pallas_call(other_rows_kernel, out_shape=(jax.ShapeDtypeStruct((2, pat...]
    ppermute x4, waiting for transfers between devices: 20.1 us -> 20.9 us  [across(): return lax.ppermute(array, 'section', edges + [(j, i) for i, j in edges])]
  transfers between devices with their start and end apart: 8 -> 8, of which waited for: 2 -> 2; matrix products, arithmetic and copies ran while one was open for 0% -> 0% of each run, Pallas kernels for 25% -> 24%
where the time goes in v8:
time: 73.1 us; the launch traced here: 72 us
  starting transfers between devices  26.2 us (36%)
  Pallas kernels  23.2 us (32%)
  waiting for transfers between devices  20.9 us (29%)
  between operations  1.65 us (2%)
    ppermute x4, starting transfers between devices, swapped(): return lax.ppermute(array, 'head', [(0, 1), (1, 0)])  22.6 us
    ppermute x4, waiting for transfers between devices, across(): return lax.ppermute(array, 'section', edges + [(j, i) for i, j in edges])  20.9 us
    pallas_call x2, Pallas kernels, finish(): pl.pallas_call(functools.partial(finish_kernel, sections, flip), out_shap...  4.74 us
    pallas_call x1, Pallas kernels, on_device(): pl.pallas_call(other_rows_kernel, out_shape=(jax.ShapeDtypeStruct((2, pat...  4.34 us
    pallas_call x2, Pallas kernels, near(): pl.pallas_call(functools.partial(near_kernel, sections, edge), out_shape=...  4.03 us
    ppermute x4, starting transfers between devices, across(): return lax.ppermute(array, 'section', edges + [(j, i) for i, j in edges])  3.62 us
    pallas_call x1, Pallas kernels, on_device(): pl.pallas_call(own_rows_kernel, out_shape=(jax.ShapeDtypeStruct((2, rows,...  3.55 us
    pallas_call x1, Pallas kernels, on_device(): pl.pallas_call(own_kernel, out_shape=total_shape, in_specs=[SMEM, VMEM, V...  3.15 us
  transfers between devices with their start and end apart: 8, of which 2 were waited for; matrix products, arithmetic and copies ran while one was open for 0% of the time, Pallas kernels for 24%

profile of v8, /device:TPU:513, one launch (start us, length us, event | category | flops | bytes accessed | tf_op | source)
XLA Modules:
  0.0 72.0 jit_solution(10457584196445061851)
XLA Ops:
  0.6 2.4 %first.1 = (bf16[256,1536]{1,0:T(8,128)(2,1)S(1)}, bf16[256,1536]{1,0:T(8,128)(2,1)}, bf16[256,1536]{1,0:T(8,128)(2,1)S(1)}, bf16[512,768]{1,0:T(8,128)(2,1)S(1)}) custom-call(s32[1]{0:T(128)} %bitcast.place, s32[64]{0:T(128)} %order.7, bf16[256,1536]{1,0:T(8,128)(2,1)} %tokens.1, f32[3,1536]{1,0:T(4,128)} %mod.1, bf16[2,512,768]{2,1,0:T(8,128)(2,1)} %stale.1), custom_call_target="tpu_custom_call" | custom-call | flops 3932160 | bytes 3932160 | tf_op jit(solution)/shard_map/first/pallas_call | solution.py:467
  3.0 20.5 %collective-permute-start.1 = (bf16[256,1536]{1,0:T(8,128)(2,1)S(1)}, bf16[256,1536]{1,0:T(8,128)(2,1)}, u32[]{:S(2)}, u32[]{:S(2)}) collective-permute-start(bf16[256,1536]{1,0:T(8,128)(2,1)S(1)} %get-tuple-element.24.half.own_half), channel_id=1, source_target_pairs={{0,1},{1,0},{2,3},{3,2},{4,5},{5,4},{6,7},{7,6},{8,9},{9,8},{10,11... | collective-permute-start | bytes 2359304 | tf_op jit(solution)/shard_map/ppermute | solution.py:430
  23.6 1.6 %collective-permute-start = (bf16[256,1536]{1,0:T(8,128)(2,1)}, bf16[256,1536]{1,0:T(8,128)(2,1)}, u32[]{:S(2)}, u32[]{:S(2)}) collective-permute-start(bf16[256,1536]{1,0:T(8,128)(2,1)} %get-tuple-element.23), channel_id=1, source_target_pairs={{2,4},{6,8},{10,12},{14,16},{18,20},{22,24},{26,28},{30,32},{34,36... | collective-permute-start | bytes 2359304 | tf_op jit(solution)/shard_map/ppermute | solution.py:436
  25.1 0.0 collective-permute-start.3
  25.1 3.5 %own_rows.1 = (bf16[2,256,768]{2,1,0:T(8,128)(2,1)S(1)}, bf16[256,768]{1,0:T(8,128)(2,1)S(1)}, bf16[1536,768]{1,0:T(8,128)(2,1)S(1)}, bf16[1536,768]{1,0:T(8,128)(2,1)S(1)}) custom-call(bf16[256,1536]{1,0:T(8,128)(2,1)S(1)} %get-tuple-element.24.half.own_half, bf16[3,1536,768]{2,1,0:T(8,128)(2,1)} %weight.5, f32[3,128]{1,0:T(4,128)} %gains.7), custom_call_target="tpu_custom_call" | custom-call | flops 1207959552 | bytes 786432 | tf_op jit(solution)/shard_map/own_rows/pallas_call | solution.py:495
  28.7 0.0 collective-permute-done.1.half_in
  28.7 0.0 copy-done.1
  28.7 0.0 copy-done.4
  28.7 4.3 %other_rows.1 = (bf16[2,512,768]{2,1,0:T(8,128)(2,1)}, bf16[512,768]{1,0:T(8,128)(2,1)S(1)}, bf16[512,768]{1,0:T(8,128)(2,1)S(1)}, bf16[6,512,256]{2,1,0:T(8,128)(2,1)S(1)}) custom-call(s32[1]{0:T(128)} %bitcast.place, s32[1]{0:T(128)} %bitcast.1.side, bf16[256,1536]{1,0:T(8,128)(2,1)S(1)} %get-tuple-element.24.half.own_half, ...), custom_call_target="tpu_custom_call" | custom-call | flops 2415919104 | bytes 786432 | tf_op jit(solution)/shard_map/other_rows/pallas_call | solution.py:515
  33.1 0.0 collective-permute-done.mine_in
  33.1 0.2 collective-permute-start.2
  33.9 0.0 copy-start.5
  33.9 3.2 %own.1.total_in = f32[512,1536]{1,0:T(8,128)S(1)} custom-call(s32[1]{0:T(128)S(6)} %copy.16.count, bf16[512,768]{1,0:T(8,128)(2,1)S(1)} %get-tuple-element.32.queries, bf16[512,768]{1,0:T(8,128)(2,1)S(1)} %get-tuple-element.34.keys, bf16[6,512,256]{2,1,0:T(8,128)(2,1)S(1)} %get-tuple-element.35.vbuf, bf16[2,256,768]{2,1,0:T(8,128)(2,1)} %text_in.1, ...), custom_call_target="tpu_custom_call" | custom-call | flops 1811939328 | bytes 2359296 | tf_op jit(solution)/shard_map/own/pallas_call | solution.py:551
  37.1 7.1 %collective-permute-done.3.mine_in = bf16[256,1536]{1,0:T(8,128)(2,1)S(1)} collective-permute-done((bf16[256,1536]{1,0:T(8,128)(2,1)S(1)}, bf16[256,1536]{1,0:T(8,128)(2,1)S(1)}, u32[]{:S(2)}, u32[]{:S(2)}) %collective-permute-start.3) | collective-permute-done | bytes 786464 | tf_op jit(solution)/shard_map/ppermute | solution.py:436
  44.2 0.9 %collective-permute-start.4 = (bf16[256,1536]{1,0:T(8,128)(2,1)S(1)}, bf16[256,1536]{1,0:T(8,128)(2,1)S(1)}, u32[]{:S(2)}, u32[]{:S(2)}) collective-permute-start(bf16[256,1536]{1,0:T(8,128)(2,1)S(1)} %collective-permute-done.3.mine_in), channel_id=1, source_target_pairs={{0,1},{1,0},{2,3},{3,2},{4,5},{5,4},{6,7},{7,6},{8,9},{9,8},{10,11... | collective-permute-start | bytes 2359304 | tf_op jit(solution)/shard_map/ppermute | solution.py:430
  45.1 0.7 collective-permute-start.5
  45.8 1.4 %collective-permute-start.6 = (bf16[512,768]{1,0:T(8,128)(2,1)S(1)}, bf16[512,768]{1,0:T(8,128)(2,1)S(1)}, u32[]{:S(2)}, u32[]{:S(2)}) collective-permute-start(bf16[512,768]{1,0:T(8,128)(2,1)S(1)} %get-tuple-element.41), channel_id=1, source_target_pairs={{0,2},{4,6},{8,10},{12,14},{16,18},{20,22},{24,26},{28,30},{32,34}... | collective-permute-start | bytes 2359304 | tf_op jit(solution)/shard_map/ppermute | solution.py:436
  47.2 0.0 collective-permute-done.2.other
  47.2 1.7 %near_odd.1 = (f32[512,1536]{1,0:T(8,128)S(1)}, bf16[6,512,512]{2,1,0:T(8,128)(2,1)S(1)}) custom-call(s32[1]{0:T(128)} %bitcast.place, s32[1]{0:T(128)} %bitcast.1.side, s32[64]{0:T(128)S(1)} %copy-done.5, bf16[256,1536]{1,0:T(8,128)(2,1)} %collective-permute-done.mine_in, ...), custom_call_target="tpu_custom_call", output_to_operand_aliasing={{0}: (10, {})} | custom-call | flops 2415919104 | bytes 2359296 | tf_op jit(solution)/shard_map/near_odd/pallas_call | solution.py:575
  48.8 0.0 collective-permute-done.4.other
  48.8 0.0 copy-start
  48.9 2.4 %near_even.1 = (f32[512,1536]{1,0:T(8,128)S(1)}, bf16[6,512,512]{2,1,0:T(8,128)(2,1)S(1)}) custom-call(s32[1]{0:T(128)} %bitcast.place, s32[1]{0:T(128)} %bitcast.1.side, s32[64]{0:T(128)S(1)} %copy-done.5, bf16[256,1536]{1,0:T(8,128)(2,1)S(1)} %collective-permute-done.3.mine_in, ...), custom_call_target="tpu_custom_call", output_to_operand_aliasing={{0}: (10, {})} | custom-call | flops 2415919104 | bytes 2359296 | tf_op jit(solution)/shard_map/near_even/pallas_call | solution.py:575
  51.2 0.0 collective-permute-done.5.odd_values
  51.2 13.8 %collective-permute-done.6.even_values = bf16[512,768]{1,0:T(8,128)(2,1)S(1)} collective-permute-done((bf16[512,768]{1,0:T(8,128)(2,1)S(1)}, bf16[512,768]{1,0:T(8,128)(2,1)S(1)}, u32[]{:S(2)}, u32[]{:S(2)}) %collective-permute-start.6) | collective-permute-done | bytes 786464 | tf_op jit(solution)/shard_map/ppermute | solution.py:436
  65.0 2.5 %finish_sent.1 = bf16[256,1536]{1,0:T(8,128)(2,1)S(1)} custom-call(s32[1]{0:T(128)} %bitcast.place, s32[1]{0:T(128)} %bitcast.1.side, s32[64]{0:T(128)S(1)} %copy-done.5, bf16[6,512,512]{2,1,0:T(8,128)(2,1)S(1)} %get-tuple-element.37.odd_weights, bf16[6,512,512]{2,1,0:T(8,128)(2,1)S(1)} %get-tuple-element.40.even_weights, ...), custom_call_target="tpu_custom_call" | custom-call | flops 603979776 | bytes 1572864 | tf_op jit(solution)/shard_map/finish_sent/pallas_call | solution.py:607
  67.5 0.0 copy-start.2
  67.5 0.0 copy-start.3
  67.5 1.0 %collective-permute-start.7 = (bf16[256,1536]{1,0:T(8,128)(2,1)S(1)}, bf16[256,1536]{1,0:T(8,128)(2,1)S(1)}, u32[]{:S(2)}, u32[]{:S(2)}) collective-permute-start(bf16[256,1536]{1,0:T(8,128)(2,1)S(1)} %finish_sent.1), channel_id=1, source_target_pairs={{0,1},{1,0},{2,3},{3,2},{4,5},{5,4},{6,7},{7,6},{8,9},{9,8},{10,11... | collective-permute-start | bytes 2359304 | tf_op jit(solution)/shard_map/ppermute | solution.py:430
  68.5 2.3 %finish_kept.1.kept = bf16[256,1536]{1,0:T(8,128)(2,1)S(1)} custom-call(s32[1]{0:T(128)} %bitcast.place, s32[1]{0:T(128)} %bitcast.1.side, s32[64]{0:T(128)S(1)} %copy-done.5, bf16[6,512,512]{2,1,0:T(8,128)(2,1)S(1)} %get-tuple-element.37.odd_weights, bf16[6,512,512]{2,1,0:T(8,128)(2,1)S(1)} %get-tuple-element.40.even_weights, ...), custom_call_target="tpu_custom_call" | custom-call | flops 603979776 | bytes 1572864 | tf_op jit(solution)/shard_map/finish_kept/pallas_call | solution.py:607
  70.8 0.0 collective-permute-done.7.received
  70.8 0.0 copy-done.2
  70.8 1.1 %add.1 = bf16[256,1536]{1,0:T(8,128)(2,1)} custom-call(bf16[256,1536]{1,0:T(8,128)(2,1)S(1)} %copy-done.2, f32[3,1536]{1,0:T(4,128)S(1)} %copy-done.3, bf16[256,1536]{1,0:T(8,128)(2,1)S(1)} %finish_kept.1.kept, bf16[256,1536]{1,0:T(8,128)(2,1)S(1)} %collective-permute-done.7.received), custom_call_target="tpu_custom_call" | custom-call | flops 2359296 | bytes 3145728 | tf_op jit(solution)/shard_map/add/pallas_call | solution.py:636
  (5 shorter events, 0.0 us)
Async XLA Ops:
  3.0 25.6 %collective-permute-start.1 = (bf16[256,1536]{1,0:T(8,128)(2,1)S(1)}, bf16[256,1536]{1,0:T(8,128)(2,1)}, u32[]{:S(2)}, u32[]{:S(2)}) collective-permute-start(bf16[256,1536]{1,0:T(8,128)(2,1)S(1)} %get-tuple-element.24.half.own_half), channel_id=1, source_target_pairs={{0,1},{1,0},{2,3},{3,2},{4,5},{5,4},{6,7},{7,6},{8,9},{9,8},{10,11... | collective-permute-start | bytes 2359304 | tf_op jit(solution)/shard_map/ppermute | solution.py:430
  23.6 9.5 %collective-permute-start = (bf16[256,1536]{1,0:T(8,128)(2,1)}, bf16[256,1536]{1,0:T(8,128)(2,1)}, u32[]{:S(2)}, u32[]{:S(2)}) collective-permute-start(bf16[256,1536]{1,0:T(8,128)(2,1)} %get-tuple-element.23), channel_id=1, source_target_pairs={{2,4},{6,8},{10,12},{14,16},{18,20},{22,24},{26,28},{30,32},{34,36... | collective-permute-start | bytes 2359304 | tf_op jit(solution)/shard_map/ppermute | solution.py:436
  25.1 19.1 %collective-permute-start.3 = (bf16[256,1536]{1,0:T(8,128)(2,1)S(1)}, bf16[256,1536]{1,0:T(8,128)(2,1)S(1)}, u32[]{:S(2)}, u32[]{:S(2)}) collective-permute-start(bf16[256,1536]{1,0:T(8,128)(2,1)S(1)} %get-tuple-element.33), channel_id=1, source_target_pairs={{0,2},{4,6},{8,10},{12,14},{16,18},{20,22},{24,26},{28,30},{32,34}... | collective-permute-start | bytes 2359304 | tf_op jit(solution)/shard_map/ppermute | solution.py:436
  25.1 3.6 %copy-start.1 = (s32[32768]{0:T(1024)S(1)}, s32[32768]{0:T(1024)}, u32[]{:S(2)}) copy-start(s32[32768]{0:T(1024)} %param.17) | copy-start | bytes 393220
  25.1 3.6 %copy-start.4 = (f32[3,128]{1,0:T(4,128)S(1)}, f32[3,128]{1,0:T(4,128)}, u32[]{:S(2)}) copy-start(f32[3,128]{1,0:T(4,128)} %gains.7) | copy-start | bytes 4612
  33.1 14.1 %collective-permute-start.2 = (bf16[256,1536]{1,0:T(8,128)(2,1)}, bf16[256,1536]{1,0:T(8,128)(2,1)S(1)}, u32[]{:S(2)}, u32[]{:S(2)}) collective-permute-start(bf16[256,1536]{1,0:T(8,128)(2,1)} %collective-permute-done.mine_in), channel_id=1, source_target_pairs={{0,1},{1,0},{2,3},{3,2},{4,5},{5,4},{6,7},{7,6},{8,9},{9,8},{10,11... | collective-permute-start | bytes 2359304 | tf_op jit(solution)/shard_map/ppermute | solution.py:430
  33.9 13.3 %copy-start.5 = (s32[64]{0:T(128)S(1)}, s32[64]{0:T(128)}, u32[]{:S(2)}) copy-start(s32[64]{0:T(128)} %order.7) | copy-start | bytes 772
  44.2 4.7 %collective-permute-start.4 = (bf16[256,1536]{1,0:T(8,128)(2,1)S(1)}, bf16[256,1536]{1,0:T(8,128)(2,1)S(1)}, u32[]{:S(2)}, u32[]{:S(2)}) collective-permute-start(bf16[256,1536]{1,0:T(8,128)(2,1)S(1)} %collective-permute-done.3.mine_in), channel_id=1, source_target_pairs={{0,1},{1,0},{2,3},{3,2},{4,5},{5,4},{6,7},{7,6},{8,9},{9,8},{10,11... | collective-permute-start | bytes 2359304 | tf_op jit(solution)/shard_map/ppermute | solution.py:430
  45.1 6.1 %collective-permute-start.5 = (bf16[512,768]{1,0:T(8,128)(2,1)S(1)}, bf16[512,768]{1,0:T(8,128)(2,1)S(1)}, u32[]{:S(2)}, u32[]{:S(2)}) collective-permute-start(bf16[512,768]{1,0:T(8,128)(2,1)S(1)} %get-tuple-element.41), channel_id=1, source_target_pairs={{2,4},{6,8},{10,12},{14,16},{18,20},{22,24},{26,28},{30,32},{34,36... | collective-permute-start | bytes 2359304 | tf_op jit(solution)/shard_map/ppermute | solution.py:436
  45.8 19.2 %collective-permute-start.6 = (bf16[512,768]{1,0:T(8,128)(2,1)S(1)}, bf16[512,768]{1,0:T(8,128)(2,1)S(1)}, u32[]{:S(2)}, u32[]{:S(2)}) collective-permute-start(bf16[512,768]{1,0:T(8,128)(2,1)S(1)} %get-tuple-element.41), channel_id=1, source_target_pairs={{0,2},{4,6},{8,10},{12,14},{16,18},{20,22},{24,26},{28,30},{32,34}... | collective-permute-start | bytes 2359304 | tf_op jit(solution)/shard_map/ppermute | solution.py:436
  48.8 16.2 %copy-start = (bf16[768,1536]{1,0:T(8,128)(2,1)S(1)}, bf16[768,1536]{1,0:T(8,128)(2,1)}, u32[]{:S(2)}) copy-start(bf16[768,1536]{1,0:T(8,128)(2,1)} %weight.7) | copy-start | bytes 7077892
  67.5 3.3 %copy-start.2 = (bf16[256,1536]{1,0:T(8,128)(2,1)S(1)}, bf16[256,1536]{1,0:T(8,128)(2,1)}, u32[]{:S(2)}) copy-start(bf16[256,1536]{1,0:T(8,128)(2,1)} %tokens.1) | copy-start | bytes 2359300
  67.5 3.3 %copy-start.3 = (f32[3,1536]{1,0:T(4,128)S(1)}, f32[3,1536]{1,0:T(4,128)}, u32[]{:S(2)}) copy-start(f32[3,1536]{1,0:T(4,128)} %mod.1) | copy-start | bytes 55300
  67.5 3.3 %collective-permute-start.7 = (bf16[256,1536]{1,0:T(8,128)(2,1)S(1)}, bf16[256,1536]{1,0:T(8,128)(2,1)S(1)}, u32[]{:S(2)}, u32[]{:S(2)}) collective-permute-start(bf16[256,1536]{1,0:T(8,128)(2,1)S(1)} %finish_sent.1), channel_id=1, source_target_pairs={{0,1},{1,0},{2,3},{3,2},{4,5},{5,4},{6,7},{7,6},{8,9},{9,8},{10,11... | collective-permute-start | bytes 2359304 | tf_op jit(solution)/shard_map/ppermute | solution.py:430
